TPU v7x, 256 devices: a whole 4x4x8 slice. The times are simulated.
256 devices in a mesh: seq: 16 (over x, y_hi, core), batch: 16 (over y_lo, z).
Axes of the slice: x: 4, y: 4 (y_hi: 2, y_lo: 2; y = y_hi * 2 + y_lo), z: 8, core: 2. Of those that a mesh axis runs over, the one named last changes fastest.
Arguments:
- query_rows: bfloat16 [16, 2048, 2048], P('batch', 'seq'), may hold values from -6 to 6, as said below
- key_rows: bfloat16 [16, 2048, 1024], P('batch', 'seq'), may hold values from -6 to 6, as said below
- value_rows: bfloat16 [16, 2048, 1024], P('batch', 'seq'), may hold values from -6 to 6, as said below
- attn_output: bfloat16 [16, 2048, 2048], P('batch', 'seq'), may hold values from -6 to 6, as said below
- output_grad: bfloat16 [16, 2048, 2048], P('batch', 'seq'), may hold values from -6 to 6
- log_norm: float32 [16, 16, 2048], P('batch', None, 'seq'), as said below
- slab_order: int32 [16, 16], P('batch', 'seq'), may hold values from 0 to 15, as said below
- normed_input: bfloat16 [16, 2048, 4608], P('batch', 'seq'), may hold values from -6 to 6
Outputs:
- grad_query: bfloat16 [16, 2048, 2048], P('batch', 'seq')
- grad_key: bfloat16 [16, 2048, 1024], P('batch', 'seq')
- grad_weight: float32 [4608, 1024], P('seq')
Inputs may be any that keep to these rules, and one draw needn't show every extreme that they name: `query_rows`: queries of a causal forward pass with 16 heads. `key_rows`: keys of the same forward pass with 8 heads. `value_rows`: values of the same forward pass. `attn_output`: the forward pass's output: for each head, sum over keys at or before the query's position of exp(score - log_norm) times the value. `log_norm`: log of the sum of exp(score) over the keys at or before the query's position, so that each row's weights sum to one. `slab_order`: each row is a permutation of the slab places.
All inputs are finite; a program needn't handle non-finite values.
Results may differ from a plain program's by a relative error of at most 0.025.
Values may be sent and summed in bfloat16 or wider, within the bound.
No kernel may reach another device: no remote copies, remote signals or barrier semaphores. Data moves between devices by JAX's collectives and lax.ppermute only.
A program may use at most 128 MiB of HBM per device.

v0:
```python
import jax
import jax.numpy as jnp
from jax import lax
from jax.sharding import PartitionSpec as P

HEADS = 16
KV_HEADS = 8
HEAD = 128


SCALE = 144.0 ** (-0.5)


def from_everyone(shard, axis):
    count = lax.axis_size(axis)
    return lax.all_to_all(
        jnp.broadcast_to(shard[None], (count, *shard.shape)), axis, 0, 0, tiled=True
    )


def joined_along(parts, dim):
    parts = jnp.moveaxis(parts, 0, dim)
    shape = parts.shape
    return parts.reshape(*shape[:dim], shape[dim] * shape[dim + 1], *shape[dim + 2 :])


def gathered_copies(shard, axis, dim):
    parts = from_everyone(shard, axis)
    return joined_along(parts, dim)


def in_one_piece(arrays, axis, dim, along):
    widths = [a.shape[along] for a in arrays]
    both = jnp.concatenate(arrays, axis=along)
    filled = lax.all_gather(both, axis, axis=dim, tiled=True)
    return tuple(jnp.split(filled, [sum(widths[:k]) for k in range(1, len(widths))], axis=along))


def in_blocks(shard, dim, count):
    shape = shard.shape
    parts = shard.reshape(*shape[:dim], count, shape[dim] // count, *shape[dim + 1 :])
    return jnp.moveaxis(parts, dim, 0)


def sum_at_owner(shard, axis, dim):
    count = lax.axis_size(axis)
    parts = lax.all_to_all(in_blocks(shard, dim, count), axis, 0, 0, tiled=True)
    return jnp.sum(parts.astype(jnp.float32), axis=0)


def sent_together(arrays, axis, dim, along):
    ends, at = ([], 0)
    for a in arrays[:-1]:
        at += a.shape[along]
        ends.append(at)
    both = jnp.concatenate(arrays, axis=along)
    return tuple(
        jnp.split(lax.psum_scatter(both, axis, scatter_dimension=dim, tiled=True), ends, axis=along)
    )


def block_terms(queries, grads, delta, norms, query_pos, key_block, value_block, key_pos):
    keys_count = key_block.shape[0]
    scores = SCALE * jnp.einsum(
        "tgrd,kgd->grtk", queries, key_block, preferred_element_type=jnp.float32
    )
    allowed = key_pos[None, :] <= query_pos[:, None]
    probs = jnp.where(allowed, jnp.exp(scores - norms[..., None]), 0.0)
    dprob = jnp.einsum("tgrd,kgd->grtk", grads, value_block, preferred_element_type=jnp.float32)
    dscore = probs * (dprob - delta[..., None])
    probs_low = probs.astype(jnp.bfloat16)
    dscore_low = dscore.astype(jnp.bfloat16)
    grad_q = SCALE * jnp.einsum(
        "grtk,kgd->tgrd", dscore_low, key_block, preferred_element_type=jnp.float32
    )
    grad_k = SCALE * jnp.einsum(
        "grtk,tgrd->kgd", dscore_low, queries, preferred_element_type=jnp.float32
    )
    grad_v = jnp.einsum("grtk,tgrd->kgd", probs_low, grads, preferred_element_type=jnp.float32)
    return (grad_q, grad_k.reshape(keys_count, -1), grad_v.reshape(keys_count, -1))


def local(
    query_rows, key_rows, value_rows, attn_output, output_grad, log_norm, slab_order, normed_input
):
    tokens = query_rows.shape[1]
    group = HEADS // KV_HEADS
    kv_width = KV_HEADS * HEAD
    slabs = lax.axis_size("seq")
    length = tokens * slabs
    orders = gathered_copies(slab_order, "seq", 1)
    queries = query_rows[0].reshape(tokens, KV_HEADS, group, HEAD)
    grads = output_grad[0].reshape(tokens, KV_HEADS, group, HEAD)
    outputs = attn_output[0].reshape(tokens, KV_HEADS, group, HEAD)
    delta = jnp.transpose(
        jnp.sum(grads.astype(jnp.float32) * outputs.astype(jnp.float32), axis=3), (1, 2, 0)
    )
    norms = log_norm[0].reshape(KV_HEADS, group, tokens)
    offsets = jnp.arange(tokens, dtype=jnp.int32)
    query_pos = slab_order[0, 0] * tokens + offsets
    width = tokens * -(-512 // tokens)
    empty_kv = jnp.zeros((length, kv_width), jnp.float32)
    empty_q = jnp.zeros((tokens, KV_HEADS, group, HEAD), jnp.float32)
    start = jnp.int32(0)
    grad_q = empty_q
    grad_k = empty_kv
    grad_v = empty_kv
    key_part, value_part = in_one_piece((key_rows, value_rows), "seq", 1, 0)
    count = key_part.shape[1]
    for begin in range(0, count, width):
        finish = min(begin + width, count)
        shards = (finish - begin) // tokens
        first = (start + begin) // tokens
        places = lax.dynamic_slice_in_dim(orders[0], first, shards, 0)
        key_pos = (places[:, None] * tokens + offsets[None, :]).reshape(-1)
        key_block = key_part[0, begin:finish].reshape(-1, KV_HEADS, HEAD)
        value_block = value_part[0, begin:finish].reshape(-1, KV_HEADS, HEAD)
        term_q, term_k, term_v = block_terms(
            queries, grads, delta, norms, query_pos, key_block, value_block, key_pos
        )
        grad_q = grad_q + term_q
        grad_k = lax.dynamic_update_slice_in_dim(grad_k, term_k, begin, 0)
        grad_v = lax.dynamic_update_slice_in_dim(grad_v, term_v, begin, 0)
    grad_q, part_key, part_value = (grad_q, grad_k, grad_v)
    key_sum, value_sum = tuple(
        (
            part.astype(jnp.float32)
            for part in sent_together(
                (part_key.astype(jnp.bfloat16), part_value.astype(jnp.bfloat16)), "seq", 0, 1
            )
        )
    )
    partial_weight = lax.dot_general(
        normed_input[0],
        value_sum.astype(jnp.bfloat16),
        (((0,), (0,)), ((), ())),
        preferred_element_type=jnp.float32,
    )
    columns = lax.psum_scatter(
        partial_weight.astype(jnp.bfloat16), "batch", scatter_dimension=1, tiled=True
    )
    block = sum_at_owner(columns, "seq", 0)
    weight = gathered_copies(block.astype(jnp.bfloat16), "batch", 1).astype(block.dtype)
    grad_query = grad_q.astype(jnp.bfloat16).reshape(1, tokens, HEADS * HEAD)
    grad_key = key_sum.astype(jnp.bfloat16).reshape(1, tokens, kv_width)
    return (grad_query, grad_key, weight)


def solution(mesh):
    placed = (
        P("batch", "seq", None),
        P("batch", "seq", None),
        P("batch", "seq", None),
        P("batch", "seq", None),
        P("batch", "seq", None),
        P("batch", None, "seq"),
        P("batch", "seq"),
        P("batch", "seq", None),
    )
    return jax.shard_map(
        local,
        mesh=mesh,
        in_specs=placed,
        out_specs=(P("batch", "seq", None), P("batch", "seq", None), P("seq", None)),
        check_vma=False,
    )
```

profile of v0, /device:TPU:2, one launch (start us, length us, event | category | flops | bytes accessed | tf_op | source)
XLA Modules:
  0.0 471.2 jit_solution(12361176742124739413)
XLA Ops:
  7.2 1.3 copy.150
  8.5 1.1 copy.151
  9.6 0.8 pad_maximum_fusion.1
  11.2 0.6 broadcast_in_dim.27
  11.8 7.5 %all-to-all-start = ((s32[16,1,1]{2,1,0:T(1,128)}), s32[16,1,1]{2,1,0:T(1,128)S(1)}, u32[]{:S(2)}, u32[]{:S(2)}) async-start(s32[16,1,1]{2,1,0:T(1,128)} %broadcast_in_dim.27), calls=%async_computation | async-start | bytes 16384 | tf_op jit(solution)/shard_map/all_to_all | solution.py:16
  19.3 1.4 reshape_squeeze.34
  20.7 1.2 copy.186
  22.1 1.9 reshape.165
  24.1 2.4 multiply_reduce_fusion
  27.6 70.4 %all-gather.2.cloned.1.call-done = bf16[2,2048,1024]{1,2,0:T(8,128)(2,1)} async-done(((bf16[2,128,1024]{1,2,0:T(8,128)(2,1)}), bf16[2,2048,1024]{1,2,0:T(8,128)(2,1)}) %all-gather.2.cloned.1.call-update) | async-done | bytes 8388624 | tf_op jit(solution)/shard_map/all_gather | solution.py:35
  98.0 5.9 %fusion.61 = (bf16[1,512,1024]{1,2,0:T(8,128)(2,1)}, bf16[1,512,1024]{1,2,0:T(8,128)(2,1)S(1)}, bf16[1,512,1024]{1,2,0:T(8,128)(2,1)}, bf16[1,512,1024]{1,2,0:T(...) fusion(bf16[2,2048,1024]{1,2,0:T(8,128)(2,1)} %all-gather.2.clo, ...), kind=kLoop, calls=%fused_computation.96 | loop fusion | bytes 16777216 | tf_op jit(solution)/shard_map/slice | solution.py:117
  104.0 0.8 fusion.66
  104.7 1.9 copy-done.7
  106.7 2.0 fusion.21
  108.7 2.3 copy.196
  110.9 4.0 fusion.2
  114.9 1.3 copy-done.4
  116.3 1.8 bitcast_multiply_fusion
  118.0 2.3 copy.184
  120.3 0.8 fusion.65
  121.1 2.0 fusion.23
  123.0 2.8 fusion.6
  125.8 2.3 copy.193
  128.1 3.4 bitcast_multiply_fusion.1
  131.5 2.3 copy.181
  133.7 2.0 fusion.64
  135.7 2.0 fusion.25
  137.7 2.8 fusion.10
  140.5 2.3 copy.190
  142.8 3.4 bitcast_multiply_fusion.2
  146.2 2.3 copy.178
  148.5 2.0 fusion.62
  150.5 2.0 fusion.27
  152.4 2.8 fusion.14
  155.2 2.3 copy.187
  157.5 3.4 bitcast_multiply_fusion.3
  160.9 2.4 copy.175
  163.3 3.8 dynamic_update_slice.24
  167.1 2.5 dynamic_update_slice.28
  169.6 1.0 constant_dynamic-update-slice_fusion.5
  170.6 1.1 constant_dynamic-update-slice_fusion.4
  171.7 1.0 constant_dynamic-update-slice_fusion.3
  172.7 1.1 constant_dynamic-update-slice_fusion.2
  173.8 1.0 constant_dynamic-update-slice_fusion.1
  174.8 1.1 constant_dynamic-update-slice_fusion
  175.9 8.2 %pad_maximum_fusion = bf16[2048,2048]{1,0:T(8,128)(2,1)} fusion(bf16[2048,1024]{1,0:T(8,128)(2,1)} %constant_dynamic-update-slice_fusion, bf16[2048,1024]{1,0:T(8,128)(2,1)} %constant_dynamic-update-slice_fusion.3), kind=kLoop, calls=%fused_computation.1 | loop fusion | flops 16777216 | bytes 16777216 | tf_op jit(solution)/shard_map/concatenate | solution.py:56
  184.1 108.7 %reduce-scatter.3.cloned.1.call-done = bf16[128,2048]{1,0:T(8,128)(2,1)} async-done(((bf16[2048,2048]{1,0:T(8,128)(2,1)}), bf16[128,2048]{1,0:T(8,128)(2,1)}) %reduce-scatter.3.cloned.1.call-update) | async-done | bytes 524304 | tf_op jit(solution)/shard_map/reduce_scatter | solution.py:58
  292.8 6.1 %fusion = bf16[4608,1024]{0,1:T(8,128)(2,1)} fusion(bf16[1,128,4608]{2,1,0:T(8,128)(2,1)S(1)} %copy-done, bf16[128,2048]{1,0:T(8,128)(2,1)} %reduce-scatter.3.cloned.1.call-done), kind=kOutput, calls=%fused_computation.2 | convolution fusion | flops 1212678144 | bytes 10878976 | tf_op jit(solution)/shard_map/dot_general | solution.py:133
  298.9 111.0 %reduce-scatter.5.cloned.1.call-done = bf16[4608,64]{0,1:T(8,128)(2,1)} async-done(((bf16[4608,1024]{0,1:T(8,128)(2,1)}), bf16[4608,64]{0,1:T(8,128)(2,1)}) %reduce-scatter.5.cloned.1.call-update) | async-done | bytes 589840 | tf_op jit(solution)/shard_map/reduce_scatter | solution.py:139
  409.9 2.2 reshape.164
  412.2 1.1 copy.197
  413.2 7.1 %all-to-all-start.1 = ((bf16[16,288,64]{1,2,0:T(8,128)(2,1)}), bf16[16,288,64]{1,2,0:T(8,128)(2,1)}, u32[]{:S(2)}, u32[]{:S(2)}) async-start(bf16[16,288,64]{1,2,0:T(8,128)(2,1)} %copy.197), calls=%async_computation.3 | async-start | bytes 1572864 | tf_op jit(solution)/shard_map/all_to_all | solution.py:47
  420.4 3.4 fusion.63
  423.8 9.4 %all-to-all-done.1 = bf16[16,288,64]{1,2,0:T(8,128)(2,1)} async-done(((bf16[16,288,64]{1,2,0:T(8,128)(2,1)}), bf16[16,288,64]{1,2,0:T(8,128)(2,1)}, u32[]{:S(2)}, u32[]{:S(2)}) %all-to-all-start.1) | async-done | bytes 589856 | tf_op jit(solution)/shard_map/all_to_all | solution.py:47
  433.2 1.3 reduce_sum.22
  434.5 1.0 broadcast_in_dim.58
  435.4 4.3 all-to-all-start.2
  439.8 2.5 convolution_add_fusion.2
  442.3 0.6 convolution_add_fusion.1
  443.8 1.0 copy.198
  444.8 0.7 slice_bitcast_fusion
  445.5 16.4 %all-to-all-done.2 = bf16[16,288,64]{1,2,0:T(8,128)(2,1)} async-done(((bf16[16,288,64]{1,2,0:T(8,128)(2,1)}), bf16[16,288,64]{1,2,0:T(8,128)(2,1)}, u32[]{:S(2)}, u32[]{:S(2)}) %all-to-all-start.2) | async-done | bytes 589856 | tf_op jit(solution)/shard_map/all_to_all | solution.py:16
  461.9 1.3 convert_element_type.89
  463.2 1.5 copy.199
  (59 shorter events, 2.5 us)
Async XLA Ops:
  7.2 285.6 %copy-start = (bf16[1,128,4608]{2,1,0:T(8,128)(2,1)S(1)}, bf16[1,128,4608]{2,1,0:T(8,128)(2,1)}, u32[]{:S(2)}) copy-start(bf16[1,128,4608]{2,1,0:T(8,128)(2,1)} %param.15) | copy-start | bytes 3538948
  7.2 14.7 %copy-start.20 = (bf16[1,128,2048]{2,1,0:T(8,128)(2,1)S(1)}, bf16[1,128,2048]{2,1,0:T(8,128)(2,1)}, u32[]{:S(2)}) copy-start(bf16[1,128,2048]{2,1,0:T(8,128)(2,1)} %param.8) | copy-start | bytes 1572868
  7.2 14.9 %copy-start.19 = (bf16[1,128,2048]{2,1,0:T(8,128)(2,1)S(1)}, bf16[1,128,2048]{2,1,0:T(8,128)(2,1)}, u32[]{:S(2)}) copy-start(bf16[1,128,2048]{2,1,0:T(8,128)(2,1)} %param.11) | copy-start | bytes 1572868
  7.2 90.8 %all-gather.2.cloned.1.call-start = ((), (), s32[]{:S(2)}) async-start(), calls=%async_computation.5 | async-start | bytes 8912896 | tf_op jit(solution)/shard_map/all_gather | solution.py:35
  11.8 14.9 %all-to-all-start = ((s32[16,1,1]{2,1,0:T(1,128)}), s32[16,1,1]{2,1,0:T(1,128)S(1)}, u32[]{:S(2)}, u32[]{:S(2)}) async-start(s32[16,1,1]{2,1,0:T(1,128)} %broadcast_in_dim.27), calls=%async_computation | async-start | bytes 16384 | tf_op jit(solution)/shard_map/all_to_all | solution.py:16
  19.2 273.6 %reduce-scatter.3.cloned.1.call-start = ((), (), s32[]{:S(2)}) async-start(), calls=%async_computation.6 | async-start | bytes 8912896 | tf_op jit(solution)/shard_map/reduce_scatter | solution.py:58
  103.9 4.7 %copy-start.2 = (bf16[1,512,1024]{1,2,0:T(8,128)(2,1)}, bf16[1,512,1024]{1,2,0:T(8,128)(2,1)S(1)}, u32[]{:S(2)}) copy-start(bf16[1,512,1024]{1,2,0:T(8,128)(2,1)S(1)} %get-tuple-element.20) | copy-start | bytes 3145732
  103.9 2.7 copy-start.21
  104.0 2.7 copy-start.22
  104.7 2.0 copy-start.7
  114.9 1.3 copy-start.4
  121.1 2.0 copy-start.17
  135.7 2.0 copy-start.16
  150.5 2.0 copy-start.15
  160.9 6.2 %copy-start.14 = (bf16[512,1024]{1,0:T(8,128)(2,1)S(1)}, bf16[512,1024]{1,0:T(8,128)(2,1)}, u32[]{:S(2)}) copy-start(bf16[512,1024]{1,0:T(8,128)(2,1)} %copy.187) | copy-start | bytes 3145732
  163.2 6.3 %copy-start.13 = (bf16[512,1024]{1,0:T(8,128)(2,1)S(1)}, bf16[512,1024]{1,0:T(8,128)(2,1)}, u32[]{:S(2)}) copy-start(bf16[512,1024]{1,0:T(8,128)(2,1)} %copy.178) | copy-start | bytes 3145732
  167.0 3.6 copy-start.11
  167.0 4.6 copy-start.9
  169.6 3.1 copy-start.12
  169.6 4.2 copy-start.10
  170.6 4.2 copy-start.8
  184.1 225.8 %reduce-scatter.5.cloned.1.call-start = ((), (), s32[]{:S(2)}) async-start(), calls=%async_computation.7 | async-start | bytes 10027008 | tf_op jit(solution)/shard_map/reduce_scatter | solution.py:139
  413.2 26.5 %copy-start.1 = (bf16[1,512,1024]{1,2,0:T(8,128)(2,1)S(1)}, bf16[1,512,1024]{1,2,0:T(8,128)(2,1)}, u32[]{:S(2)}) copy-start(bf16[1,512,1024]{1,2,0:T(8,128)(2,1)} %get-tuple-element.24) | copy-start | bytes 3145732
  413.2 20.0 %all-to-all-start.1 = ((bf16[16,288,64]{1,2,0:T(8,128)(2,1)}), bf16[16,288,64]{1,2,0:T(8,128)(2,1)}, u32[]{:S(2)}, u32[]{:S(2)}) async-start(bf16[16,288,64]{1,2,0:T(8,128)(2,1)} %copy.197), calls=%async_computation.3 | async-start | bytes 1572864 | tf_op jit(solution)/shard_map/all_to_all | solution.py:47
  435.4 26.4 %all-to-all-start.2 = ((bf16[16,288,64]{1,2,0:T(8,128)(2,1)}), bf16[16,288,64]{1,2,0:T(8,128)(2,1)}, u32[]{:S(2)}, u32[]{:S(2)}) async-start(bf16[16,288,64]{1,2,0:T(8,128)(2,1)} %broadcast_in_dim.58), calls=%async_computation.4 | async-start | bytes 1572864 | tf_op jit(solution)/shard_map/all_to_all | solution.py:16
  439.7 2.6 copy-start.6
  439.8 3.1 copy-start.3
  439.8 3.5 copy-start.5
  443.2 1.6 copy-start.18
Sparse Core Ops, SparseCore 0:
  11.1 86.8 all-gather.1
  184.2 108.5 reduce-scatter.2
  299.0 110.8 reduce-scatter.4
where the time goes:
time: 472 us; the launch traced here: 471 us
  waiting for transfers between devices  316 us (67%)
  local copies, waits for them, and re-layouts  56 us (12%)
  matrix products  50.7 us (11%)
  starting transfers between devices  19 us (4%)
  other arithmetic  14.9 us (3%)
  between operations  14.7 us (3%)
    reduce_scatter x1, waiting for transfers between devices, local(): lax.psum_scatter(partial_weight.astype(jnp.bfloat16), 'batch', scatter_di...  111 us
    reduce_scatter x1, waiting for transfers between devices, sent_together(): lax.psum_scatter(both, axis, scatter_dimension=dim, tiled=True)  109 us
    all_gather x1, waiting for transfers between devices, in_one_piece(): filled = lax.all_gather(both, axis, axis=dim, tiled=True)  70.4 us
    all_to_all x2, waiting for transfers between devices, from_everyone(): lax.all_to_all(jnp.broadcast_to(shard[None], (count, *shard.shape)), axis...  16.4 us
    dot_general x4, matrix products, block_terms(): jnp.einsum('tgrd,kgd->grtk', grads, value_block, preferred_element_type=j...  12.4 us
    dot_general x4, matrix products, block_terms(): jnp.einsum('grtk,tgrd->kgd', dscore_low, queries, preferred_element_type=...  11.9 us
    all_to_all x2, starting transfers between devices, from_everyone(): lax.all_to_all(jnp.broadcast_to(shard[None], (count, *shard.shape)), axis...  11.8 us
    all_to_all x1, waiting for transfers between devices, sum_at_owner(): parts = lax.all_to_all(in_blocks(shard, dim, count), axis, 0, 0, tiled=True)  9.44 us
  transfers between devices with their start and end apart: 6, of which 5 were waited for; matrix products, arithmetic and copies ran while one was open for 4% of the time, Pallas kernels for 0%

commit v1 on v0

v1 whole, which is shorter than its diff:
```python
import jax
import jax.numpy as jnp
from jax import lax
from jax.experimental import pallas as pl
from jax.experimental.pallas import tpu as pltpu
from jax.sharding import PartitionSpec as P

HEADS = 16
KV_HEADS = 8
HEAD = 128
TOK = 128
SLABS = 16
LENGTH = 2048
CHIPS = 8
D = 4608
ROWS = D // SLABS
BK = 256
BQ = 512
PACK = 3 * TOK + 8
XW = 640

SCALE = 144.0 ** (-0.5)
LOG2E = 1.4426950408889634

f32 = jnp.float32
bf16 = jnp.bfloat16


def dot(a, b, dims):
    return lax.dot_general(a, b, (dims, ((), ())), preferred_element_type=f32)


def three_parts(x):
    hi = x.astype(bf16).astype(f32)
    rest = x - hi
    mid = rest.astype(bf16).astype(f32)
    low = (rest - mid).astype(bf16).astype(f32)
    return hi, mid, low


def pack_kernel(place_ref, q_ref, g_ref, o_ref, k_ref, v_ref, n_ref, out_ref):
    place = jnp.full((1, TOK), place_ref[0, 0], jnp.int32).astype(f32)
    for s in range(SLABS):
        cols = slice(s * HEAD, (s + 1) * HEAD)
        kv_cols = slice((s // 2) * HEAD, (s // 2 + 1) * HEAD)
        grads = g_ref[:, cols]
        out_ref[s, 0:TOK, :] = q_ref[:, cols]
        out_ref[s, TOK : 2 * TOK, :] = grads
        out_ref[s, 2 * TOK : 3 * TOK, :] = (k_ref if s % 2 == 0 else v_ref)[:, kv_cols]
        prod = grads.astype(f32) * o_ref[:, cols].astype(f32)
        delta = jnp.sum(prod.T, axis=0, keepdims=True)
        rows = (*three_parts(n_ref[s : s + 1, :]), *three_parts(delta), place, jnp.zeros_like(place))
        out_ref[s, 3 * TOK :, :] = jnp.concatenate(rows, axis=0).astype(bf16)


def attn_kernel(
    core_ref, in_ref, oth_ref, qk_ref, keep_ref, send_ref,
    q_s, g_s, k_s, v_s, nd_s, dq_s, dk_s, dv_s, inv_s,
):
    core = core_ref[0, 0]
    for s in range(SLABS):
        extra = in_ref[s, 3 * TOK :, :].astype(f32)
        p = jnp.max(extra[6:7, :]).astype(jnp.int32)
        inv_s[p] = s
        at = pl.ds(pl.multiple_of(p * TOK, TOK), TOK)
        q_s[at, :] = in_ref[s, 0:TOK, :]
        g_s[at, :] = in_ref[s, TOK : 2 * TOK, :]
        own = in_ref[s, 2 * TOK : 3 * TOK, :]
        oth = oth_ref[s]
        k_s[at, :] = jnp.where(core == 0, own, oth)
        v_s[at, :] = jnp.where(core == 0, oth, own)
        norm = (extra[0:1] + extra[1:2] + extra[2:3]) * LOG2E
        delta = extra[3:4] + extra[4:5] + extra[5:6]
        nd_s[p, 0:1, :] = norm
        nd_s[p, 1:2, :] = delta
    dq_s[...] = jnp.zeros_like(dq_s)

    def one(j, i, kb, kt, vb, masked):
        qb = q_s[pl.ds(pl.multiple_of(i * BQ, BQ), BQ), :]
        gb = g_s[pl.ds(pl.multiple_of(i * BQ, BQ), BQ), :]
        norm = jnp.concatenate([nd_s[i * (BQ // TOK) + t, 0:1, :] for t in range(BQ // TOK)], axis=1)
        delta = jnp.concatenate([nd_s[i * (BQ // TOK) + t, 1:2, :] for t in range(BQ // TOK)], axis=1)
        st = dot(kb, qb, ((1,), (1,)))
        probs = jnp.exp2(st * (SCALE * LOG2E) - norm)
        if masked:
            key_at = lax.broadcasted_iota(jnp.int32, (BK, BQ), 0) + j * BK
            query_at = lax.broadcasted_iota(jnp.int32, (BK, BQ), 1) + i * BQ
            probs = jnp.where(key_at <= query_at, probs, 0.0)
        dprob = dot(vb, gb, ((1,), (1,)))
        ds = (probs * (dprob - delta)).astype(bf16)
        dv = dot(probs.astype(bf16), gb, ((1,), (0,)))
        dk = dot(ds, qb, ((1,), (0,)))
        dq_s[i] += dot(kt, ds, ((1,), (0,)))
        return dk, dv

    def per_key_block(j, _):
        at = pl.ds(pl.multiple_of(j * BK, BK), BK)
        kb = k_s[at, :]
        vb = v_s[at, :]
        kt = kb.T
        first = j // (BQ // BK)
        dk, dv = one(j, first, kb, kt, vb, True)
        dk_s[...] = dk
        dv_s[...] = dv

        def per_query_block(i, _):
            dk, dv = one(j, i, kb, kt, vb, False)
            dk_s[...] += dk
            dv_s[...] += dv
            return 0

        lax.fori_loop(first + 1, LENGTH // BQ, per_query_block, 0)
        for t in range(BK // TOK):
            s = inv_s[j * (BK // TOK) + t]
            qk_ref[s, TOK:, :] = (dk_s[t * TOK : (t + 1) * TOK, :] * SCALE).astype(bf16)
            part = dv_s[t * TOK : (t + 1) * TOK, :]

            @pl.when(s % 2 == core)
            def _():
                keep_ref[s // 2] = part

            @pl.when(s % 2 != core)
            def _():
                send_ref[s // 2] = part.astype(bf16)

        return 0

    lax.fori_loop(0, LENGTH // BK, per_key_block, 0)
    for i in range(LENGTH // BQ):
        rows = (dq_s[i].T * SCALE).astype(bf16)
        for t in range(BQ // TOK):
            s = inv_s[i * (BQ // TOK) + t]
            qk_ref[s, 0:TOK, :] = rows[t * TOK : (t + 1) * TOK, :]


def weight_kernel(place_ref, xt_ref, dv_ref, keep_ref, send_ref):
    core = place_ref[0, 0]
    base = place_ref[0, 1]
    own = pl.multiple_of(base + core * ROWS, 32)
    other = pl.multiple_of(base + (1 - core) * ROWS, 32)
    grads = jnp.concatenate([dv_ref[0], dv_ref[1]], axis=1)
    mine = dot(xt_ref[pl.ds(own, ROWS), :], grads, ((1,), (0,)))
    sent = dot(xt_ref[pl.ds(other, ROWS), :], grads, ((1,), (0,))).astype(bf16)
    half = ROWS // 2
    for r in range(2):
        for h in range(2):
            keep_ref[r, h] = mine[r * half : (r + 1) * half, h * HEAD : (h + 1) * HEAD]
            send_ref[r, h] = sent[r * half : (r + 1) * half, h * HEAD : (h + 1) * HEAD]


VMEM = pl.BlockSpec(memory_space=pltpu.VMEM)
SMEM = pl.BlockSpec(memory_space=pltpu.SMEM)


def pack(place, q, g, o, k, v, n):
    return pl.pallas_call(
        pack_kernel,
        in_specs=[SMEM] + [VMEM] * 6,
        out_specs=VMEM,
        out_shape=jax.ShapeDtypeStruct((SLABS, PACK, HEAD), bf16),
        name="pack",
    )(place, q, g, o, k, v, n)


def attention(core, packed, other):
    half = (CHIPS, TOK, HEAD)
    return pl.pallas_call(
        attn_kernel,
        in_specs=[SMEM, VMEM, VMEM],
        out_specs=[VMEM] * 3,
        out_shape=[
            jax.ShapeDtypeStruct((SLABS, 2 * TOK, HEAD), bf16),
            jax.ShapeDtypeStruct(half, f32),
            jax.ShapeDtypeStruct(half, bf16),
        ],
        scratch_shapes=[pltpu.VMEM((LENGTH, HEAD), bf16)] * 4
        + [
            pltpu.VMEM((SLABS, 8, TOK), f32),
            pltpu.VMEM((LENGTH // BQ, HEAD, BQ), f32),
            pltpu.VMEM((BK, HEAD), f32),
            pltpu.VMEM((BK, HEAD), f32),
            pltpu.SMEM((SLABS,), jnp.int32),
        ],
        cost_estimate=pl.CostEstimate(flops=6 * 10**9, bytes_accessed=4 * 10**6, transcendentals=2 * 10**6),
        name="attention",
    )(core, packed, other)


def weight_rows(place, xt, dv):
    shape = (2, KV_HEADS, ROWS // 2, HEAD)
    block = pl.BlockSpec((2, 2, ROWS // 2, HEAD), lambda n: (0, n, 0, 0))
    return pl.pallas_call(
        weight_kernel,
        grid=(KV_HEADS // 2,),
        in_specs=[SMEM, VMEM, pl.BlockSpec((2, LENGTH // 2, HEAD), lambda n: (n, 0, 0))],
        out_specs=[block, block],
        out_shape=[jax.ShapeDtypeStruct(shape, f32), jax.ShapeDtypeStruct(shape, bf16)],
        cost_estimate=pl.CostEstimate(flops=2 * 10**9, bytes_accessed=5 * 10**6, transcendentals=0),
        name="weight",
    )(place, xt, dv)


SWAP = [(i, i ^ 1) for i in range(SLABS)]
SAME_CORE = [list(range(c, SLABS, 2)) for c in range(2)]


def local(
    query_rows, key_rows, value_rows, attn_output, output_grad, log_norm, slab_order, normed_input
):
    me = lax.axis_index("seq")
    core = me % 2
    packed = pack(
        slab_order, query_rows[0], output_grad[0], attn_output[0], key_rows[0], value_rows[0], log_norm[0]
    )
    got = lax.all_to_all(packed, "seq", 0, 0, tiled=True)
    other = lax.ppermute(got[:, 2 * TOK : 3 * TOK, :], "seq", SWAP)
    x = normed_input[0]
    starts = [1152 * (d // 2) + 512 * (d % 2) for d in range(CHIPS)]
    x_out = jnp.stack([x[:, a : a + XW] for a in starts])
    got, x_out = lax.optimization_barrier((got, x_out))
    x_in = lax.all_to_all(x_out, "seq", 0, 0, axis_index_groups=SAME_CORE, tiled=True)
    qk, keep, send = attention(core.reshape(1, 1), got, other)
    dv = (keep + lax.ppermute(send, "seq", SWAP).astype(f32)).astype(bf16)
    dv = dv.reshape(1, LENGTH // 2, HEAD)
    dv_all = lax.all_to_all(
        jnp.broadcast_to(dv, (CHIPS, LENGTH // 2, HEAD)), "seq", 0, 0, axis_index_groups=SAME_CORE, tiled=True
    )
    xt = x_in.reshape(LENGTH // 2, XW).T
    qk, dv_all = lax.optimization_barrier((qk, dv_all))
    qk_in = lax.all_to_all(qk, "seq", 0, 0, tiled=True)
    place = jnp.stack([core, (me // 2 % 2) * 64]).reshape(1, 2)
    w_keep, w_send = weight_rows(place, xt, dv_all)
    w = (w_keep + lax.ppermute(w_send, "seq", SWAP).astype(f32)).astype(bf16)
    parts = lax.all_to_all(w.reshape(SLABS, ROWS // 2, HEAD), "batch", 0, 0, tiled=True)
    piece = jnp.sum(parts.astype(f32), axis=0).astype(bf16)
    pieces = lax.all_to_all(
        jnp.broadcast_to(piece[None], (SLABS, ROWS // 2, HEAD)), "batch", 0, 0, tiled=True
    )
    weight = pieces.reshape(2, KV_HEADS, ROWS // 2, HEAD).transpose(0, 2, 1, 3).reshape(ROWS, KV_HEADS * HEAD)
    grad_query = qk_in[:, :TOK, :].transpose(1, 0, 2).reshape(1, TOK, HEADS * HEAD)
    pair = qk_in[:, TOK:, :].astype(f32).reshape(KV_HEADS, 2, TOK, HEAD)
    grad_key = (pair[:, 0] + pair[:, 1]).astype(bf16).transpose(1, 0, 2).reshape(1, TOK, KV_HEADS * HEAD)
    return (grad_query, grad_key, weight.astype(f32))


def solution(mesh):
    placed = (
        P("batch", "seq", None),
        P("batch", "seq", None),
        P("batch", "seq", None),
        P("batch", "seq", None),
        P("batch", "seq", None),
        P("batch", None, "seq"),
        P("batch", "seq"),
        P("batch", "seq", None),
    )
    return jax.shard_map(
        local,
        mesh=mesh,
        in_specs=placed,
        out_specs=(P("batch", "seq", None), P("batch", "seq", None), P("seq", None)),
        check_vma=False,
    )
```

time: 472 us -> 180 us (0.38)
  waiting for transfers between devices: 316 us -> 80.2 us
  matrix products: 50.7 us -> 0 us
  local copies, waits for them, and re-layouts: 56 us -> 15 us
  blocking collectives: 0 us -> 27.9 us
  Pallas kernels: 0 us -> 21.6 us
  between operations: 14.7 us -> 1.38 us
  other arithmetic: 14.9 us -> 3.4 us
  starting transfers between devices: 19 us -> 29.2 us
    reduce_scatter x2 -> x0, waiting for transfers between devices: 220 us -> none  [the longest x1 111 us: local(): lax.psum_scatter(partial_weight.astype(jnp.bfloat16), 'batch', scatter_di...]
    all_gather x1 -> x0, waiting for transfers between devices: 70.4 us -> none  [in_one_piece(): filled = lax.all_gather(both, axis, axis=dim, tiled=True)]
    dot_general x21 -> x0, matrix products: 50.7 us -> none  [the longest x4 12.4 us: block_terms(): jnp.einsum('tgrd,kgd->grtk', grads, value_block, preferred_element_type=j...]
    all_to_all x3 -> x5, waiting for transfers between devices: 25.8 us -> 76.3 us  [the longest x1 25.8 us: local(): lax.all_to_all(jnp.broadcast_to(dv, (CHIPS, LENGTH // 2, HEAD)), 'seq', 0...]
    all_to_all x0 -> x1, blocking collectives: none -> 27.9 us  [local(): lax.all_to_all(w.reshape(SLABS, ROWS // 2, HEAD), 'batch', 0, 0, tiled=True)]
    pallas_call x0 -> x3, Pallas kernels: none -> 21.6 us  [the longest x1 13.4 us: attention(): pl.pallas_call(attn_kernel, in_specs=[SMEM, VMEM, VMEM], out_specs=[VMEM]...]
    reshape x11 -> x2, local copies, waits for them, and re-layouts: 22.3 us -> 2.33 us  [the longest x1 1.51 us: local(): xt = x_in.reshape(LENGTH // 2, XW).T]
    dynamic_update_slice x8 -> x0, local copies, waits for them, and re-layouts: 12.6 us -> none  [the longest x4 6.92 us: local(): grad_k = lax.dynamic_update_slice_in_dim(grad_k, term_k, begin, 0)]
  transfers between devices with their start and end apart: 6 -> 8, of which waited for: 5 -> 7; matrix products, arithmetic and copies ran while one was open for 4% -> 6% of each run, Pallas kernels for 0% -> 7%
where the time goes in v1:
time: 180 us; the launch traced here: 179 us
  waiting for transfers between devices  80.2 us (45%)
  starting transfers between devices  29.2 us (16%)
  blocking collectives  27.9 us (16%)
  Pallas kernels  21.6 us (12%)
  local copies, waits for them, and re-layouts  15 us (8%)
  other arithmetic  3.4 us (2%)
    all_to_all x1, blocking collectives, local(): lax.all_to_all(w.reshape(SLABS, ROWS // 2, HEAD), 'batch', 0, 0, tiled=True)  27.9 us
    all_to_all x1, waiting for transfers between devices, local(): lax.all_to_all(jnp.broadcast_to(dv, (CHIPS, LENGTH // 2, HEAD)), 'seq', 0...  25.8 us
    all_to_all x1, waiting for transfers between devices, local(): got = lax.all_to_all(packed, 'seq', 0, 0, tiled=True)  18 us
    all_to_all x1, waiting for transfers between devices, local(): qk_in = lax.all_to_all(qk, 'seq', 0, 0, tiled=True)  15.7 us
    all_to_all x1, waiting for transfers between devices, local(): lax.all_to_all(jnp.broadcast_to(piece[None], (SLABS, ROWS // 2, HEAD)), '...  14.4 us
    pallas_call x1, Pallas kernels, attention(): pl.pallas_call(attn_kernel, in_specs=[SMEM, VMEM, VMEM], out_specs=[VMEM]...  13.4 us
    unnamed x15, local copies, waits for them, and re-layouts  8.52 us
    all_to_all x1, starting transfers between devices, local(): got = lax.all_to_all(packed, 'seq', 0, 0, tiled=True)  7.61 us
  transfers between devices with their start and end apart: 8, of which 7 were waited for; matrix products, arithmetic and copies ran while one was open for 6% of the time, Pallas kernels for 7%

profile of v1, /device:TPU:2, one launch (start us, length us, event | category | flops | bytes accessed | tf_op | source)
XLA Modules:
  0.0 178.7 jit_solution(12628108258156094561)
XLA Ops:
  1.3 3.2 %pack.1 = bf16[16,392,128]{2,1,0:T(8,128)(2,1)} custom-call(s32[1,1]{1,0:T(1,128)S(6)} %copy.33.place_ref, bf16[128,2048]{1,0:T(8,128)(2,1)} %bitcast.83, bf16[128,2048]{1,0:T(8,128)(2,1)} %bitcast.84, bf16[128,2048]{1,0:T(8,128)(2,1)} %bitcast.85, bf16[128,1024]{1,0:T(8,128)(2,1)} %bitcast.86, bf16[128,1024]{1,0:T(8,128)(2,1)} %bitcast.87, f32[16,128]{1,0:T(8,128)} %bitcast.88), custom_call_target="tpu_custom_call" | custom-call | tf_op jit(solution)/shard_map/pack/pallas_call | solution.py:156
  4.4 0.0 copy-start.2
  4.4 7.6 %all-to-all-start = ((bf16[16,392,128]{2,1,0:T(8,128)(2,1)}), bf16[16,392,128]{2,1,0:T(8,128)(2,1)S(1)}, u32[]{:S(2)}, u32[]{:S(2)}) async-start(bf16[16,392,128]{2,1,0:T(8,128)(2,1)} %pack.1), calls=%async_computation | async-start | bytes 3211264 | tf_op jit(solution)/shard_map/all_to_all | solution.py:215
  12.0 0.0 copy-done.2
  12.1 0.7 fusion.9
  12.7 0.7 fusion.8
  13.4 0.7 fusion.7
  14.1 0.7 fusion.6
  14.8 0.7 fusion.5
  15.5 0.7 fusion.4
  16.1 18.0 %all-to-all-done.in_ref = bf16[16,392,128]{2,1,0:T(8,128)(2,1)S(1)} async-done(((bf16[16,392,128]{2,1,0:T(8,128)(2,1)}), bf16[16,392,128]{2,1,0:T(8,128)(2,1)S(1)}, u32[]{:S(2)}, u32[]{:S(2)}) %all-to-all-start) | async-done | bytes 1605664 | tf_op jit(solution)/shard_map/all_to_all | solution.py:215
  34.1 0.0 copy-start
  34.2 0.1 collective-permute-start
  34.3 0.8 fusion.3
  35.1 0.7 fusion.2
  35.8 0.0 copy-done
  35.8 6.1 %all-to-all-start.3 = ((bf16[8,128,640]{2,1,0:T(8,128)(2,1)}), bf16[8,128,640]{2,1,0:T(8,128)(2,1)S(1)}, u32[]{:S(2)}, u32[]{:S(2)}) async-start(bf16[8,128,640]{2,1,0:T(8,128)(2,1)} %fusion.2), calls=%async_computation.3 | async-start | bytes 2621440 | tf_op jit(solution)/shard_map/all_to_all | solution.py:221
  41.9 0.0 collective-permute-done.oth_ref
  41.9 13.4 %attention.1 = (bf16[16,256,128]{2,1,0:T(8,128)(2,1)}, f32[8,128,128]{2,1,0:T(8,128)}, bf16[8,128,128]{2,1,0:T(8,128)(2,1)}) custom-call(s32[1,1]{1,0:T(1,128)} %bitcast.core_ref, bf16[16,392,128]{2,1,0:T(8,128)(2,1)} %copy-done, bf16[16,128,128]{2,1,0:T(8,128)(2,1)} %collective-permute-done.oth_ref), custom_call_target="tpu_custom_call" | custom-call | flops 6000000000 | bytes 4000000 | tf_op jit(solution)/shard_map/attention/pallas_call | solution.py:167
  55.3 0.0 collective-permute-start.1
  55.3 1.7 collective-permute-done.1
  57.0 1.1 add_convert_fusion.1
  58.1 2.4 %all-to-all-done.3 = bf16[8,128,640]{2,1,0:T(8,128)(2,1)S(1)} async-done(((bf16[8,128,640]{2,1,0:T(8,128)(2,1)}), bf16[8,128,640]{2,1,0:T(8,128)(2,1)S(1)}, u32[]{:S(2)}, u32[]{:S(2)}) %all-to-all-start.3) | async-done | bytes 1310752 | tf_op jit(solution)/shard_map/all_to_all | solution.py:221
  60.5 1.6 broadcast_in_dim.14
  62.1 5.7 %all-to-all-start.1 = ((bf16[8,1024,128]{2,1,0:T(8,128)(2,1)}), bf16[8,1024,128]{2,1,0:T(8,128)(2,1)S(1)}, u32[]{:S(2)}, u32[]{:S(2)}) async-start(bf16[8,1024,128]{2,1,0:T(8,128)(2,1)} %broadcast_in_dim.14), calls=%async_computation.1 | async-start | bytes 4194304 | tf_op jit(solution)/shard_map/all_to_all | solution.py:225
  67.8 0.6 add_bitcast_fusion.place_ref
  68.4 1.5 copy.22
  69.9 25.8 %all-to-all-done.1.dv_ref = bf16[8,1024,128]{2,1,0:T(8,128)(2,1)S(1)} async-done(((bf16[8,1024,128]{2,1,0:T(8,128)(2,1)}), bf16[8,1024,128]{2,1,0:T(8,128)(2,1)S(1)}, u32[]{:S(2)}, u32[]{:S(2)}) %all-to-all-start.1) | async-done | bytes 2097184 | tf_op jit(solution)/shard_map/all_to_all | solution.py:225
  95.8 0.0 copy-start.1
  95.8 1.3 copy-done.1
  97.1 5.1 %weight.1 = (f32[2,8,144,128]{3,2,1,0:T(8,128)}, bf16[2,8,144,128]{3,2,1,0:T(8,128)(2,1)}) custom-call(s32[1,2]{1,0:T(1,128)} %add_bitcast_fusion.place_ref, bf16[640,1024]{1,0:T(8,128)(2,1)} %bitcast.80, bf16[8,1024,128]{2,1,0:T(8,128)(2,1)} %copy-done.1), custom_call_target="tpu_custom_call" | custom-call | flops 2000000000 | bytes 5000000 | tf_op jit(solution)/shard_map/weight/pallas_call | solution.py:192
  102.2 0.0 collective-permute-start.2
  102.2 2.2 %collective-permute-done.2 = bf16[2,8,144,128]{3,2,1,0:T(8,128)(2,1)S(1)} collective-permute-done((bf16[2,8,144,128]{3,2,1,0:T(8,128)(2,1)}, bf16[2,8,144,128]{3,2,1,0:T(8,128)(2,1)S(1)}, u32[]{:S(2)}, u32[]{:S(2)}) %collective-permute-start.2) | collective-permute-done | bytes 589856 | tf_op jit(solution)/shard_map/ppermute | solution.py:233
  104.4 1.4 add_convert_fusion
  105.8 27.9 %all_to_all.30 = bf16[16,144,128]{2,1,0:T(8,128)(2,1)S(1)} all-to-all(bf16[16,144,128]{2,1,0:T(8,128)(2,1)S(1)} %bitcast.69), channel_id=1, replica_groups=mesh['seq'=16,'batch'=16] {'batch'}, dimensions={0} | all-to-all | bytes 1179648 | tf_op jit(solution)/shard_map/all_to_all | solution.py:234
  133.7 6.1 %all-to-all-start.2 = ((bf16[16,256,128]{2,1,0:T(8,128)(2,1)}), bf16[16,256,128]{2,1,0:T(8,128)(2,1)S(1)}, u32[]{:S(2)}, u32[]{:S(2)}) async-start(bf16[16,256,128]{2,1,0:T(8,128)(2,1)} %get-tuple-element.16), calls=%async_computation.2 | async-start | bytes 2097152 | tf_op jit(solution)/shard_map/all_to_all | solution.py:230
  139.8 0.1 reduce_sum.12
  139.9 15.7 %all-to-all-done.2 = bf16[16,256,128]{2,1,0:T(8,128)(2,1)S(1)} async-done(((bf16[16,256,128]{2,1,0:T(8,128)(2,1)}), bf16[16,256,128]{2,1,0:T(8,128)(2,1)S(1)}, u32[]{:S(2)}, u32[]{:S(2)}) %all-to-all-start.2) | async-done | bytes 1048608 | tf_op jit(solution)/shard_map/all_to_all | solution.py:230
  155.6 0.9 broadcast_in_dim.15
  156.5 3.6 %all-to-all-start.5 = ((bf16[16,144,128]{2,1,0:T(8,128)(2,1)}), bf16[16,144,128]{2,1,0:T(8,128)(2,1)S(1)}, u32[]{:S(2)}, u32[]{:S(2)}) async-start(bf16[16,144,128]{2,1,0:T(8,128)(2,1)} %broadcast_in_dim.15), calls=%async_computation.5 | async-start | bytes 1179648 | tf_op jit(solution)/shard_map/all_to_all | solution.py:236
  160.1 0.1 fusion.10
  160.2 0.1 convert.5
  160.3 0.1 fusion.1
  160.4 0.2 copy.18
  160.6 0.8 reshape.45
  161.4 0.3 copy.17
  161.7 1.0 copy.21
  162.7 14.4 %all-to-all-done.5 = bf16[16,144,128]{2,1,0:T(8,128)(2,1)S(1)} async-done(((bf16[16,144,128]{2,1,0:T(8,128)(2,1)}), bf16[16,144,128]{2,1,0:T(8,128)(2,1)S(1)}, u32[]{:S(2)}, u32[]{:S(2)}) %all-to-all-start.5) | async-done | bytes 589856 | tf_op jit(solution)/shard_map/all_to_all | solution.py:236
  177.0 0.1 convert_bitcast_fusion
  177.1 0.4 copy.20
  177.5 1.2 copy.25
  (1 shorter events, 0.0 us)
Async XLA Ops:
  4.4 7.6 %copy-start.2 = (bf16[1,128,4608]{2,1,0:T(8,128)(2,1)S(1)}, bf16[1,128,4608]{2,1,0:T(8,128)(2,1)}, u32[]{:S(2)}) copy-start(bf16[1,128,4608]{2,1,0:T(8,128)(2,1)} %param.15) | copy-start | bytes 3538948
  4.4 29.7 %all-to-all-start = ((bf16[16,392,128]{2,1,0:T(8,128)(2,1)}), bf16[16,392,128]{2,1,0:T(8,128)(2,1)S(1)}, u32[]{:S(2)}, u32[]{:S(2)}) async-start(bf16[16,392,128]{2,1,0:T(8,128)(2,1)} %pack.1), calls=%async_computation | async-start | bytes 3211264 | tf_op jit(solution)/shard_map/all_to_all | solution.py:215
  34.1 1.7 copy-start
  34.2 7.7 %collective-permute-start = (bf16[16,128,128]{2,1,0:T(8,128)(2,1)S(1)}, bf16[16,128,128]{2,1,0:T(8,128)(2,1)}, u32[]{:S(2)}, u32[]{:S(2)}) collective-permute-start(bf16[16,128,128]{2,1,0:T(8,128)(2,1)S(1)} %slice.60), channel_id=1, source_target_pairs={{0,16},{16,0},{32,48},{48,32},{64,80},{80,64},{96,112},{112,96},{1... | collective-permute-start | bytes 1572872 | tf_op jit(solution)/shard_map/ppermute | solution.py:216
  35.8 24.7 %all-to-all-start.3 = ((bf16[8,128,640]{2,1,0:T(8,128)(2,1)}), bf16[8,128,640]{2,1,0:T(8,128)(2,1)S(1)}, u32[]{:S(2)}, u32[]{:S(2)}) async-start(bf16[8,128,640]{2,1,0:T(8,128)(2,1)} %fusion.2), calls=%async_computation.3 | async-start | bytes 2621440 | tf_op jit(solution)/shard_map/all_to_all | solution.py:221
  55.3 1.7 collective-permute-start.1
  62.1 33.7 %all-to-all-start.1 = ((bf16[8,1024,128]{2,1,0:T(8,128)(2,1)}), bf16[8,1024,128]{2,1,0:T(8,128)(2,1)S(1)}, u32[]{:S(2)}, u32[]{:S(2)}) async-start(bf16[8,1024,128]{2,1,0:T(8,128)(2,1)} %broadcast_in_dim.14), calls=%async_computation.1 | async-start | bytes 4194304 | tf_op jit(solution)/shard_map/all_to_all | solution.py:225
  95.8 1.3 copy-start.1
  102.2 2.2 %collective-permute-start.2 = (bf16[2,8,144,128]{3,2,1,0:T(8,128)(2,1)}, bf16[2,8,144,128]{3,2,1,0:T(8,128)(2,1)S(1)}, u32[]{:S(2)}, u32[]{:S(2)}) collective-permute-start(bf16[2,8,144,128]{3,2,1,0:T(8,128)(2,1)} %get-tuple-element.20), channel_id=1, source_target_pairs={{0,16},{16,0},{32,48},{48,32},{64,80},{80,64},{96,112},{112,96},{1... | collective-permute-start | bytes 1769480 | tf_op jit(solution)/shard_map/ppermute | solution.py:233
  133.7 21.9 %all-to-all-start.2 = ((bf16[16,256,128]{2,1,0:T(8,128)(2,1)}), bf16[16,256,128]{2,1,0:T(8,128)(2,1)S(1)}, u32[]{:S(2)}, u32[]{:S(2)}) async-start(bf16[16,256,128]{2,1,0:T(8,128)(2,1)} %get-tuple-element.16), calls=%async_computation.2 | async-start | bytes 2097152 | tf_op jit(solution)/shard_map/all_to_all | solution.py:230
  156.5 20.5 %all-to-all-start.5 = ((bf16[16,144,128]{2,1,0:T(8,128)(2,1)}), bf16[16,144,128]{2,1,0:T(8,128)(2,1)S(1)}, u32[]{:S(2)}, u32[]{:S(2)}) async-start(bf16[16,144,128]{2,1,0:T(8,128)(2,1)} %broadcast_in_dim.15), calls=%async_computation.5 | async-start | bytes 1179648 | tf_op jit(solution)/shard_map/all_to_all | solution.py:236

commit v2 on v1

v2 whole, which is shorter than its diff:
```python
import jax
import jax.numpy as jnp
from jax import lax
from jax.experimental import pallas as pl
from jax.experimental.pallas import tpu as pltpu
from jax.sharding import PartitionSpec as P


HEADS = 16
KV_HEADS = 8
HEAD = 128
TOK = 128
SLABS = 16
LENGTH = 2048
CHIPS = 8
D = 4608
ROWS = D // SLABS
BK = 256
BQ = 512
HALF = TOK // 2
PACK = 2 * TOK + HALF + 8
TILES = 5

SCALE = 144.0 ** (-0.5)
LOG2E = 1.4426950408889634

f32 = jnp.float32
bf16 = jnp.bfloat16


def dot(a, b, dims):
    return lax.dot_general(a, b, (dims, ((), ())), preferred_element_type=f32)


def three_parts(x):
    hi = x.astype(bf16).astype(f32)
    rest = x - hi
    mid = rest.astype(bf16).astype(f32)
    low = (rest - mid).astype(bf16).astype(f32)
    return hi, mid, low


def pack_kernel(place_ref, q_ref, g_ref, o_ref, k_ref, n_ref, out_ref):
    place = jnp.full((1, TOK), place_ref[0, 0], jnp.int32).astype(f32)
    for s in range(SLABS):
        cols = slice(s * HEAD, (s + 1) * HEAD)
        kv_cols = slice((s // 2) * HEAD, (s // 2 + 1) * HEAD)
        half = slice((s % 2) * HALF, (s % 2 + 1) * HALF)
        grads = g_ref[:, cols]
        out_ref[s, 0:TOK, :] = q_ref[:, cols]
        out_ref[s, TOK : 2 * TOK, :] = grads
        out_ref[s, 2 * TOK : 2 * TOK + HALF, :] = k_ref[half, kv_cols]
        prod = grads.astype(f32) * o_ref[:, cols].astype(f32)
        delta = jnp.sum(prod.T, axis=0, keepdims=True)
        rows = (*three_parts(n_ref[s : s + 1, :]), *three_parts(delta), place, jnp.zeros_like(place))
        out_ref[s, 2 * TOK + HALF :, :] = jnp.concatenate(rows, axis=0).astype(bf16)


def pack_late_kernel(x_ref, v_ref, out_ref):
    for d in range(CHIPS):
        first = 9 * (d // 2) + 4 * (d % 2)
        for t in range(TILES):
            out_ref[d, t * TOK : (t + 1) * TOK, :] = x_ref[:, (first + t) * 128 : (first + t + 1) * 128]
        out_ref[d, TILES * TOK :, :] = v_ref[:, d * HEAD : (d + 1) * HEAD]


def sort_slabs(core, in_ref, oth_ref, q_s, g_s, k_s, nd_s, inv_s):
    for s in range(SLABS):
        extra = in_ref[s, 2 * TOK + HALF :, :].astype(f32)
        p = jnp.max(extra[6:7, :]).astype(jnp.int32)
        inv_s[p] = s
        at = pl.ds(pl.multiple_of(p * TOK, TOK), TOK)
        q_s[at, :] = in_ref[s, 0:TOK, :]
        g_s[at, :] = in_ref[s, TOK : 2 * TOK, :]
        own = in_ref[s, 2 * TOK : 2 * TOK + HALF, :]
        oth = oth_ref[s]
        k_s[pl.ds(pl.multiple_of(p * TOK, TOK), HALF), :] = jnp.where(core == 0, own, oth)
        k_s[pl.ds(pl.multiple_of(p * TOK + HALF, HALF), HALF), :] = jnp.where(core == 0, oth, own)
        nd_s[p, 0:1, :] = (extra[0:1] + extra[1:2] + extra[2:3]) * LOG2E
        nd_s[p, 1:2, :] = extra[3:4] + extra[4:5] + extra[5:6]


def row_of(nd_s, i, row):
    return jnp.concatenate([nd_s[i * (BQ // TOK) + t, row : row + 1, :] for t in range(BQ // TOK)], axis=1)


def block_at(i, size):
    return pl.ds(pl.multiple_of(i * size, size), size)


def probs_of(j, i, kb, qb, nd_s, masked):
    st = dot(kb, qb, ((1,), (1,)))
    probs = jnp.exp2(st * (SCALE * LOG2E) - row_of(nd_s, i, 0))
    if masked:
        key_at = lax.broadcasted_iota(jnp.int32, (BK, BQ), 0) + j * BK
        query_at = lax.broadcasted_iota(jnp.int32, (BK, BQ), 1) + i * BQ
        probs = jnp.where(key_at <= query_at, probs, 0.0)
    return probs


def value_kernel(where_ref, in_ref, oth_ref, keep_ref, send_ref, q_s, g_s, k_s, nd_s, dv_s, inv_s):
    core = where_ref[0, 0]
    sort_slabs(core, in_ref, oth_ref, q_s, g_s, k_s, nd_s, inv_s)

    def per_key_block(j, _):
        kb = k_s[block_at(j, BK), :]
        first = j // (BQ // BK)

        def one(i, masked):
            probs = probs_of(j, i, kb, q_s[block_at(i, BQ), :], nd_s, masked)
            return dot(probs.astype(bf16), g_s[block_at(i, BQ), :], ((1,), (0,)))

        dv_s[...] = one(first, True)

        def per_query_block(i, _):
            dv_s[...] += one(i, False)
            return 0

        lax.fori_loop(first + 1, LENGTH // BQ, per_query_block, 0)
        for t in range(BK // TOK):
            s = inv_s[j * (BK // TOK) + t]
            part = dv_s[t * TOK : (t + 1) * TOK, :]

            @pl.when(s % 2 == core)
            def _():
                keep_ref[s // 2] = part

            @pl.when(s % 2 != core)
            def _():
                send_ref[s // 2] = part.astype(bf16)

        return 0

    lax.fori_loop(0, LENGTH // BK, per_key_block, 0)


def score_kernel(
    where_ref, in_ref, oth_ref, v_ref, voth_ref, qkeep_ref, qsend_ref, kkeep_ref, ksend_ref,
    q_s, g_s, k_s, v_s, nd_s, dq_s, dk_s, inv_s,
):
    core = where_ref[0, 0]
    chip = where_ref[0, 1]
    sort_slabs(core, in_ref, oth_ref, q_s, g_s, k_s, nd_s, inv_s)
    for p in range(SLABS):
        s = inv_s[p]
        at = slice(p * TOK, (p + 1) * TOK)
        v_s[at, :] = jnp.where(s % 2 == core, v_ref[s // 2], voth_ref[s // 2])
    dq_s[...] = jnp.zeros_like(dq_s)

    def per_key_block(j, _):
        kb = k_s[block_at(j, BK), :]
        vb = v_s[block_at(j, BK), :]
        kt = kb.T
        first = j // (BQ // BK)

        def one(i, masked):
            qb = q_s[block_at(i, BQ), :]
            probs = probs_of(j, i, kb, qb, nd_s, masked)
            dprob = dot(vb, g_s[block_at(i, BQ), :], ((1,), (1,)))
            ds = (probs * (dprob - row_of(nd_s, i, 1))).astype(bf16)
            dq_s[i] += dot(kt, ds, ((1,), (0,)))
            return dot(ds, qb, ((1,), (0,)))

        dk_s[...] = one(first, True)

        def per_query_block(i, _):
            dk_s[...] += one(i, False)
            return 0

        lax.fori_loop(first + 1, LENGTH // BQ, per_query_block, 0)
        for t in range(BK // TOK):
            s = inv_s[j * (BK // TOK) + t]
            to = (s // 2) ^ chip
            part = dk_s[t * TOK : (t + 1) * TOK, :] * SCALE

            @pl.when(s % 2 == core)
            def _():
                kkeep_ref[to] = part

            @pl.when(s % 2 != core)
            def _():
                ksend_ref[to] = part.astype(bf16)

        return 0

    lax.fori_loop(0, LENGTH // BK, per_key_block, 0)
    for i in range(LENGTH // BQ):
        rows = (dq_s[i].T * SCALE).astype(bf16)
        for t in range(BQ // TOK):
            s = inv_s[i * (BQ // TOK) + t]
            to = (s // 2) ^ chip
            part = rows[t * TOK : (t + 1) * TOK, :]

            @pl.when(s % 2 == core)
            def _():
                qkeep_ref[to] = part

            @pl.when(s % 2 != core)
            def _():
                qsend_ref[to] = part


def spread_kernel(keep_ref, got_ref, out_ref):
    total = (keep_ref[...] + got_ref[...].astype(f32)).astype(bf16)
    for d in range(CHIPS):
        out_ref[d] = total


def turn_kernel(x_ref, out_ref):
    for i in range(CHIPS):
        for t in range(TILES):
            out_ref[t * 128 : (t + 1) * 128, i * TOK : (i + 1) * TOK] = x_ref[i, t * TOK : (t + 1) * TOK, :].T


def weight_kernel(where_ref, xt_ref, dv_ref, keep_ref, send_ref):
    core = where_ref[0, 0]
    base = (where_ref[0, 1] % 2) * 64
    own = pl.multiple_of(base + core * ROWS, 32)
    other = pl.multiple_of(base + (1 - core) * ROWS, 32)
    grads = jnp.concatenate([dv_ref[0], dv_ref[1]], axis=1)
    mine = dot(xt_ref[pl.ds(own, ROWS), :], grads, ((1,), (0,)))
    sent = dot(xt_ref[pl.ds(other, ROWS), :], grads, ((1,), (0,))).astype(bf16)
    half = ROWS // 2
    for r in range(2):
        for h in range(2):
            keep_ref[r, h] = mine[r * half : (r + 1) * half, h * HEAD : (h + 1) * HEAD]
            send_ref[r, h] = sent[r * half : (r + 1) * half, h * HEAD : (h + 1) * HEAD]


def join_kernel(q_ref, q_came_ref, k_ref, k_came_ref, *out_refs):
    for k in range(CHIPS):
        out_refs[k][0] = q_ref[k]
        out_refs[k][1] = q_came_ref[k]
        out_refs[k][2] = (k_ref[k] + k_came_ref[k].astype(f32)).astype(bf16)


def place_kernel(where_ref, *refs):
    core = where_ref[0, 0]
    chip = where_ref[0, 1]
    q_ref, k_ref = refs[CHIPS:]
    for k in range(CHIPS):
        part = refs[k]
        head = chip ^ k
        q_ref[:, block_at(2 * head + core, HEAD)] = part[0]
        q_ref[:, block_at(2 * head + 1 - core, HEAD)] = part[1]
        k_ref[:, block_at(head, HEAD)] = part[2]


VMEM = pl.BlockSpec(memory_space=pltpu.VMEM)
SMEM = pl.BlockSpec(memory_space=pltpu.SMEM)
TOKENS = (CHIPS, TOK, HEAD)


def shaped(shape, dtype):
    return jax.ShapeDtypeStruct(shape, dtype)


def call(kernel, specs, outs, scratch=(), flops=10**6, moved=10**6, **more):
    return pl.pallas_call(
        kernel,
        in_specs=specs,
        out_shape=outs,
        scratch_shapes=list(scratch),
        cost_estimate=pl.CostEstimate(flops=flops, bytes_accessed=moved, transcendentals=0),
        **({"out_specs": [VMEM] * len(outs)} | more),
    )


SORTED = [pltpu.VMEM((LENGTH, HEAD), bf16)] * 3
ROWED = [pltpu.VMEM((SLABS, 8, TOK), f32)]
PLACES = [pltpu.SMEM((SLABS,), jnp.int32)]
BLOCK = [pltpu.VMEM((BK, HEAD), f32)]
SWAP = [(i, i ^ 1) for i in range(SLABS)]
SAME_CORE = [list(range(c, SLABS, 2)) for c in range(2)]


def swapped(array):
    return lax.ppermute(array, "seq", SWAP)


def inner(
    query_rows, key_rows, value_rows, attn_output, output_grad, log_norm, slab_order, normed_input
):
    me = lax.axis_index("seq").astype(jnp.int32)
    where = jnp.stack([me & 1, me >> 1]).reshape(1, 2)
    (packed,) = call(
        pack_kernel, [SMEM] + [VMEM] * 5, [shaped((SLABS, PACK, HEAD), bf16)]
    )(slab_order, query_rows[0], output_grad[0], attn_output[0], key_rows[0], log_norm[0])
    got = lax.all_to_all(packed, "seq", 0, 0, tiled=True)
    (late,) = call(pack_late_kernel, [VMEM] * 2, [shaped((CHIPS, 768, 128), bf16)])(normed_input[0], value_rows[0])
    got, late = lax.optimization_barrier((got, late))
    other = swapped(got[:, 2 * TOK : 2 * TOK + HALF, :])
    late_in = lax.all_to_all(late, "seq", 0, 0, axis_index_groups=SAME_CORE, tiled=True)
    keep, send = call(
        value_kernel, [SMEM, VMEM, VMEM], [shaped(TOKENS, f32), shaped(TOKENS, bf16)],
        SORTED + ROWED + BLOCK + PLACES, flops=3 * 10**9,
    )(where, got, other)
    came = swapped(send)
    (dv,) = call(spread_kernel, [VMEM] * 2, [shaped((CHIPS, *TOKENS), bf16)])(keep, came)
    dv_all = lax.all_to_all(dv.reshape(CHIPS, LENGTH // 2, HEAD), "seq", 0, 0, axis_index_groups=SAME_CORE, tiled=True)
    v_in = late_in[:, TILES * TOK :, :]
    v_other = swapped(v_in)
    q_keep, q_send, k_keep, k_send = call(
        score_kernel, [SMEM] + [VMEM] * 4,
        [shaped(TOKENS, bf16), shaped(TOKENS, bf16), shaped(TOKENS, f32), shaped(TOKENS, bf16)],
        SORTED + [pltpu.VMEM((LENGTH, HEAD), bf16)] + ROWED
        + [pltpu.VMEM((LENGTH // BQ, HEAD, BQ), f32)] + BLOCK + PLACES,
        flops=5 * 10**9,
    )(where, got, other, v_in, v_other)
    q_came, k_came = swapped(jnp.stack([q_send, k_send]))
    (xt,) = call(turn_kernel, [VMEM], [shaped((TILES * 128, LENGTH // 2), bf16)], flops=10**9)(late_in)
    block = pl.BlockSpec((2, 2, ROWS // 2, HEAD), lambda n: (0, n, 0, 0))
    w_shape = (2, KV_HEADS, ROWS // 2, HEAD)
    w_keep, w_send = call(
        weight_kernel,
        [SMEM, VMEM, pl.BlockSpec((2, LENGTH // 2, HEAD), lambda n: (n, 0, 0))],
        [shaped(w_shape, f32), shaped(w_shape, bf16)], flops=2 * 10**9,
        grid=(KV_HEADS // 2,), out_specs=[block, block],
    )(where, xt, dv_all)
    w_came = swapped(w_send)
    w = (w_keep + w_came.astype(f32)).astype(bf16)
    w, q_keep, q_came, k_keep, k_came = lax.optimization_barrier((w, q_keep, q_came, k_keep, k_came))
    back = call(join_kernel, [VMEM] * 4, [shaped((3, TOK, HEAD), bf16)] * CHIPS)(
        q_keep, q_came, k_keep, k_came
    )
    parts = lax.all_to_all(w.reshape(SLABS, ROWS // 2, HEAD), "batch", 0, 0, tiled=True)
    pieces = [back[0]]
    for k in range(1, CHIPS):
        pieces.append(lax.ppermute(back[k], "seq", [(i, i ^ (2 * k)) for i in range(SLABS)]))
    piece = jnp.sum(parts.astype(f32), axis=0).astype(bf16)
    blocks = lax.all_to_all(
        jnp.broadcast_to(piece[None], (SLABS, ROWS // 2, HEAD)), "batch", 0, 0, tiled=True
    )
    weight = blocks.reshape(2, KV_HEADS, ROWS // 2, HEAD).transpose(0, 2, 1, 3).reshape(ROWS, KV_HEADS * HEAD)
    grad_query, grad_key = call(
        place_kernel, [SMEM] + [VMEM] * CHIPS,
        [shaped((TOK, HEADS * HEAD), bf16), shaped((TOK, KV_HEADS * HEAD), bf16)],
    )(where, *pieces)
    return (grad_query[None], grad_key[None], weight.astype(f32))


def solution(mesh):
    placed = (
        P("batch", "seq", None),
        P("batch", "seq", None),
        P("batch", "seq", None),
        P("batch", "seq", None),
        P("batch", "seq", None),
        P("batch", None, "seq"),
        P("batch", "seq"),
        P("batch", "seq", None),
    )
    return jax.shard_map(
        inner,
        mesh=mesh,
        in_specs=placed,
        out_specs=(P("batch", "seq", None), P("batch", "seq", None), P("seq", None)),
        check_vma=False,
    )
```

time: 180 us -> 168 us (0.933)
  the two profiles are of different devices: /device:TPU:2 before, /device:TPU:38 now
where the time goes in v2:
time: 168 us; the launch traced here: 167 us
  Pallas kernels  46.5 us (28%)
  starting transfers between devices  44.4 us (26%)
  waiting for transfers between devices  38.3 us (23%)
  blocking collectives  26.8 us (16%)
  local copies, waits for them, and re-layouts  6.13 us (4%)
  other arithmetic  3.24 us (2%)
    all_to_all x1, blocking collectives, inner(): lax.all_to_all(w.reshape(SLABS, ROWS // 2, HEAD), 'batch', 0, 0, tiled=True)  26.8 us
    ppermute x7, starting transfers between devices, inner(): lax.ppermute(back[k], 'seq', [(i, i ^ 2 * k) for i in range(SLABS)])  18.1 us
    all_to_all x1, waiting for transfers between devices, inner(): got = lax.all_to_all(packed, 'seq', 0, 0, tiled=True)  16.2 us
    pallas_call x1, Pallas kernels, inner(): call(score_kernel, [SMEM] + [VMEM] * 4, [shaped(TOKENS, bf16), shaped(TOK...  15.1 us
    pallas_call x1, Pallas kernels, inner(): call(value_kernel, [SMEM, VMEM, VMEM], [shaped(TOKENS, f32), shaped(TOKEN...  10.6 us
    ppermute x7, waiting for transfers between devices, inner(): lax.ppermute(back[k], 'seq', [(i, i ^ 2 * k) for i in range(SLABS)])  8.38 us
    all_to_all x1, starting transfers between devices, inner(): lax.all_to_all(dv.reshape(CHIPS, LENGTH // 2, HEAD), 'seq', 0, 0, axis_in...  7.67 us
    all_to_all x1, starting transfers between devices, inner(): got = lax.all_to_all(packed, 'seq', 0, 0, tiled=True)  7.43 us
  transfers between devices with their start and end apart: 16, of which 8 were waited for; matrix products, arithmetic and copies ran while one was open for 2% of the time, Pallas kernels for 26%

profile of v2, /device:TPU:38, one launch (start us, length us, event | category | flops | bytes accessed | tf_op | source)
XLA Modules:
  0.0 166.8 jit_solution(3966156404895968461)
XLA Ops:
  1.3 2.9 %shard_map.103 = bf16[16,328,128]{2,1,0:T(8,128)(2,1)} custom-call(s32[1,1]{1,0:T(1,128)S(6)} %copy.15.place_ref, bf16[128,2048]{1,0:T(8,128)(2,1)} %bitcast.36, bf16[128,2048]{1,0:T(8,128)(2,1)} %bitcast.37, bf16[128,2048]{1,0:T(8,128)(2,1)} %bitcast.38, bf16[128,1024]{1,0:T(8,128)(2,1)} %bitcast.42, f32[16,128]{1,0:T(8,128)} %bitcast.43), custom_call_target="tpu_custom_call" | custom-call | flops 1000000 | bytes 1000000 | tf_op jit(solution)/shard_map/pallas_call | solution.py:286
  4.2 7.4 %all-to-all-start = ((bf16[16,328,128]{2,1,0:T(8,128)(2,1)}), bf16[16,328,128]{2,1,0:T(8,128)(2,1)S(1)}, u32[]{:S(2)}, u32[]{:S(2)}) async-start(bf16[16,328,128]{2,1,0:T(8,128)(2,1)} %shard_map.103), calls=%async_computation | async-start | bytes 2686976 | tf_op jit(solution)/shard_map/all_to_all | solution.py:289
  11.6 2.7 %shard_map.104 = bf16[8,768,128]{2,1,0:T(8,128)(2,1)} custom-call(bf16[128,4608]{1,0:T(8,128)(2,1)} %bitcast.35, bf16[128,1024]{1,0:T(8,128)(2,1)} %bitcast.39), custom_call_target="tpu_custom_call" | custom-call | flops 1000000 | bytes 1000000 | tf_op jit(solution)/shard_map/pallas_call | solution.py:290
  14.4 16.2 %all-to-all-done.in_ref = bf16[16,328,128]{2,1,0:T(8,128)(2,1)S(1)} async-done(((bf16[16,328,128]{2,1,0:T(8,128)(2,1)}), bf16[16,328,128]{2,1,0:T(8,128)(2,1)S(1)}, u32[]{:S(2)}, u32[]{:S(2)}) %all-to-all-start) | async-done | bytes 1343520 | tf_op jit(solution)/shard_map/all_to_all | solution.py:289
  30.6 5.8 %all-to-all-start.1 = ((bf16[8,768,128]{2,1,0:T(8,128)(2,1)}), bf16[8,768,128]{2,1,0:T(8,128)(2,1)S(1)}, u32[]{:S(2)}, u32[]{:S(2)}) async-start(bf16[8,768,128]{2,1,0:T(8,128)(2,1)} %shard_map.104), calls=%async_computation.1 | async-start | bytes 3145728 | tf_op jit(solution)/shard_map/all_to_all | solution.py:293
  36.4 0.0 copy-done.1
  36.4 0.1 collective-permute-start
  36.5 0.6 add_bitcast_fusion.where_ref
  37.1 0.9 collective-permute-done.oth_ref
  38.0 0.7 copy-done.11
  38.7 10.6 %shard_map.106 = (f32[8,128,128]{2,1,0:T(8,128)}, bf16[8,128,128]{2,1,0:T(8,128)(2,1)}) custom-call(s32[1,2]{1,0:T(1,128)} %add_bitcast_fusion.where_ref, bf16[16,328,128]{2,1,0:T(8,128)(2,1)} %copy-done.1, bf16[16,64,128]{2,1,0:T(8,128)(2,1)} %copy-done.11), custom_call_target="tpu_custom_call" | custom-call | flops 3000000000 | bytes 1000000 | tf_op jit(solution)/shard_map/pallas_call | solution.py:294
  49.4 0.1 collective-permute-start.1
  49.5 1.6 collective-permute-done.1.got_ref
  51.1 0.7 copy-done.3
  51.8 2.6 %shard_map.107 = bf16[8,8,128,128]{3,2,1,0:T(8,128)(2,1)} custom-call(f32[8,128,128]{2,1,0:T(8,128)} %get-tuple-element.30.keep_ref, bf16[8,128,128]{2,1,0:T(8,128)(2,1)} %copy-done.3), custom_call_target="tpu_custom_call" | custom-call | flops 1000000 | bytes 1000000 | tf_op jit(solution)/shard_map/pallas_call | solution.py:299
  54.4 3.2 %all-to-all-done.1.x_ref = bf16[8,768,128]{2,1,0:T(8,128)(2,1)S(1)} async-done(((bf16[8,768,128]{2,1,0:T(8,128)(2,1)}), bf16[8,768,128]{2,1,0:T(8,128)(2,1)S(1)}, u32[]{:S(2)}, u32[]{:S(2)}) %all-to-all-start.1) | async-done | bytes 1572896 | tf_op jit(solution)/shard_map/all_to_all | solution.py:293
  57.6 7.7 %all-to-all-start.2 = ((bf16[8,1024,128]{2,1,0:T(8,128)(2,1)}), bf16[8,1024,128]{2,1,0:T(8,128)(2,1)}, u32[]{:S(2)}, u32[]{:S(2)}) async-start(bf16[8,1024,128]{2,1,0:T(8,128)(2,1)} %bitcast.30), calls=%async_computation.2 | async-start | bytes 4194304 | tf_op jit(solution)/shard_map/all_to_all | solution.py:300
  65.3 0.0 copy-done
  65.3 0.0 copy-start.2
  65.3 0.1 collective-permute-start.3
  65.4 3.0 %shard_map.105.xt_ref = bf16[640,1024]{1,0:T(8,128)(2,1)} custom-call(bf16[8,768,128]{2,1,0:T(8,128)(2,1)} %copy-done), custom_call_target="tpu_custom_call" | custom-call | flops 1000000000 | bytes 1000000 | tf_op jit(solution)/shard_map/pallas_call | solution.py:311
  68.4 0.0 copy-done.2
  68.4 0.0 collective-permute-done.3.voth_ref
  68.4 0.7 copy-done.12
  69.2 15.1 %shard_map.109 = (bf16[8,128,128]{2,1,0:T(8,128)(2,1)}, bf16[8,128,128]{2,1,0:T(8,128)(2,1)}, f32[8,128,128]{2,1,0:T(8,128)}, bf16[8,128,128]{2,1,0:T(8,128)(2,1)}) custom-call(s32[1,2]{1,0:T(1,128)} %add_bitcast_fusion.where_ref, bf16[16,328,128]{2,1,0:T(8,128)(2,1)} %copy-done.1, bf16[16,64,128]{2,1,0:T(8,128)(2,1)} %copy-done.11, ...), custom_call_target="tpu_custom_call" | custom-call | flops 5000000000 | bytes 1000000 | tf_op jit(solution)/shard_map/pallas_call | solution.py:303
  84.3 1.1 pad_maximum_fusion
  85.3 0.6 collective-permute-start.4
  85.9 6.6 %all-to-all-done.2.dv_ref = bf16[8,1024,128]{2,1,0:T(8,128)(2,1)} async-done(((bf16[8,1024,128]{2,1,0:T(8,128)(2,1)}), bf16[8,1024,128]{2,1,0:T(8,128)(2,1)}, u32[]{:S(2)}, u32[]{:S(2)}) %all-to-all-start.2) | async-done | bytes 2097184 | tf_op jit(solution)/shard_map/all_to_all | solution.py:300
  92.5 5.0 %shard_map.108 = (f32[2,8,144,128]{3,2,1,0:T(8,128)}, bf16[2,8,144,128]{3,2,1,0:T(8,128)(2,1)}) custom-call(s32[1,2]{1,0:T(1,128)} %add_bitcast_fusion.where_ref, bf16[640,1024]{1,0:T(8,128)(2,1)} %shard_map.105.xt_ref, bf16[8,1024,128]{2,1,0:T(8,128)(2,1)} %all-to-all-done.2.dv_ref), custom_call_target="tpu_custom_call" | custom-call | flops 2000000000 | bytes 1000000 | tf_op jit(solution)/shard_map/pallas_call | solution.py:314
  97.6 0.0 collective-permute-start.2
  97.6 0.0 collective-permute-done.4
  97.6 0.8 slice_bitcast_fusion
  98.4 1.4 collective-permute-done.2
  99.8 1.4 add_convert_fusion
  101.2 26.8 %all_to_all.25 = bf16[16,144,128]{2,1,0:T(8,128)(2,1)S(1)} all-to-all(bf16[16,144,128]{2,1,0:T(8,128)(2,1)S(1)} %bitcast.33), channel_id=1, replica_groups=mesh['seq'=16,'batch'=16] {'batch'}, dimensions={0} | all-to-all | bytes 1179648 | tf_op jit(solution)/shard_map/all_to_all | solution.py:326
  128.0 0.1 reduce_sum.12
  128.1 0.9 broadcast_in_dim.14
  129.0 4.5 %all-to-all-start.4 = ((bf16[16,144,128]{2,1,0:T(8,128)(2,1)}), bf16[16,144,128]{2,1,0:T(8,128)(2,1)S(1)}, u32[]{:S(2)}, u32[]{:S(2)}) async-start(bf16[16,144,128]{2,1,0:T(8,128)(2,1)} %broadcast_in_dim.14), calls=%async_computation.4 | async-start | bytes 1179648 | tf_op jit(solution)/shard_map/all_to_all | solution.py:331
  133.5 2.2 %shard_map.110 = (bf16[3,128,128]{2,1,0:T(8,128)(2,1)}, bf16[3,128,128]{2,1,0:T(8,128)(2,1)}, bf16[3,128,128]{2,1,0:T(8,128)(2,1)}, bf16[3,128,128]{2,1,0:T(8,12...) custom-call(bf16[8,128,128]{2,1,0:T(8,128)(2,1)} %get-tuple-element., ...), custom_call_target="tpu_custom_call" | custom-call | flops 1000000 | bytes 1000000 | tf_op jit(solution)/shard_map/pallas_call | solution.py:323
  135.7 3.0 %collective-permute-start.5 = (bf16[3,128,128]{2,1,0:T(8,128)(2,1)}, bf16[3,128,128]{2,1,0:T(8,128)(2,1)S(1)}, u32[]{:S(2)}, u32[]{:S(2)}) collective-permute-start(bf16[3,128,128]{2,1,0:T(8,128)(2,1)} %get-tuple-element.43), channel_id=1, source_target_pairs={{0,32},{16,48},{32,0},{48,16},{64,96},{80,112},{96,64},{112,80},{1... | collective-permute-start | bytes 294920 | tf_op jit(solution)/shard_map/ppermute | solution.py:329
  138.6 0.0 collective-permute-start.6
  138.6 2.0 %collective-permute-start.7 = (bf16[3,128,128]{2,1,0:T(8,128)(2,1)}, bf16[3,128,128]{2,1,0:T(8,128)(2,1)S(1)}, u32[]{:S(2)}, u32[]{:S(2)}) collective-permute-start(bf16[3,128,128]{2,1,0:T(8,128)(2,1)} %get-tuple-element.45), channel_id=1, source_target_pairs={{0,96},{16,112},{32,64},{48,80},{64,32},{80,48},{96,0},{112,16},{1... | collective-permute-start | bytes 294920 | tf_op jit(solution)/shard_map/ppermute | solution.py:329
  140.7 3.0 %collective-permute-start.8 = (bf16[3,128,128]{2,1,0:T(8,128)(2,1)}, bf16[3,128,128]{2,1,0:T(8,128)(2,1)S(1)}, u32[]{:S(2)}, u32[]{:S(2)}) collective-permute-start(bf16[3,128,128]{2,1,0:T(8,128)(2,1)} %get-tuple-element.46), channel_id=1, source_target_pairs={{0,128},{16,144},{32,160},{48,176},{64,192},{80,208},{96,224},{112... | collective-permute-start | bytes 294920 | tf_op jit(solution)/shard_map/ppermute | solution.py:329
  143.6 2.9 %collective-permute-start.9 = (bf16[3,128,128]{2,1,0:T(8,128)(2,1)}, bf16[3,128,128]{2,1,0:T(8,128)(2,1)S(1)}, u32[]{:S(2)}, u32[]{:S(2)}) collective-permute-start(bf16[3,128,128]{2,1,0:T(8,128)(2,1)} %get-tuple-element.47), channel_id=1, source_target_pairs={{0,160},{16,176},{32,128},{48,144},{64,224},{80,240},{96,192},{112... | collective-permute-start | bytes 294920 | tf_op jit(solution)/shard_map/ppermute | solution.py:329
  146.6 0.0 collective-permute-done.5.refs_1_
  146.6 7.1 %collective-permute-start.10 = (bf16[3,128,128]{2,1,0:T(8,128)(2,1)}, bf16[3,128,128]{2,1,0:T(8,128)(2,1)S(1)}, u32[]{:S(2)}, u32[]{:S(2)}) collective-permute-start(bf16[3,128,128]{2,1,0:T(8,128)(2,1)} %get-tuple-element.48), channel_id=1, source_target_pairs={{0,192},{16,208},{32,224},{48,240},{64,128},{80,144},{96,160},{112... | collective-permute-start | bytes 294920 | tf_op jit(solution)/shard_map/ppermute | solution.py:329
  153.7 0.0 collective-permute-done.6.refs_2_
  153.7 0.0 collective-permute-start.11
  153.7 0.0 collective-permute-done.7.refs_3_
  153.8 0.0 copy-start.6
  153.8 0.0 collective-permute-done.8.refs_4_
  153.8 0.0 copy-start.7
  153.8 0.0 collective-permute-done.9.refs_5_
  153.8 0.0 copy-start.8
  153.8 2.7 %collective-permute-done.10.refs_6_ = bf16[3,128,128]{2,1,0:T(8,128)(2,1)S(1)} collective-permute-done((bf16[3,128,128]{2,1,0:T(8,128)(2,1)}, bf16[3,128,128]{2,1,0:T(8,128)(2,1)S(1)}, u32[]{:S(2)}, u32[]{:S(2)}) %collective-permute-start.10) | collective-permute-done | bytes 98336 | tf_op jit(solution)/shard_map/ppermute | solution.py:329
  156.5 5.6 %collective-permute-done.11.refs_7_ = bf16[3,128,128]{2,1,0:T(8,128)(2,1)S(1)} collective-permute-done((bf16[3,128,128]{2,1,0:T(8,128)(2,1)}, bf16[3,128,128]{2,1,0:T(8,128)(2,1)S(1)}, u32[]{:S(2)}, u32[]{:S(2)}) %collective-permute-start.11) | collective-permute-done | bytes 98336 | tf_op jit(solution)/shard_map/ppermute | solution.py:329
  162.2 0.0 copy-done.4
  162.2 0.0 copy-done.5
  162.2 0.6 copy-done.10
  162.8 2.3 %shard_map.111 = (bf16[128,2048]{1,0:T(8,128)(2,1)}, bf16[128,1024]{1,0:T(8,128)(2,1)}) custom-call(s32[1,2]{1,0:T(1,128)} %add_bitcast_fusion.where_ref, bf16[3,128,128]{2,1,0:T(8,128)(2,1)} %get-tuple-element.42.refs_0_, bf16[3,128,128]{2,1,0:T(8,128)(2,1)} %copy-done.4, bf16[3,128,128]{2,1,0:T(8,128)(2,1)} %copy-done.5, bf16[3,128,128]{2,1,0:T(8,128)(2,1)} %copy-done.6, ...), custom_call_target="tpu_custom_call" | custom-call | flops 1000000 | bytes 1000000 | tf_op jit(solution)/shard_map/pallas_call | solution.py:335
  165.1 0.0 all-to-all-done.4
  165.1 0.1 convert_bitcast_fusion
  165.2 0.4 copy.11
  165.6 1.2 copy.14
  (15 shorter events, 0.1 us)
Async XLA Ops:
  4.2 26.3 %all-to-all-start = ((bf16[16,328,128]{2,1,0:T(8,128)(2,1)}), bf16[16,328,128]{2,1,0:T(8,128)(2,1)S(1)}, u32[]{:S(2)}, u32[]{:S(2)}) async-start(bf16[16,328,128]{2,1,0:T(8,128)(2,1)} %shard_map.103), calls=%async_computation | async-start | bytes 2686976 | tf_op jit(solution)/shard_map/all_to_all | solution.py:289
  30.6 5.8 %copy-start.1 = (bf16[16,328,128]{2,1,0:T(8,128)(2,1)}, bf16[16,328,128]{2,1,0:T(8,128)(2,1)S(1)}, u32[]{:S(2)}) copy-start(bf16[16,328,128]{2,1,0:T(8,128)(2,1)S(1)} %all-to-all-done.in_ref) | copy-start | bytes 4030468
  30.6 27.1 %all-to-all-start.1 = ((bf16[8,768,128]{2,1,0:T(8,128)(2,1)}), bf16[8,768,128]{2,1,0:T(8,128)(2,1)S(1)}, u32[]{:S(2)}, u32[]{:S(2)}) async-start(bf16[8,768,128]{2,1,0:T(8,128)(2,1)} %shard_map.104), calls=%async_computation.1 | async-start | bytes 3145728 | tf_op jit(solution)/shard_map/all_to_all | solution.py:293
  36.4 1.6 collective-permute-start
  38.0 0.7 copy-start.11
  49.4 1.7 %collective-permute-start.1 = (bf16[8,128,128]{2,1,0:T(8,128)(2,1)}, bf16[8,128,128]{2,1,0:T(8,128)(2,1)S(1)}, u32[]{:S(2)}, u32[]{:S(2)}) collective-permute-start(bf16[8,128,128]{2,1,0:T(8,128)(2,1)} %get-tuple-element.31), channel_id=1, source_target_pairs={{0,16},{16,0},{32,48},{48,32},{64,80},{80,64},{96,112},{112,96},{1... | collective-permute-start | bytes 786440 | tf_op jit(solution)/shard_map/ppermute | solution.py:278
  51.1 0.7 copy-start.3
  57.6 7.7 %copy-start = (bf16[8,768,128]{2,1,0:T(8,128)(2,1)}, bf16[8,768,128]{2,1,0:T(8,128)(2,1)S(1)}, u32[]{:S(2)}) copy-start(bf16[8,768,128]{2,1,0:T(8,128)(2,1)S(1)} %all-to-all-done.1.x_ref) | copy-start | bytes 4718596
  57.6 34.9 %all-to-all-start.2 = ((bf16[8,1024,128]{2,1,0:T(8,128)(2,1)}), bf16[8,1024,128]{2,1,0:T(8,128)(2,1)}, u32[]{:S(2)}, u32[]{:S(2)}) async-start(bf16[8,1024,128]{2,1,0:T(8,128)(2,1)} %bitcast.30), calls=%async_computation.2 | async-start | bytes 4194304 | tf_op jit(solution)/shard_map/all_to_all | solution.py:300
  65.3 3.1 %copy-start.2 = (bf16[8,128,128]{2,1,0:T(8,128)(2,1)}, bf16[8,128,128]{2,1,0:T(8,128)(2,1)S(1)}, u32[]{:S(2)}) copy-start(bf16[8,128,128]{2,1,0:T(8,128)(2,1)S(1)} %slice.8.v_ref) | copy-start | bytes 786436
  65.3 3.1 %collective-permute-start.3 = (bf16[8,128,128]{2,1,0:T(8,128)(2,1)S(1)}, bf16[8,128,128]{2,1,0:T(8,128)(2,1)S(1)}, u32[]{:S(2)}, u32[]{:S(2)}) collective-permute-start(bf16[8,128,128]{2,1,0:T(8,128)(2,1)S(1)} %slice.8.v_ref), channel_id=1, source_target_pairs={{0,16},{16,0},{32,48},{48,32},{64,80},{80,64},{96,112},{112,96},{1... | collective-permute-start | bytes 786440 | tf_op jit(solution)/shard_map/ppermute | solution.py:278
  68.4 0.7 copy-start.12
  85.3 12.2 %collective-permute-start.4 = (bf16[2,8,128,128]{3,2,1,0:T(8,128)(2,1)S(1)}, bf16[2,8,128,128]{3,2,1,0:T(8,128)(2,1)S(1)}, u32[]{:S(2)}, u32[]{:S(2)}) collective-permute-start(bf16[2,8,128,128]{3,2,1,0:T(8,128)(2,1)S(1)} %pad_maximum_fusion), channel_id=1, source_target_pairs={{0,16},{16,0},{32,48},{48,32},{64,80},{80,64},{96,112},{112,96},{1... | collective-permute-start | bytes 1572872 | tf_op jit(solution)/shard_map/ppermute | solution.py:278
  97.6 2.2 %collective-permute-start.2 = (bf16[2,8,144,128]{3,2,1,0:T(8,128)(2,1)}, bf16[2,8,144,128]{3,2,1,0:T(8,128)(2,1)S(1)}, u32[]{:S(2)}, u32[]{:S(2)}) collective-permute-start(bf16[2,8,144,128]{3,2,1,0:T(8,128)(2,1)} %get-tuple-element.33), channel_id=1, source_target_pairs={{0,16},{16,0},{32,48},{48,32},{64,80},{80,64},{96,112},{112,96},{1... | collective-permute-start | bytes 1769480 | tf_op jit(solution)/shard_map/ppermute | solution.py:278
  129.0 36.1 %all-to-all-start.4 = ((bf16[16,144,128]{2,1,0:T(8,128)(2,1)}), bf16[16,144,128]{2,1,0:T(8,128)(2,1)S(1)}, u32[]{:S(2)}, u32[]{:S(2)}) async-start(bf16[16,144,128]{2,1,0:T(8,128)(2,1)} %broadcast_in_dim.14), calls=%async_computation.4 | async-start | bytes 1179648 | tf_op jit(solution)/shard_map/all_to_all | solution.py:331
  135.7 10.9 %collective-permute-start.5 = (bf16[3,128,128]{2,1,0:T(8,128)(2,1)}, bf16[3,128,128]{2,1,0:T(8,128)(2,1)S(1)}, u32[]{:S(2)}, u32[]{:S(2)}) collective-permute-start(bf16[3,128,128]{2,1,0:T(8,128)(2,1)} %get-tuple-element.43), channel_id=1, source_target_pairs={{0,32},{16,48},{32,0},{48,16},{64,96},{80,112},{96,64},{112,80},{1... | collective-permute-start | bytes 294920 | tf_op jit(solution)/shard_map/ppermute | solution.py:329
  138.6 15.1 %collective-permute-start.6 = (bf16[3,128,128]{2,1,0:T(8,128)(2,1)}, bf16[3,128,128]{2,1,0:T(8,128)(2,1)S(1)}, u32[]{:S(2)}, u32[]{:S(2)}) collective-permute-start(bf16[3,128,128]{2,1,0:T(8,128)(2,1)} %get-tuple-element.44), channel_id=1, source_target_pairs={{0,64},{16,80},{32,96},{48,112},{64,0},{80,16},{96,32},{112,48},{1... | collective-permute-start | bytes 294920 | tf_op jit(solution)/shard_map/ppermute | solution.py:329
  138.6 15.1 %collective-permute-start.7 = (bf16[3,128,128]{2,1,0:T(8,128)(2,1)}, bf16[3,128,128]{2,1,0:T(8,128)(2,1)S(1)}, u32[]{:S(2)}, u32[]{:S(2)}) collective-permute-start(bf16[3,128,128]{2,1,0:T(8,128)(2,1)} %get-tuple-element.45), channel_id=1, source_target_pairs={{0,96},{16,112},{32,64},{48,80},{64,32},{80,48},{96,0},{112,16},{1... | collective-permute-start | bytes 294920 | tf_op jit(solution)/shard_map/ppermute | solution.py:329
  140.7 13.1 %collective-permute-start.8 = (bf16[3,128,128]{2,1,0:T(8,128)(2,1)}, bf16[3,128,128]{2,1,0:T(8,128)(2,1)S(1)}, u32[]{:S(2)}, u32[]{:S(2)}) collective-permute-start(bf16[3,128,128]{2,1,0:T(8,128)(2,1)} %get-tuple-element.46), channel_id=1, source_target_pairs={{0,128},{16,144},{32,160},{48,176},{64,192},{80,208},{96,224},{112... | collective-permute-start | bytes 294920 | tf_op jit(solution)/shard_map/ppermute | solution.py:329
  143.6 10.1 %collective-permute-start.9 = (bf16[3,128,128]{2,1,0:T(8,128)(2,1)}, bf16[3,128,128]{2,1,0:T(8,128)(2,1)S(1)}, u32[]{:S(2)}, u32[]{:S(2)}) collective-permute-start(bf16[3,128,128]{2,1,0:T(8,128)(2,1)} %get-tuple-element.47), channel_id=1, source_target_pairs={{0,160},{16,176},{32,128},{48,144},{64,224},{80,240},{96,192},{112... | collective-permute-start | bytes 294920 | tf_op jit(solution)/shard_map/ppermute | solution.py:329
  146.6 15.6 %copy-start.4 = (bf16[3,128,128]{2,1,0:T(8,128)(2,1)}, bf16[3,128,128]{2,1,0:T(8,128)(2,1)S(1)}, u32[]{:S(2)}) copy-start(bf16[3,128,128]{2,1,0:T(8,128)(2,1)S(1)} %collective-permute-done.5.refs_1_) | copy-start | bytes 294916
  146.6 9.9 %collective-permute-start.10 = (bf16[3,128,128]{2,1,0:T(8,128)(2,1)}, bf16[3,128,128]{2,1,0:T(8,128)(2,1)S(1)}, u32[]{:S(2)}, u32[]{:S(2)}) collective-permute-start(bf16[3,128,128]{2,1,0:T(8,128)(2,1)} %get-tuple-element.48), channel_id=1, source_target_pairs={{0,192},{16,208},{32,224},{48,240},{64,128},{80,144},{96,160},{112... | collective-permute-start | bytes 294920 | tf_op jit(solution)/shard_map/ppermute | solution.py:329
  153.7 8.5 %copy-start.5 = (bf16[3,128,128]{2,1,0:T(8,128)(2,1)}, bf16[3,128,128]{2,1,0:T(8,128)(2,1)S(1)}, u32[]{:S(2)}) copy-start(bf16[3,128,128]{2,1,0:T(8,128)(2,1)S(1)} %collective-permute-done.6.refs_2_) | copy-start | bytes 294916
  153.7 8.4 %collective-permute-start.11 = (bf16[3,128,128]{2,1,0:T(8,128)(2,1)}, bf16[3,128,128]{2,1,0:T(8,128)(2,1)S(1)}, u32[]{:S(2)}, u32[]{:S(2)}) collective-permute-start(bf16[3,128,128]{2,1,0:T(8,128)(2,1)} %get-tuple-element.49), channel_id=1, source_target_pairs={{0,224},{16,240},{32,192},{48,208},{64,160},{80,176},{96,128},{112... | collective-permute-start | bytes 294920 | tf_op jit(solution)/shard_map/ppermute | solution.py:329
  153.8 8.4 %copy-start.6 = (bf16[3,128,128]{2,1,0:T(8,128)(2,1)}, bf16[3,128,128]{2,1,0:T(8,128)(2,1)S(1)}, u32[]{:S(2)}) copy-start(bf16[3,128,128]{2,1,0:T(8,128)(2,1)S(1)} %collective-permute-done.7.refs_3_) | copy-start | bytes 294916
  153.8 8.4 %copy-start.7 = (bf16[3,128,128]{2,1,0:T(8,128)(2,1)}, bf16[3,128,128]{2,1,0:T(8,128)(2,1)S(1)}, u32[]{:S(2)}) copy-start(bf16[3,128,128]{2,1,0:T(8,128)(2,1)S(1)} %collective-permute-done.8.refs_4_) | copy-start | bytes 294916
  153.8 8.4 %copy-start.8 = (bf16[3,128,128]{2,1,0:T(8,128)(2,1)}, bf16[3,128,128]{2,1,0:T(8,128)(2,1)S(1)}, u32[]{:S(2)}) copy-start(bf16[3,128,128]{2,1,0:T(8,128)(2,1)S(1)} %collective-permute-done.9.refs_5_) | copy-start | bytes 294916
  156.5 5.7 %copy-start.9 = (bf16[3,128,128]{2,1,0:T(8,128)(2,1)}, bf16[3,128,128]{2,1,0:T(8,128)(2,1)S(1)}, u32[]{:S(2)}) copy-start(bf16[3,128,128]{2,1,0:T(8,128)(2,1)S(1)} %collective-permute-done.10.refs_6_) | copy-start | bytes 294916
  162.2 0.6 copy-start.10

commit v3 on v2

--- a/solution.py
+++ b/solution.py
@@ -3,7 +3,7 @@
 from jax import lax
 from jax.experimental import pallas as pl
 from jax.experimental.pallas import tpu as pltpu
-from jax.sharding import PartitionSpec as P
+from jax.sharding import Mesh, PartitionSpec as P
 
 
 HEADS = 16
@@ -15,11 +15,13 @@
 CHIPS = 8
 D = 4608
 ROWS = D // SLABS
+QUARTER = ROWS // 4
 BK = 256
 BQ = 512
 HALF = TOK // 2
 PACK = 2 * TOK + HALF + 8
-TILES = 5
+TILES = 9
+XS = 4
 
 SCALE = 144.0 ** (-0.5)
 LOG2E = 1.4426950408889634
@@ -40,7 +42,9 @@
     return hi, mid, low
 
 
-def pack_kernel(place_ref, q_ref, g_ref, o_ref, k_ref, n_ref, out_ref):
+def pack_kernel(place_ref, where_ref, q_ref, g_ref, o_ref, k_ref, v_ref, n_ref, out_ref, v_out_ref):
+    for x in range(XS):
+        v_out_ref[x] = v_ref[:, block_at(2 * x + 1 - where_ref[0, 2], HEAD)]
     place = jnp.full((1, TOK), place_ref[0, 0], jnp.int32).astype(f32)
     for s in range(SLABS):
         cols = slice(s * HEAD, (s + 1) * HEAD)
@@ -56,12 +60,13 @@
         out_ref[s, 2 * TOK + HALF :, :] = jnp.concatenate(rows, axis=0).astype(bf16)
 
 
-def pack_late_kernel(x_ref, v_ref, out_ref):
-    for d in range(CHIPS):
-        first = 9 * (d // 2) + 4 * (d % 2)
+def pack_late_kernel(where_ref, x_ref, v_ref, v_came_ref, out_ref):
+    for x in range(XS):
         for t in range(TILES):
-            out_ref[d, t * TOK : (t + 1) * TOK, :] = x_ref[:, (first + t) * 128 : (first + t + 1) * 128]
-        out_ref[d, TILES * TOK :, :] = v_ref[:, d * HEAD : (d + 1) * HEAD]
+            tile = TILES * x + t
+            out_ref[x, t * TOK : (t + 1) * TOK, :] = x_ref[:, tile * 128 : (tile + 1) * 128].T
+        out_ref[x, TILES * TOK : (TILES + 1) * TOK, :] = v_ref[:, block_at(2 * x + where_ref[0, 2], HEAD)]
+        out_ref[x, (TILES + 1) * TOK :, :] = v_came_ref[x]
 
 
 def sort_slabs(core, in_ref, oth_ref, q_s, g_s, k_s, nd_s, inv_s):
@@ -135,7 +140,7 @@
 
 
 def score_kernel(
-    where_ref, in_ref, oth_ref, v_ref, voth_ref, qkeep_ref, qsend_ref, kkeep_ref, ksend_ref,
+    where_ref, in_ref, oth_ref, v_ref, voth_ref, qkeep_ref, kkeep_ref, send_ref,
     q_s, g_s, k_s, v_s, nd_s, dq_s, dk_s, inv_s,
 ):
     core = where_ref[0, 0]
@@ -144,7 +149,9 @@
     for p in range(SLABS):
         s = inv_s[p]
         at = slice(p * TOK, (p + 1) * TOK)
-        v_s[at, :] = jnp.where(s % 2 == core, v_ref[s // 2], voth_ref[s // 2])
+        at_x = s // 4
+        rows = block_at(((s // 2) ^ chip) & 1, TOK)
+        v_s[at, :] = jnp.where(s % 2 == core, v_ref[at_x, rows, :], voth_ref[at_x, rows, :])
     dq_s[...] = jnp.zeros_like(dq_s)
 
     def per_key_block(j, _):
@@ -179,7 +186,7 @@
 
             @pl.when(s % 2 != core)
             def _():
-                ksend_ref[to] = part.astype(bf16)
+                send_ref[1, to] = part.astype(bf16)
 
         return 0
 
@@ -197,41 +204,53 @@
 
             @pl.when(s % 2 != core)
             def _():
-                qsend_ref[to] = part
-
-
-def spread_kernel(keep_ref, got_ref, out_ref):
-    total = (keep_ref[...] + got_ref[...].astype(f32)).astype(bf16)
-    for d in range(CHIPS):
-        out_ref[d] = total
-
-
-def turn_kernel(x_ref, out_ref):
+                send_ref[0, to] = part
+
+
+def sum_kernel(keep_ref, came_ref, out_ref):
+    out_ref[...] = (keep_ref[...] + came_ref[...].astype(f32)).astype(bf16)
+
+
+def weight_kernel(where_ref, mine_ref, came_ref, *refs):
+    core = where_ref[0, 0]
+    high = where_ref[0, 2]
+    at_x = where_ref[0, 3]
+    dv_refs, (keep_ref, send_ref, grad_s) = refs[:XS], refs[XS:]
     for i in range(CHIPS):
-        for t in range(TILES):
-            out_ref[t * 128 : (t + 1) * 128, i * TOK : (i + 1) * TOK] = x_ref[i, t * TOK : (t + 1) * TOK, :].T
-
-
-def weight_kernel(where_ref, xt_ref, dv_ref, keep_ref, send_ref):
-    core = where_ref[0, 0]
-    base = (where_ref[0, 1] % 2) * 64
-    own = pl.multiple_of(base + core * ROWS, 32)
-    other = pl.multiple_of(base + (1 - core) * ROWS, 32)
-    grads = jnp.concatenate([dv_ref[0], dv_ref[1]], axis=1)
-    mine = dot(xt_ref[pl.ds(own, ROWS), :], grads, ((1,), (0,)))
-    sent = dot(xt_ref[pl.ds(other, ROWS), :], grads, ((1,), (0,))).astype(bf16)
-    half = ROWS // 2
-    for r in range(2):
-        for h in range(2):
-            keep_ref[r, h] = mine[r * half : (r + 1) * half, h * HEAD : (h + 1) * HEAD]
-            send_ref[r, h] = sent[r * half : (r + 1) * half, h * HEAD : (h + 1) * HEAD]
-
-
-def join_kernel(q_ref, q_came_ref, k_ref, k_came_ref, *out_refs):
+        slab = 2 * (i % XS) + (high if i < XS else 1 - high)
+        for k in range(XS):
+            grad_s[i * TOK : (i + 1) * TOK, k * HEAD : (k + 1) * HEAD] = dv_refs[k][slab]
+    grads = grad_s[...]
+
+    def rows_of(part, c):
+        at = pl.ds(pl.multiple_of(part * 2 * ROWS + c * ROWS, 32), ROWS)
+        tokens = [mine_ref[i, at, :] for i in range(XS)] + [came_ref[i, at, :] for i in range(XS)]
+        return dot(jnp.concatenate(tokens, axis=1), grads, ((1,), (0,)))
+
+    for part in range(2):
+        mine = rows_of(part, core)
+        for k in range(XS):
+            for r in range(4):
+                keep_ref[r, at_x ^ k, part] = mine[r * QUARTER : (r + 1) * QUARTER, k * HEAD : (k + 1) * HEAD]
+        sent = rows_of(part, 1 - core).astype(bf16)
+        for k in range(XS):
+            for r in range(4):
+                send_ref[r, at_x ^ k, part] = sent[r * QUARTER : (r + 1) * QUARTER, k * HEAD : (k + 1) * HEAD]
+
+
+def finish_kernel(in_ref, out_ref):
+    for high in range(2):
+        for b in range(SLABS):
+            head = 2 * (b % XS) + high
+            rows = slice((b // XS) * QUARTER, (b // XS + 1) * QUARTER)
+            out_ref[rows, head * HEAD : (head + 1) * HEAD] = in_ref[high * SLABS + b].astype(f32)
+
+
+def join_kernel(q_ref, k_ref, came_ref, *out_refs):
     for k in range(CHIPS):
         out_refs[k][0] = q_ref[k]
-        out_refs[k][1] = q_came_ref[k]
-        out_refs[k][2] = (k_ref[k] + k_came_ref[k].astype(f32)).astype(bf16)
+        out_refs[k][1] = came_ref[0, k]
+        out_refs[k][2] = (k_ref[k] + came_ref[1, k].astype(f32)).astype(bf16)
 
 
 def place_kernel(where_ref, *refs):
@@ -270,90 +289,88 @@
 ROWED = [pltpu.VMEM((SLABS, 8, TOK), f32)]
 PLACES = [pltpu.SMEM((SLABS,), jnp.int32)]
 BLOCK = [pltpu.VMEM((BK, HEAD), f32)]
-SWAP = [(i, i ^ 1) for i in range(SLABS)]
-SAME_CORE = [list(range(c, SLABS, 2)) for c in range(2)]
-
-
-def swapped(array):
-    return lax.ppermute(array, "seq", SWAP)
+SEQ = ("x", "yh", "core")
+SWAP = [(0, 1), (1, 0)]
+
+
+def swapped(array, axis="core"):
+    return lax.ppermute(array, axis, SWAP)
 
 
 def inner(
     query_rows, key_rows, value_rows, attn_output, output_grad, log_norm, slab_order, normed_input
 ):
-    me = lax.axis_index("seq").astype(jnp.int32)
-    where = jnp.stack([me & 1, me >> 1]).reshape(1, 2)
-    (packed,) = call(
-        pack_kernel, [SMEM] + [VMEM] * 5, [shaped((SLABS, PACK, HEAD), bf16)]
-    )(slab_order, query_rows[0], output_grad[0], attn_output[0], key_rows[0], log_norm[0])
-    got = lax.all_to_all(packed, "seq", 0, 0, tiled=True)
-    (late,) = call(pack_late_kernel, [VMEM] * 2, [shaped((CHIPS, 768, 128), bf16)])(normed_input[0], value_rows[0])
+    core, high, at_x = (lax.axis_index(a).astype(jnp.int32) for a in ("core", "yh", "x"))
+    where = jnp.stack([core, at_x * 2 + high, high, at_x]).reshape(1, 4)
+    packed, v_high = call(
+        pack_kernel, [SMEM] * 2 + [VMEM] * 6,
+        [shaped((SLABS, PACK, HEAD), bf16), shaped((XS, TOK, HEAD), bf16)],
+    )(slab_order, where, query_rows[0], output_grad[0], attn_output[0], key_rows[0], value_rows[0], log_norm[0])
+    got = lax.all_to_all(packed, SEQ, 0, 0, tiled=True)
+    v_came = swapped(v_high, "yh")
+    (late,) = call(
+        pack_late_kernel, [SMEM] + [VMEM] * 3, [shaped((XS, (TILES + 2) * TOK, 128), bf16)]
+    )(where, normed_input[0], value_rows[0], v_came)
     got, late = lax.optimization_barrier((got, late))
     other = swapped(got[:, 2 * TOK : 2 * TOK + HALF, :])
-    late_in = lax.all_to_all(late, "seq", 0, 0, axis_index_groups=SAME_CORE, tiled=True)
+    late_in = lax.all_to_all(late, "x", 0, 0, tiled=True)
+    x_mine = late_in[:, : TILES * TOK, :]
+    x_came = swapped(x_mine, "yh")
     keep, send = call(
         value_kernel, [SMEM, VMEM, VMEM], [shaped(TOKENS, f32), shaped(TOKENS, bf16)],
         SORTED + ROWED + BLOCK + PLACES, flops=3 * 10**9,
     )(where, got, other)
     came = swapped(send)
-    (dv,) = call(spread_kernel, [VMEM] * 2, [shaped((CHIPS, *TOKENS), bf16)])(keep, came)
-    dv_all = lax.all_to_all(dv.reshape(CHIPS, LENGTH // 2, HEAD), "seq", 0, 0, axis_index_groups=SAME_CORE, tiled=True)
+    (dv,) = call(sum_kernel, [VMEM] * 2, [shaped(TOKENS, bf16)])(keep, came)
+    dvs = [dv]
+    for k in range(1, XS):
+        dvs.append(lax.ppermute(dv, "x", [(i, i ^ k) for i in range(XS)]))
     v_in = late_in[:, TILES * TOK :, :]
     v_other = swapped(v_in)
-    q_keep, q_send, k_keep, k_send = call(
+    q_keep, k_keep, qk_send = call(
         score_kernel, [SMEM] + [VMEM] * 4,
-        [shaped(TOKENS, bf16), shaped(TOKENS, bf16), shaped(TOKENS, f32), shaped(TOKENS, bf16)],
+        [shaped(TOKENS, bf16), shaped(TOKENS, f32), shaped((2, *TOKENS), bf16)],
         SORTED + [pltpu.VMEM((LENGTH, HEAD), bf16)] + ROWED
         + [pltpu.VMEM((LENGTH // BQ, HEAD, BQ), f32)] + BLOCK + PLACES,
         flops=5 * 10**9,
     )(where, got, other, v_in, v_other)
-    q_came, k_came = swapped(jnp.stack([q_send, k_send]))
-    (xt,) = call(turn_kernel, [VMEM], [shaped((TILES * 128, LENGTH // 2), bf16)], flops=10**9)(late_in)
-    block = pl.BlockSpec((2, 2, ROWS // 2, HEAD), lambda n: (0, n, 0, 0))
-    w_shape = (2, KV_HEADS, ROWS // 2, HEAD)
+    qk_came = swapped(qk_send)
+    w_shape = (4, XS, 2, QUARTER, HEAD)
     w_keep, w_send = call(
-        weight_kernel,
-        [SMEM, VMEM, pl.BlockSpec((2, LENGTH // 2, HEAD), lambda n: (n, 0, 0))],
-        [shaped(w_shape, f32), shaped(w_shape, bf16)], flops=2 * 10**9,
-        grid=(KV_HEADS // 2,), out_specs=[block, block],
-    )(where, xt, dv_all)
+        weight_kernel, [SMEM] + [VMEM] * (2 + XS),
+        [shaped(w_shape, f32), shaped(w_shape, bf16)],
+        [pltpu.VMEM((LENGTH // 2, XS * HEAD), bf16)], flops=2 * 10**9,
+    )(where, x_mine, x_came, *dvs)
     w_came = swapped(w_send)
     w = (w_keep + w_came.astype(f32)).astype(bf16)
-    w, q_keep, q_came, k_keep, k_came = lax.optimization_barrier((w, q_keep, q_came, k_keep, k_came))
-    back = call(join_kernel, [VMEM] * 4, [shaped((3, TOK, HEAD), bf16)] * CHIPS)(
-        q_keep, q_came, k_keep, k_came
+    w, q_keep, k_keep, qk_came = lax.optimization_barrier((w, q_keep, k_keep, qk_came))
+    parts = lax.all_to_all(w.reshape(SLABS, 2 * QUARTER, HEAD), "batch", 0, 0, tiled=True)
+    back = call(join_kernel, [VMEM] * 3, [shaped((3, TOK, HEAD), bf16)] * CHIPS)(
+        q_keep, k_keep, qk_came
     )
-    parts = lax.all_to_all(w.reshape(SLABS, ROWS // 2, HEAD), "batch", 0, 0, tiled=True)
     pieces = [back[0]]
     for k in range(1, CHIPS):
-        pieces.append(lax.ppermute(back[k], "seq", [(i, i ^ (2 * k)) for i in range(SLABS)]))
-    piece = jnp.sum(parts.astype(f32), axis=0).astype(bf16)
+        pieces.append(lax.ppermute(back[k], SEQ, [(i, i ^ (2 * k)) for i in range(SLABS)]))
+    piece = jnp.sum(parts.astype(f32), axis=0).astype(bf16).reshape(2, 1, QUARTER, HEAD)
     blocks = lax.all_to_all(
-        jnp.broadcast_to(piece[None], (SLABS, ROWS // 2, HEAD)), "batch", 0, 0, tiled=True
+        jnp.broadcast_to(piece, (2, SLABS, QUARTER, HEAD)).reshape(2 * SLABS, QUARTER, HEAD),
+        ("yh", "batch"), 0, 0, tiled=True,
     )
-    weight = blocks.reshape(2, KV_HEADS, ROWS // 2, HEAD).transpose(0, 2, 1, 3).reshape(ROWS, KV_HEADS * HEAD)
     grad_query, grad_key = call(
         place_kernel, [SMEM] + [VMEM] * CHIPS,
         [shaped((TOK, HEADS * HEAD), bf16), shaped((TOK, KV_HEADS * HEAD), bf16)],
     )(where, *pieces)
-    return (grad_query[None], grad_key[None], weight.astype(f32))
+    (weight,) = call(finish_kernel, [VMEM], [shaped((ROWS, KV_HEADS * HEAD), f32)])(blocks)
+    return (grad_query[None], grad_key[None], weight)
 
 
 def solution(mesh):
-    placed = (
-        P("batch", "seq", None),
-        P("batch", "seq", None),
-        P("batch", "seq", None),
-        P("batch", "seq", None),
-        P("batch", "seq", None),
-        P("batch", None, "seq"),
-        P("batch", "seq"),
-        P("batch", "seq", None),
-    )
+    fine = Mesh(mesh.devices.reshape(4, 2, 2, 16), (*SEQ, "batch"))
+    rows = P("batch", SEQ, None)
     return jax.shard_map(
         inner,
-        mesh=mesh,
-        in_specs=placed,
-        out_specs=(P("batch", "seq", None), P("batch", "seq", None), P("seq", None)),
+        mesh=fine,
+        in_specs=(rows, rows, rows, rows, rows, P("batch", None, SEQ), P("batch", SEQ), rows),
+        out_specs=(rows, rows, P(SEQ, None)),
         check_vma=False,
     )

time: 168 us -> 185 us (1.10)
  the two profiles are of different devices: /device:TPU:38 before, /device:TPU:2 now
where the time goes in v3:
time: 185 us; the launch traced here: 183 us
  blocking collectives  50.6 us (27%)
  Pallas kernels  44.5 us (24%)
  waiting for transfers between devices  39.9 us (22%)
  starting transfers between devices  38.8 us (21%)
  local copies, waits for them, and re-layouts  6.93 us (4%)
    all_to_all x1, blocking collectives, inner(): lax.all_to_all(w.reshape(SLABS, 2 * QUARTER, HEAD), 'batch', 0, 0, tiled=...  28.1 us
    ppermute x7, waiting for transfers between devices, swapped(): return lax.ppermute(array, axis, SWAP)  23 us
    all_to_all x1, blocking collectives, inner(): late_in = lax.all_to_all(late, 'x', 0, 0, tiled=True)  22.6 us
    ppermute x7, starting transfers between devices, inner(): lax.ppermute(back[k], SEQ, [(i, i ^ 2 * k) for i in range(SLABS)])  16.6 us
    pallas_call x1, Pallas kernels, inner(): call(score_kernel, [SMEM] + [VMEM] * 4, [shaped(TOKENS, bf16), shaped(TOK...  15.1 us
    ppermute x3, waiting for transfers between devices, inner(): dvs.append(lax.ppermute(dv, 'x', [(i, i ^ k) for i in range(XS)]))  11.8 us
    pallas_call x1, Pallas kernels, inner(): call(value_kernel, [SMEM, VMEM, VMEM], [shaped(TOKENS, f32), shaped(TOKEN...  10.6 us
    all_to_all x1, starting transfers between devices, inner(): got = lax.all_to_all(packed, SEQ, 0, 0, tiled=True)  7.61 us
  transfers between devices with their start and end apart: 19, of which 8 were waited for; matrix products, arithmetic and copies ran while one was open for 0% of the time, Pallas kernels for 21%

profile of v3, /device:TPU:2, one launch (start us, length us, event | category | flops | bytes accessed | tf_op | source)
XLA Modules:
  0.0 183.1 jit_solution(14057415704947501250)
XLA Ops:
  1.3 0.7 add_bitcast_fusion.where_ref
  2.0 3.0 %shard_map.103 = (bf16[16,328,128]{2,1,0:T(8,128)(2,1)}, bf16[4,128,128]{2,1,0:T(8,128)(2,1)}) custom-call(s32[1,1]{1,0:T(1,128)S(6)} %copy.11.place_ref, s32[1,4]{1,0:T(1,128)} %add_bitcast_fusion.where_ref, bf16[128,2048]{1,0:T(8,128)(2,1)} %bitcast.22, bf16[128,2048]{1,0:T(8,128)(2,1)} %bitcast.23, bf16[128,2048]{1,0:T(8,128)(2,1)} %bitcast.24, ...), custom_call_target="tpu_custom_call" | custom-call | flops 1000000 | bytes 1000000 | tf_op jit(solution)/shard_map/pallas_call | solution.py:305
  5.0 7.6 %all-to-all-start = ((bf16[16,328,128]{2,1,0:T(8,128)(2,1)}), bf16[16,328,128]{2,1,0:T(8,128)(2,1)S(1)}, u32[]{:S(2)}, u32[]{:S(2)}) async-start(bf16[16,328,128]{2,1,0:T(8,128)(2,1)} %get-tuple-element.28), calls=%async_computation | async-start | bytes 2686976 | tf_op jit(solution)/shard_map/all_to_all | solution.py:309
  12.6 3.1 %collective-permute-start = (bf16[4,128,128]{2,1,0:T(8,128)(2,1)S(1)}, bf16[4,128,128]{2,1,0:T(8,128)(2,1)S(1)}, u32[]{:S(2)}, u32[]{:S(2)}) collective-permute-start(bf16[4,128,128]{2,1,0:T(8,128)(2,1)S(1)} %copy-done.19), channel_id=1, source_target_pairs={{0,32},{32,0},{1,33},{33,1},{2,34},{34,2},{3,35},{35,3},{4,36},{36... | collective-permute-start | bytes 393224 | tf_op jit(solution)/shard_map/ppermute | solution.py:297
  15.7 18.3 %collective-permute-done.v_came_ref = bf16[4,128,128]{2,1,0:T(8,128)(2,1)S(1)} collective-permute-done((bf16[4,128,128]{2,1,0:T(8,128)(2,1)S(1)}, bf16[4,128,128]{2,1,0:T(8,128)(2,1)S(1)}, u32[]{:S(2)}, u32[]{:S(2)}) %collective-permute-start) | collective-permute-done | bytes 131104 | tf_op jit(solution)/shard_map/ppermute | solution.py:297
  33.9 0.7 copy-done.6
  34.6 2.9 %shard_map.104 = bf16[4,1408,128]{2,1,0:T(8,128)(2,1)} custom-call(s32[1,4]{1,0:T(1,128)} %add_bitcast_fusion.where_ref, bf16[128,4608]{1,0:T(8,128)(2,1)} %bitcast.19, bf16[128,1024]{1,0:T(8,128)(2,1)} %bitcast.21, bf16[4,128,128]{2,1,0:T(8,128)(2,1)} %copy-done.6), custom_call_target="tpu_custom_call" | custom-call | flops 1000000 | bytes 1000000 | tf_op jit(solution)/shard_map/pallas_call | solution.py:311
  37.5 0.0 all-to-all-done.in_ref
  37.5 22.6 %all_to_all.20 = bf16[4,1408,128]{2,1,0:T(8,128)(2,1)S(1)} all-to-all(bf16[4,1408,128]{2,1,0:T(8,128)(2,1)} %shard_map.104), channel_id=1, replica_groups=mesh['x'=4,'yh'=2,'core'=2,'batch'=16] {'x'}, dimensions={0} | all-to-all | bytes 2883584 | tf_op jit(solution)/shard_map/all_to_all | solution.py:316
  60.0 1.1 slice.12.mine_ref
  61.1 0.3 collective-permute-start.1
  61.5 0.1 collective-permute-start.2
  61.6 1.5 collective-permute-done.2.oth_ref
  63.1 0.7 copy-done.14
  63.8 10.6 %shard_map.105 = (f32[8,128,128]{2,1,0:T(8,128)}, bf16[8,128,128]{2,1,0:T(8,128)(2,1)}) custom-call(s32[1,4]{1,0:T(1,128)} %add_bitcast_fusion.where_ref, bf16[16,328,128]{2,1,0:T(8,128)(2,1)} %copy-done.1, bf16[16,64,128]{2,1,0:T(8,128)(2,1)} %copy-done.14), custom_call_target="tpu_custom_call" | custom-call | flops 3000000000 | bytes 1000000 | tf_op jit(solution)/shard_map/pallas_call | solution.py:319
  74.4 0.1 collective-permute-start.3
  74.6 1.6 collective-permute-done.3.came_ref
  76.2 0.7 copy-done.5
  76.9 1.9 %shard_map.106.refs_0_ = bf16[8,128,128]{2,1,0:T(8,128)(2,1)} custom-call(f32[8,128,128]{2,1,0:T(8,128)} %get-tuple-element.32.keep_ref, bf16[8,128,128]{2,1,0:T(8,128)(2,1)} %copy-done.5), custom_call_target="tpu_custom_call" | custom-call | flops 1000000 | bytes 1000000 | tf_op jit(solution)/shard_map/pallas_call | solution.py:324
  78.8 0.2 collective-permute-start.6
  79.0 3.3 %collective-permute-start.5 = (bf16[8,128,128]{2,1,0:T(8,128)(2,1)}, bf16[8,128,128]{2,1,0:T(8,128)(2,1)S(1)}, u32[]{:S(2)}, u32[]{:S(2)}) collective-permute-start(bf16[8,128,128]{2,1,0:T(8,128)(2,1)} %shard_map.106.refs_0_), channel_id=1, source_target_pairs={{0,128},{64,192},{128,0},{192,64},{1,129},{65,193},{129,1},{193,65... | collective-permute-start | bytes 786440 | tf_op jit(solution)/shard_map/ppermute | solution.py:327
  82.3 0.6 collective-permute-start.4
  82.9 0.1 collective-permute-start.8
  83.0 9.9 %collective-permute-done.6.refs_3_ = bf16[8,128,128]{2,1,0:T(8,128)(2,1)S(1)} collective-permute-done((bf16[8,128,128]{2,1,0:T(8,128)(2,1)}, bf16[8,128,128]{2,1,0:T(8,128)(2,1)S(1)}, u32[]{:S(2)}, u32[]{:S(2)}) %collective-permute-start.6) | collective-permute-done | bytes 262176 | tf_op jit(solution)/shard_map/ppermute | solution.py:327
  92.9 0.0 collective-permute-done.5.refs_2_
  92.9 1.8 collective-permute-done.4.refs_1_
  94.8 0.0 collective-permute-done.1.came_ref
  94.8 0.0 copy-done.17
  94.8 0.7 copy-done.18
  95.5 4.4 %shard_map.107 = (f32[4,4,2,72,128]{4,3,2,1,0:T(8,128)}, bf16[4,4,2,72,128]{4,3,2,1,0:T(8,128)(2,1)}) custom-call(s32[1,4]{1,0:T(1,128)} %add_bitcast_fusion.where_ref, bf16[4,1152,128]{2,1,0:T(8,128)(2,1)} %slice.12.mine_ref, bf16[4,1152,128]{2,1,0:T(8,128)(2,1)} %collective-permute-done.1.came_ref, bf16[8,128,128]{2,1,0:T(8,128)(2,1)} %shard_map.106.refs_0_, ...), custom_call_target="tpu_custom_call" | custom-call | flops 2000000000 | bytes 1000000 | tf_op jit(solution)/shard_map/pallas_call | solution.py:339
  99.8 0.0 copy-done.4
  99.9 0.1 collective-permute-start.7
  99.9 0.0 collective-permute-done.8.voth_ref
  100.0 0.7 copy-done.15
  100.7 15.1 %shard_map.108 = (bf16[8,128,128]{2,1,0:T(8,128)(2,1)}, f32[8,128,128]{2,1,0:T(8,128)}, bf16[2,8,128,128]{3,2,1,0:T(8,128)(2,1)}) custom-call(s32[1,4]{1,0:T(1,128)} %add_bitcast_fusion.where_ref, bf16[16,328,128]{2,1,0:T(8,128)(2,1)} %copy-done.1, bf16[16,64,128]{2,1,0:T(8,128)(2,1)} %copy-done.14, bf16[4,256,128]{2,1,0:T(8,128)(2,1)} %copy-done.4, ...), custom_call_target="tpu_custom_call" | custom-call | flops 5000000000 | bytes 1000000 | tf_op jit(solution)/shard_map/pallas_call | solution.py:330
  115.8 0.5 collective-permute-start.9
  116.3 0.0 collective-permute-done.7
  116.3 0.0 copy-done.2
  116.3 0.1 add_convert_fusion
  116.4 1.6 collective-permute-done.9.came_ref
  118.0 28.1 %all_to_all.21 = bf16[16,144,128]{2,1,0:T(8,128)(2,1)S(1)} all-to-all(bf16[16,144,128]{2,1,0:T(8,128)(2,1)S(1)} %bitcast.18), channel_id=1, replica_groups=mesh['x'=4,'yh'=2,'core'=2,'batch'=16] {'batch'}, dimensions={0} | all-to-all | bytes 1179648 | tf_op jit(solution)/shard_map/all_to_all | solution.py:347
  146.1 0.1 reduce_sum.12
  146.2 0.9 broadcast_in_dim.16
  147.1 6.3 %all-to-all-start.3 = ((bf16[32,72,128]{2,1,0:T(8,128)(2,1)}), bf16[32,72,128]{2,1,0:T(8,128)(2,1)S(1)}, u32[]{:S(2)}, u32[]{:S(2)}) async-start(bf16[32,72,128]{2,1,0:T(8,128)(2,1)} %bitcast.16), calls=%async_computation.3 | async-start | bytes 1179648 | tf_op jit(solution)/shard_map/all_to_all | solution.py:355
  153.3 2.2 %shard_map.109 = (bf16[3,128,128]{2,1,0:T(8,128)(2,1)}, bf16[3,128,128]{2,1,0:T(8,128)(2,1)}, bf16[3,128,128]{2,1,0:T(8,128)(2,1)}, bf16[3,128,128]{2,1,0:T(8,12...) custom-call(bf16[8,128,128]{2,1,0:T(8,128)(2,1)} %get-tuple-element., ...), custom_call_target="tpu_custom_call" | custom-call | flops 1000000 | bytes 1000000 | tf_op jit(solution)/shard_map/pallas_call | solution.py:348
  155.5 3.1 %collective-permute-start.10 = (bf16[3,128,128]{2,1,0:T(8,128)(2,1)}, bf16[3,128,128]{2,1,0:T(8,128)(2,1)S(1)}, u32[]{:S(2)}, u32[]{:S(2)}) collective-permute-start(bf16[3,128,128]{2,1,0:T(8,128)(2,1)} %get-tuple-element.43), channel_id=1, source_target_pairs={{0,32},{16,48},{32,0},{48,16},{64,96},{80,112},{96,64},{112,80},{1... | collective-permute-start | bytes 294920 | tf_op jit(solution)/shard_map/ppermute | solution.py:353
  158.6 1.5 collective-permute-start.11
  160.1 0.4 collective-permute-start.12
  160.5 1.5 collective-permute-start.13
  162.0 4.6 %collective-permute-start.14 = (bf16[3,128,128]{2,1,0:T(8,128)(2,1)}, bf16[3,128,128]{2,1,0:T(8,128)(2,1)S(1)}, u32[]{:S(2)}, u32[]{:S(2)}) collective-permute-start(bf16[3,128,128]{2,1,0:T(8,128)(2,1)} %get-tuple-element.47), channel_id=1, source_target_pairs={{0,160},{16,176},{32,128},{48,144},{64,224},{80,240},{96,192},{112... | collective-permute-start | bytes 294920 | tf_op jit(solution)/shard_map/ppermute | solution.py:353
  166.6 1.3 collective-permute-done.10.refs_1_
  167.8 0.0 collective-permute-start.15
  167.8 0.0 collective-permute-done.11.refs_2_
  167.9 5.5 %collective-permute-start.16 = (bf16[3,128,128]{2,1,0:T(8,128)(2,1)}, bf16[3,128,128]{2,1,0:T(8,128)(2,1)S(1)}, u32[]{:S(2)}, u32[]{:S(2)}) collective-permute-start(bf16[3,128,128]{2,1,0:T(8,128)(2,1)} %get-tuple-element.49), channel_id=1, source_target_pairs={{0,224},{16,240},{32,192},{48,208},{64,160},{80,176},{96,128},{112... | collective-permute-start | bytes 294920 | tf_op jit(solution)/shard_map/ppermute | solution.py:353
  173.3 0.0 collective-permute-done.12.refs_3_
  173.3 0.0 collective-permute-done.13.refs_4_
  173.3 0.0 collective-permute-done.14.refs_5_
  173.4 0.0 collective-permute-done.15.refs_6_
  173.4 3.8 %collective-permute-done.16.refs_7_ = bf16[3,128,128]{2,1,0:T(8,128)(2,1)S(1)} collective-permute-done((bf16[3,128,128]{2,1,0:T(8,128)(2,1)}, bf16[3,128,128]{2,1,0:T(8,128)(2,1)S(1)}, u32[]{:S(2)}, u32[]{:S(2)}) %collective-permute-start.16) | collective-permute-done | bytes 98336 | tf_op jit(solution)/shard_map/ppermute | solution.py:353
  177.2 0.6 copy-done.13
  177.8 2.3 %shard_map.110 = (bf16[128,2048]{1,0:T(8,128)(2,1)}, bf16[128,1024]{1,0:T(8,128)(2,1)}) custom-call(s32[1,4]{1,0:T(1,128)} %add_bitcast_fusion.where_ref, bf16[3,128,128]{2,1,0:T(8,128)(2,1)} %get-tuple-element.42.refs_0_, bf16[3,128,128]{2,1,0:T(8,128)(2,1)} %copy-done.7, bf16[3,128,128]{2,1,0:T(8,128)(2,1)} %copy-done.8, bf16[3,128,128]{2,1,0:T(8,128)(2,1)} %copy-done.9, ...), custom_call_target="tpu_custom_call" | custom-call | flops 1000000 | bytes 1000000 | tf_op jit(solution)/shard_map/pallas_call | solution.py:359
  180.1 0.0 all-to-all-done.3.in_ref
  180.1 0.8 copy-done
  181.0 2.2 %shard_map.111 = f32[288,1024]{1,0:T(8,128)} custom-call(bf16[32,72,128]{2,1,0:T(8,128)(2,1)} %copy-done), custom_call_target="tpu_custom_call" | custom-call | flops 1000000 | bytes 1000000 | tf_op jit(solution)/shard_map/pallas_call | solution.py:363
  (32 shorter events, 0.1 us)
Async XLA Ops:
  5.0 7.6 %copy-start.19 = (bf16[4,128,128]{2,1,0:T(8,128)(2,1)S(1)}, bf16[4,128,128]{2,1,0:T(8,128)(2,1)}, u32[]{:S(2)}) copy-start(bf16[4,128,128]{2,1,0:T(8,128)(2,1)} %get-tuple-element.29) | copy-start | bytes 393220
  5.0 32.5 %all-to-all-start = ((bf16[16,328,128]{2,1,0:T(8,128)(2,1)}), bf16[16,328,128]{2,1,0:T(8,128)(2,1)S(1)}, u32[]{:S(2)}, u32[]{:S(2)}) async-start(bf16[16,328,128]{2,1,0:T(8,128)(2,1)} %get-tuple-element.28), calls=%async_computation | async-start | bytes 2686976 | tf_op jit(solution)/shard_map/all_to_all | solution.py:309
  12.6 21.3 %collective-permute-start = (bf16[4,128,128]{2,1,0:T(8,128)(2,1)S(1)}, bf16[4,128,128]{2,1,0:T(8,128)(2,1)S(1)}, u32[]{:S(2)}, u32[]{:S(2)}) collective-permute-start(bf16[4,128,128]{2,1,0:T(8,128)(2,1)S(1)} %copy-done.19), channel_id=1, source_target_pairs={{0,32},{32,0},{1,33},{33,1},{2,34},{34,2},{3,35},{35,3},{4,36},{36... | collective-permute-start | bytes 393224 | tf_op jit(solution)/shard_map/ppermute | solution.py:297
  33.9 0.7 copy-start.6
  37.5 24.0 %copy-start.1 = (bf16[16,328,128]{2,1,0:T(8,128)(2,1)}, bf16[16,328,128]{2,1,0:T(8,128)(2,1)S(1)}, u32[]{:S(2)}) copy-start(bf16[16,328,128]{2,1,0:T(8,128)(2,1)S(1)} %all-to-all-done.in_ref) | copy-start | bytes 4030468
  61.1 33.6 %collective-permute-start.1 = (bf16[4,1152,128]{2,1,0:T(8,128)(2,1)}, bf16[4,1152,128]{2,1,0:T(8,128)(2,1)}, u32[]{:S(2)}, u32[]{:S(2)}) collective-permute-start(bf16[4,1152,128]{2,1,0:T(8,128)(2,1)} %slice.12.mine_ref), channel_id=1, source_target_pairs={{0,32},{32,0},{1,33},{33,1},{2,34},{34,2},{3,35},{35,3},{4,36},{36... | collective-permute-start | bytes 3538952 | tf_op jit(solution)/shard_map/ppermute | solution.py:297
  61.5 1.6 collective-permute-start.2
  63.1 0.7 copy-start.14
  74.4 1.7 collective-permute-start.3
  76.2 0.7 copy-start.5
  78.8 14.2 %collective-permute-start.6 = (bf16[8,128,128]{2,1,0:T(8,128)(2,1)}, bf16[8,128,128]{2,1,0:T(8,128)(2,1)S(1)}, u32[]{:S(2)}, u32[]{:S(2)}) collective-permute-start(bf16[8,128,128]{2,1,0:T(8,128)(2,1)} %shard_map.106.refs_0_), channel_id=1, source_target_pairs={{0,192},{64,128},{128,64},{192,0},{1,193},{65,129},{129,65},{193,1... | collective-permute-start | bytes 786440 | tf_op jit(solution)/shard_map/ppermute | solution.py:327
  79.0 14.0 %collective-permute-start.5 = (bf16[8,128,128]{2,1,0:T(8,128)(2,1)}, bf16[8,128,128]{2,1,0:T(8,128)(2,1)S(1)}, u32[]{:S(2)}, u32[]{:S(2)}) collective-permute-start(bf16[8,128,128]{2,1,0:T(8,128)(2,1)} %shard_map.106.refs_0_), channel_id=1, source_target_pairs={{0,128},{64,192},{128,0},{192,64},{1,129},{65,193},{129,1},{193,65... | collective-permute-start | bytes 786440 | tf_op jit(solution)/shard_map/ppermute | solution.py:327
  82.3 12.5 %collective-permute-start.4 = (bf16[8,128,128]{2,1,0:T(8,128)(2,1)}, bf16[8,128,128]{2,1,0:T(8,128)(2,1)S(1)}, u32[]{:S(2)}, u32[]{:S(2)}) collective-permute-start(bf16[8,128,128]{2,1,0:T(8,128)(2,1)} %shard_map.106.refs_0_), channel_id=1, source_target_pairs={{0,64},{64,0},{128,192},{192,128},{1,65},{65,1},{129,193},{193,129... | collective-permute-start | bytes 786440 | tf_op jit(solution)/shard_map/ppermute | solution.py:327
  82.9 17.0 %copy-start.4 = (bf16[4,256,128]{2,1,0:T(8,128)(2,1)}, bf16[4,256,128]{2,1,0:T(8,128)(2,1)S(1)}, u32[]{:S(2)}) copy-start(bf16[4,256,128]{2,1,0:T(8,128)(2,1)S(1)} %slice.13.v_ref) | copy-start | bytes 786436
  82.9 17.1 %collective-permute-start.8 = (bf16[4,256,128]{2,1,0:T(8,128)(2,1)S(1)}, bf16[4,256,128]{2,1,0:T(8,128)(2,1)S(1)}, u32[]{:S(2)}, u32[]{:S(2)}) collective-permute-start(bf16[4,256,128]{2,1,0:T(8,128)(2,1)S(1)} %slice.13.v_ref), channel_id=1, source_target_pairs={{0,16},{16,0},{1,17},{17,1},{2,18},{18,2},{3,19},{19,3},{4,20},{20... | collective-permute-start | bytes 786440 | tf_op jit(solution)/shard_map/ppermute | solution.py:297
  92.9 1.8 %copy-start.16 = (bf16[8,128,128]{2,1,0:T(8,128)(2,1)}, bf16[8,128,128]{2,1,0:T(8,128)(2,1)S(1)}, u32[]{:S(2)}) copy-start(bf16[8,128,128]{2,1,0:T(8,128)(2,1)S(1)} %collective-permute-done.6.refs_3_) | copy-start | bytes 786436
  92.9 1.8 %copy-start.17 = (bf16[8,128,128]{2,1,0:T(8,128)(2,1)}, bf16[8,128,128]{2,1,0:T(8,128)(2,1)S(1)}, u32[]{:S(2)}) copy-start(bf16[8,128,128]{2,1,0:T(8,128)(2,1)S(1)} %collective-permute-done.5.refs_2_) | copy-start | bytes 786436
  94.8 0.7 copy-start.18
  99.9 16.4 %copy-start.2 = (f32[4,4,2,72,128]{4,3,2,1,0:T(8,128)S(1)}, f32[4,4,2,72,128]{4,3,2,1,0:T(8,128)}, u32[]{:S(2)}) copy-start(f32[4,4,2,72,128]{4,3,2,1,0:T(8,128)} %get-tuple-element.34) | copy-start | bytes 3538948
  99.9 16.4 %collective-permute-start.7 = (bf16[4,4,2,72,128]{4,3,2,1,0:T(8,128)(2,1)}, bf16[4,4,2,72,128]{4,3,2,1,0:T(8,128)(2,1)S(1)}, u32[]{:S(2)}, u32[]{:S(2)}) collective-permute-start(bf16[4,4,2,72,128]{4,3,2,1,0:T(8,128)(2,1)} %get-tuple-element.35), channel_id=1, source_target_pairs={{0,16},{16,0},{1,17},{17,1},{2,18},{18,2},{3,19},{19,3},{4,20},{20... | collective-permute-start | bytes 1769480 | tf_op jit(solution)/shard_map/ppermute | solution.py:297
  100.0 0.7 copy-start.15
  115.8 2.2 %collective-permute-start.9 = (bf16[2,8,128,128]{3,2,1,0:T(8,128)(2,1)}, bf16[2,8,128,128]{3,2,1,0:T(8,128)(2,1)S(1)}, u32[]{:S(2)}, u32[]{:S(2)}) collective-permute-start(bf16[2,8,128,128]{3,2,1,0:T(8,128)(2,1)} %get-tuple-element.38), channel_id=1, source_target_pairs={{0,16},{16,0},{1,17},{17,1},{2,18},{18,2},{3,19},{19,3},{4,20},{20... | collective-permute-start | bytes 1572872 | tf_op jit(solution)/shard_map/ppermute | solution.py:297
  118.0 29.0 %copy-start.3 = (bf16[2,8,128,128]{3,2,1,0:T(8,128)(2,1)}, bf16[2,8,128,128]{3,2,1,0:T(8,128)(2,1)S(1)}, u32[]{:S(2)}) copy-start(bf16[2,8,128,128]{3,2,1,0:T(8,128)(2,1)S(1)} %collective-permute-done.9.came_ref) | copy-start | bytes 1572868
  147.1 33.1 %all-to-all-start.3 = ((bf16[32,72,128]{2,1,0:T(8,128)(2,1)}), bf16[32,72,128]{2,1,0:T(8,128)(2,1)S(1)}, u32[]{:S(2)}, u32[]{:S(2)}) async-start(bf16[32,72,128]{2,1,0:T(8,128)(2,1)} %bitcast.16), calls=%async_computation.3 | async-start | bytes 1179648 | tf_op jit(solution)/shard_map/all_to_all | solution.py:355
  155.5 12.3 %collective-permute-start.10 = (bf16[3,128,128]{2,1,0:T(8,128)(2,1)}, bf16[3,128,128]{2,1,0:T(8,128)(2,1)S(1)}, u32[]{:S(2)}, u32[]{:S(2)}) collective-permute-start(bf16[3,128,128]{2,1,0:T(8,128)(2,1)} %get-tuple-element.43), channel_id=1, source_target_pairs={{0,32},{16,48},{32,0},{48,16},{64,96},{80,112},{96,64},{112,80},{1... | collective-permute-start | bytes 294920 | tf_op jit(solution)/shard_map/ppermute | solution.py:353
  158.6 9.2 %collective-permute-start.11 = (bf16[3,128,128]{2,1,0:T(8,128)(2,1)}, bf16[3,128,128]{2,1,0:T(8,128)(2,1)S(1)}, u32[]{:S(2)}, u32[]{:S(2)}) collective-permute-start(bf16[3,128,128]{2,1,0:T(8,128)(2,1)} %get-tuple-element.44), channel_id=1, source_target_pairs={{0,64},{16,80},{32,96},{48,112},{64,0},{80,16},{96,32},{112,48},{1... | collective-permute-start | bytes 294920 | tf_op jit(solution)/shard_map/ppermute | solution.py:353
  160.1 13.2 %collective-permute-start.12 = (bf16[3,128,128]{2,1,0:T(8,128)(2,1)}, bf16[3,128,128]{2,1,0:T(8,128)(2,1)S(1)}, u32[]{:S(2)}, u32[]{:S(2)}) collective-permute-start(bf16[3,128,128]{2,1,0:T(8,128)(2,1)} %get-tuple-element.45), channel_id=1, source_target_pairs={{0,96},{16,112},{32,64},{48,80},{64,32},{80,48},{96,0},{112,16},{1... | collective-permute-start | bytes 294920 | tf_op jit(solution)/shard_map/ppermute | solution.py:353
  160.5 12.8 %collective-permute-start.13 = (bf16[3,128,128]{2,1,0:T(8,128)(2,1)}, bf16[3,128,128]{2,1,0:T(8,128)(2,1)S(1)}, u32[]{:S(2)}, u32[]{:S(2)}) collective-permute-start(bf16[3,128,128]{2,1,0:T(8,128)(2,1)} %get-tuple-element.46), channel_id=1, source_target_pairs={{0,128},{16,144},{32,160},{48,176},{64,192},{80,208},{96,224},{112... | collective-permute-start | bytes 294920 | tf_op jit(solution)/shard_map/ppermute | solution.py:353
  162.0 11.4 %collective-permute-start.14 = (bf16[3,128,128]{2,1,0:T(8,128)(2,1)}, bf16[3,128,128]{2,1,0:T(8,128)(2,1)S(1)}, u32[]{:S(2)}, u32[]{:S(2)}) collective-permute-start(bf16[3,128,128]{2,1,0:T(8,128)(2,1)} %get-tuple-element.47), channel_id=1, source_target_pairs={{0,160},{16,176},{32,128},{48,144},{64,224},{80,240},{96,192},{112... | collective-permute-start | bytes 294920 | tf_op jit(solution)/shard_map/ppermute | solution.py:353
  167.8 9.3 %copy-start.7 = (bf16[3,128,128]{2,1,0:T(8,128)(2,1)}, bf16[3,128,128]{2,1,0:T(8,128)(2,1)S(1)}, u32[]{:S(2)}) copy-start(bf16[3,128,128]{2,1,0:T(8,128)(2,1)S(1)} %collective-permute-done.10.refs_1_) | copy-start | bytes 294916
  167.8 5.5 %collective-permute-start.15 = (bf16[3,128,128]{2,1,0:T(8,128)(2,1)}, bf16[3,128,128]{2,1,0:T(8,128)(2,1)S(1)}, u32[]{:S(2)}, u32[]{:S(2)}) collective-permute-start(bf16[3,128,128]{2,1,0:T(8,128)(2,1)} %get-tuple-element.48), channel_id=1, source_target_pairs={{0,192},{16,208},{32,224},{48,240},{64,128},{80,144},{96,160},{112... | collective-permute-start | bytes 294920 | tf_op jit(solution)/shard_map/ppermute | solution.py:353
  167.8 9.3 %copy-start.8 = (bf16[3,128,128]{2,1,0:T(8,128)(2,1)}, bf16[3,128,128]{2,1,0:T(8,128)(2,1)S(1)}, u32[]{:S(2)}) copy-start(bf16[3,128,128]{2,1,0:T(8,128)(2,1)S(1)} %collective-permute-done.11.refs_2_) | copy-start | bytes 294916
  167.9 9.3 %collective-permute-start.16 = (bf16[3,128,128]{2,1,0:T(8,128)(2,1)}, bf16[3,128,128]{2,1,0:T(8,128)(2,1)S(1)}, u32[]{:S(2)}, u32[]{:S(2)}) collective-permute-start(bf16[3,128,128]{2,1,0:T(8,128)(2,1)} %get-tuple-element.49), channel_id=1, source_target_pairs={{0,224},{16,240},{32,192},{48,208},{64,160},{80,176},{96,128},{112... | collective-permute-start | bytes 294920 | tf_op jit(solution)/shard_map/ppermute | solution.py:353
  173.3 3.9 %copy-start.9 = (bf16[3,128,128]{2,1,0:T(8,128)(2,1)}, bf16[3,128,128]{2,1,0:T(8,128)(2,1)S(1)}, u32[]{:S(2)}) copy-start(bf16[3,128,128]{2,1,0:T(8,128)(2,1)S(1)} %collective-permute-done.12.refs_3_) | copy-start | bytes 294916
  173.3 3.9 %copy-start.10 = (bf16[3,128,128]{2,1,0:T(8,128)(2,1)}, bf16[3,128,128]{2,1,0:T(8,128)(2,1)S(1)}, u32[]{:S(2)}) copy-start(bf16[3,128,128]{2,1,0:T(8,128)(2,1)S(1)} %collective-permute-done.13.refs_4_) | copy-start | bytes 294916
  173.4 3.8 %copy-start.11 = (bf16[3,128,128]{2,1,0:T(8,128)(2,1)}, bf16[3,128,128]{2,1,0:T(8,128)(2,1)S(1)}, u32[]{:S(2)}) copy-start(bf16[3,128,128]{2,1,0:T(8,128)(2,1)S(1)} %collective-permute-done.14.refs_5_) | copy-start | bytes 294916
  173.4 3.8 %copy-start.12 = (bf16[3,128,128]{2,1,0:T(8,128)(2,1)}, bf16[3,128,128]{2,1,0:T(8,128)(2,1)S(1)}, u32[]{:S(2)}) copy-start(bf16[3,128,128]{2,1,0:T(8,128)(2,1)S(1)} %collective-permute-done.15.refs_6_) | copy-start | bytes 294916
  177.2 0.6 copy-start.13
  180.1 0.8 copy-start

commit v4 on v3

v4 whole, which is shorter than its diff:
```python
import jax
import jax.numpy as jnp
from jax import lax
from jax.experimental import pallas as pl
from jax.experimental.pallas import tpu as pltpu
from jax.sharding import Mesh, PartitionSpec as P


HEADS = 16
KV_HEADS = 8
HEAD = 128
TOK = 128
SLABS = 16
LENGTH = 2048
CHIPS = 8
D = 4608
ROWS = D // SLABS
QUARTER = ROWS // 4
BK = 256
BQ = 512
HALF = TOK // 2
PACK = 3 * TOK + 8
TILES = 9
XS = 4
EARLY = (0, 1, 3)

SCALE = 144.0 ** (-0.5)
LOG2E = 1.4426950408889634

f32 = jnp.float32
bf16 = jnp.bfloat16


def dot(a, b, dims):
    return lax.dot_general(a, b, (dims, ((), ())), preferred_element_type=f32)


def three_parts(x):
    hi = x.astype(bf16).astype(f32)
    rest = x - hi
    mid = rest.astype(bf16).astype(f32)
    low = (rest - mid).astype(bf16).astype(f32)
    return hi, mid, low


def pack_kernel(place_ref, q_ref, g_ref, o_ref, k_ref, v_ref, n_ref, out_ref):
    place = jnp.full((1, TOK), place_ref[0, 0], jnp.int32).astype(f32)
    for s in range(SLABS):
        cols = slice(s * HEAD, (s + 1) * HEAD)
        kv_cols = slice((s // 2) * HEAD, (s // 2 + 1) * HEAD)
        half = slice((s % 2) * HALF, (s % 2 + 1) * HALF)
        grads = g_ref[:, cols]
        out_ref[s, 0:TOK, :] = q_ref[:, cols]
        out_ref[s, TOK : 2 * TOK, :] = grads
        out_ref[s, 2 * TOK : 2 * TOK + HALF, :] = k_ref[half, kv_cols]
        out_ref[s, 2 * TOK + HALF : 3 * TOK, :] = v_ref[half, kv_cols]
        prod = grads.astype(f32) * o_ref[:, cols].astype(f32)
        delta = jnp.sum(prod.T, axis=0, keepdims=True)
        rows = (*three_parts(n_ref[s : s + 1, :]), *three_parts(delta), place, jnp.zeros_like(place))
        out_ref[s, 3 * TOK :, :] = jnp.concatenate(rows, axis=0).astype(bf16)


def pack_late_kernel(where_ref, x_ref, out_ref, early_ref):
    for x in range(XS):
        for t in range(TILES):
            tile = TILES * x + t
            out_ref[x, t * TOK : (t + 1) * TOK, :] = x_ref[:, tile * 128 : (tile + 1) * 128].T
    for j, k in enumerate(EARLY):
        early_ref[j] = out_ref[where_ref[0, 3] ^ k]


def sort_slabs(core, in_ref, oth_ref, q_s, g_s, k_s, v_s, nd_s, inv_s):
    for s in range(SLABS):
        extra = in_ref[s, 3 * TOK :, :].astype(f32)
        p = jnp.max(extra[6:7, :]).astype(jnp.int32)
        inv_s[p] = s
        at = pl.ds(pl.multiple_of(p * TOK, TOK), TOK)
        q_s[at, :] = in_ref[s, 0:TOK, :]
        g_s[at, :] = in_ref[s, TOK : 2 * TOK, :]
        low = pl.ds(pl.multiple_of(p * TOK, TOK), HALF)
        high = pl.ds(pl.multiple_of(p * TOK + HALF, HALF), HALF)
        for part, out in enumerate((k_s, v_s)):
            own = in_ref[s, 2 * TOK + part * HALF : 2 * TOK + (part + 1) * HALF, :]
            oth = oth_ref[s, part * HALF : (part + 1) * HALF, :]
            out[low, :] = jnp.where(core == 0, own, oth)
            out[high, :] = jnp.where(core == 0, oth, own)
        nd_s[p, 0:1, :] = (extra[0:1] + extra[1:2] + extra[2:3]) * LOG2E
        nd_s[p, 1:2, :] = extra[3:4] + extra[4:5] + extra[5:6]


def row_of(nd_s, i, row):
    return jnp.concatenate([nd_s[i * (BQ // TOK) + t, row : row + 1, :] for t in range(BQ // TOK)], axis=1)


def block_at(i, size):
    return pl.ds(pl.multiple_of(i * size, size), size)


def attn_kernel(
    where_ref, in_ref, oth_ref, vkeep_ref, vsend_ref, qkeep_ref, kkeep_ref, send_ref,
    q_s, g_s, k_s, v_s, nd_s, dq_s, dk_s, dv_s, inv_s,
):
    core = where_ref[0, 0]
    chip = where_ref[0, 1]
    sort_slabs(core, in_ref, oth_ref, q_s, g_s, k_s, v_s, nd_s, inv_s)
    dq_s[...] = jnp.zeros_like(dq_s)

    def per_key_block(j, _):
        kb = k_s[block_at(j, BK), :]
        vb = v_s[block_at(j, BK), :]
        kt = kb.T
        first = j // (BQ // BK)

        def one(i, masked):
            qb = q_s[block_at(i, BQ), :]
            gb = g_s[block_at(i, BQ), :]
            st = dot(kb, qb, ((1,), (1,)))
            probs = jnp.exp2(st * (SCALE * LOG2E) - row_of(nd_s, i, 0))
            if masked:
                key_at = lax.broadcasted_iota(jnp.int32, (BK, BQ), 0) + j * BK
                query_at = lax.broadcasted_iota(jnp.int32, (BK, BQ), 1) + i * BQ
                probs = jnp.where(key_at <= query_at, probs, 0.0)
            dprob = dot(vb, gb, ((1,), (1,)))
            ds = (probs * (dprob - row_of(nd_s, i, 1))).astype(bf16)
            dv = dot(probs.astype(bf16), gb, ((1,), (0,)))
            dk = dot(ds, qb, ((1,), (0,)))
            dq_s[i] += dot(kt, ds, ((1,), (0,)))
            return dk, dv

        dk_s[...], dv_s[...] = one(first, True)

        def per_query_block(i, _):
            dk, dv = one(i, False)
            dk_s[...] += dk
            dv_s[...] += dv
            return 0

        lax.fori_loop(first + 1, LENGTH // BQ, per_query_block, 0)
        for t in range(BK // TOK):
            s = inv_s[j * (BK // TOK) + t]
            to = (s // 2) ^ chip
            rows = slice(t * TOK, (t + 1) * TOK)

            @pl.when(s % 2 == core)
            def _():
                vkeep_ref[s // 2] = dv_s[rows, :]
                kkeep_ref[to] = dk_s[rows, :] * SCALE

            @pl.when(s % 2 != core)
            def _():
                vsend_ref[s // 2] = dv_s[rows, :].astype(bf16)
                send_ref[1, to] = (dk_s[rows, :] * SCALE).astype(bf16)

        return 0

    lax.fori_loop(0, LENGTH // BK, per_key_block, 0)
    for i in range(LENGTH // BQ):
        rows = (dq_s[i].T * SCALE).astype(bf16)
        for t in range(BQ // TOK):
            s = inv_s[i * (BQ // TOK) + t]
            to = (s // 2) ^ chip
            part = rows[t * TOK : (t + 1) * TOK, :]

            @pl.when(s % 2 == core)
            def _():
                qkeep_ref[to] = part

            @pl.when(s % 2 != core)
            def _():
                send_ref[0, to] = part


def sum_kernel(keep_ref, came_ref, out_ref):
    out_ref[...] = (keep_ref[...] + came_ref[...].astype(f32)).astype(bf16)


def weight_kernel(where_ref, mine_ref, early_ref, one_ref, two_ref, three_ref, *refs):
    core = where_ref[0, 0]
    high = where_ref[0, 2]
    at_x = where_ref[0, 3]
    dv_refs, (keep_ref, send_ref, grad_s) = refs[:XS], refs[XS:]
    for i in range(CHIPS):
        slab = 2 * i + high if i < XS else 2 * (at_x ^ (i - XS)) + 1 - high
        for k in range(XS):
            grad_s[i * TOK : (i + 1) * TOK, k * HEAD : (k + 1) * HEAD] = dv_refs[k][slab]
    grads = grad_s[...]

    def rows_of(part, c):
        at = pl.ds(pl.multiple_of(part * 2 * ROWS + c * ROWS, 32), ROWS)
        tokens = [mine_ref[i, at, :] for i in range(XS)]
        tokens += [early_ref[0, at, :]] + [ref[at, :] for ref in (one_ref, two_ref, three_ref)]
        return dot(jnp.concatenate(tokens, axis=1), grads, ((1,), (0,)))

    for part in range(2):
        mine = rows_of(part, core)
        for k in range(XS):
            for r in range(4):
                keep_ref[r, at_x ^ k, part] = mine[r * QUARTER : (r + 1) * QUARTER, k * HEAD : (k + 1) * HEAD]
        sent = rows_of(part, 1 - core).astype(bf16)
        for k in range(XS):
            for r in range(4):
                send_ref[r, at_x ^ k, part] = sent[r * QUARTER : (r + 1) * QUARTER, k * HEAD : (k + 1) * HEAD]


def finish_kernel(in_ref, out_ref):
    for high in range(2):
        for b in range(SLABS):
            head = 2 * (b % XS) + high
            rows = slice((b // XS) * QUARTER, (b // XS + 1) * QUARTER)
            out_ref[rows, head * HEAD : (head + 1) * HEAD] = in_ref[high * SLABS + b].astype(f32)


def join_kernel(q_ref, k_ref, came_ref, *out_refs):
    for k in range(CHIPS):
        out_refs[k][0] = q_ref[k]
        out_refs[k][1] = came_ref[0, k]
        out_refs[k][2] = (k_ref[k] + came_ref[1, k].astype(f32)).astype(bf16)


def place_query_kernel(where_ref, *refs):
    core = where_ref[0, 0]
    chip = where_ref[0, 1]
    for k in range(CHIPS):
        head = chip ^ k
        refs[CHIPS][:, block_at(2 * head + core, HEAD)] = refs[k][0]
        refs[CHIPS][:, block_at(2 * head + 1 - core, HEAD)] = refs[k][1]


def place_key_kernel(where_ref, *refs):
    for k in range(CHIPS):
        refs[CHIPS][:, block_at(where_ref[0, 1] ^ k, HEAD)] = refs[k][2]


VMEM = pl.BlockSpec(memory_space=pltpu.VMEM)
SMEM = pl.BlockSpec(memory_space=pltpu.SMEM)
TOKENS = (CHIPS, TOK, HEAD)


def shaped(shape, dtype):
    return jax.ShapeDtypeStruct(shape, dtype)


def call(kernel, specs, outs, scratch=(), flops=10**6, moved=10**6, **more):
    return pl.pallas_call(
        kernel,
        in_specs=specs,
        out_shape=outs,
        scratch_shapes=list(scratch),
        cost_estimate=pl.CostEstimate(flops=flops, bytes_accessed=moved, transcendentals=0),
        **({"out_specs": [VMEM] * len(outs)} | more),
    )


SORTED = [pltpu.VMEM((LENGTH, HEAD), bf16)] * 4
ROWED = [pltpu.VMEM((SLABS, 8, TOK), f32)]
PLACES = [pltpu.SMEM((SLABS,), jnp.int32)]
BLOCK = [pltpu.VMEM((BK, HEAD), f32)]
SEQ = ("x", "yh", "core")
SWAP = [(0, 1), (1, 0)]


def swapped(array, axis="core"):
    return lax.ppermute(array, axis, SWAP)


def along_x(array, k):
    return lax.ppermute(array, "x", [(i, i ^ k) for i in range(XS)])


def inner(
    query_rows, key_rows, value_rows, attn_output, output_grad, log_norm, slab_order, normed_input
):
    core, high, at_x = (lax.axis_index(a).astype(jnp.int32) for a in ("core", "yh", "x"))
    where = jnp.stack([core, at_x * 2 + high, high, at_x]).reshape(1, 4)
    (packed,) = call(pack_kernel, [SMEM] + [VMEM] * 6, [shaped((SLABS, PACK, HEAD), bf16)])(
        slab_order, query_rows[0], output_grad[0], attn_output[0], key_rows[0], value_rows[0], log_norm[0]
    )
    got = lax.all_to_all(packed, SEQ, 0, 0, tiled=True)
    late, early = call(
        pack_late_kernel, [SMEM, VMEM],
        [shaped((XS, TILES * TOK, 128), bf16), shaped((len(EARLY), TILES * TOK, 128), bf16)],
    )(where, normed_input[0])
    early = swapped(early, "yh")
    got, late = lax.optimization_barrier((got, late))
    other = swapped(got[:, 2 * TOK : 3 * TOK, :])
    late = lax.all_to_all(late, "x", 0, 0, tiled=True)
    v_keep, v_send, q_keep, k_keep, qk_send = call(
        attn_kernel, [SMEM, VMEM, VMEM],
        [shaped(TOKENS, f32), shaped(TOKENS, bf16), shaped(TOKENS, bf16), shaped(TOKENS, f32), shaped((2, *TOKENS), bf16)],
        SORTED + ROWED + [pltpu.VMEM((LENGTH // BQ, HEAD, BQ), f32)] + BLOCK * 2 + PLACES,
        flops=6 * 10**9,
    )(where, got, other)
    v_came = swapped(v_send)
    (dv,) = call(sum_kernel, [VMEM] * 2, [shaped(TOKENS, bf16)])(v_keep, v_came)
    dvs = [dv]
    for k in range(1, XS):
        dvs.append(along_x(dv, k))
    two = swapped(lax.dynamic_index_in_dim(late, at_x ^ 2, 0, False), "yh")
    one, three = along_x(early[1], 1), along_x(early[2], 3)
    qk_came = swapped(qk_send)
    w_shape = (4, XS, 2, QUARTER, HEAD)
    w_keep, w_send = call(
        weight_kernel, [SMEM] + [VMEM] * (5 + XS),
        [shaped(w_shape, f32), shaped(w_shape, bf16)],
        [pltpu.VMEM((LENGTH // 2, XS * HEAD), bf16)], flops=2 * 10**9,
    )(where, late, early, one, two, three, *dvs)
    w_came = swapped(w_send)
    w = (w_keep + w_came.astype(f32)).astype(bf16)
    parts = lax.all_to_all(w.reshape(SLABS, 2 * QUARTER, HEAD), "batch", 0, 0, tiled=True)
    back = call(join_kernel, [VMEM] * 3, [shaped((3, TOK, HEAD), bf16)] * CHIPS)(
        q_keep, k_keep, qk_came
    )
    pieces = [back[0]]
    for k in range(1, CHIPS):
        pieces.append(lax.ppermute(back[k], SEQ, [(i, i ^ (2 * k)) for i in range(SLABS)]))
    piece = jnp.sum(parts.astype(f32), axis=0).astype(bf16).reshape(2, 1, QUARTER, HEAD)
    blocks = lax.all_to_all(
        jnp.broadcast_to(piece, (2, SLABS, QUARTER, HEAD)).reshape(2 * SLABS, QUARTER, HEAD),
        ("yh", "batch"), 0, 0, tiled=True,
    )
    (grad_query,) = call(
        place_query_kernel, [SMEM] + [VMEM] * CHIPS, [shaped((TOK, HEADS * HEAD), bf16)]
    )(where, *pieces)
    (grad_key,) = call(
        place_key_kernel, [SMEM] + [VMEM] * CHIPS, [shaped((TOK, KV_HEADS * HEAD), bf16)]
    )(where, *pieces)
    (weight,) = call(finish_kernel, [VMEM], [shaped((ROWS, KV_HEADS * HEAD), f32)])(blocks)
    return (grad_query[None], grad_key[None], weight)


def solution(mesh):
    fine = Mesh(mesh.devices.reshape(4, 2, 2, 16), (*SEQ, "batch"))
    rows = P("batch", SEQ, None)
    return jax.shard_map(
        inner,
        mesh=fine,
        in_specs=(rows, rows, rows, rows, rows, P("batch", None, SEQ), P("batch", SEQ), rows),
        out_specs=(rows, rows, P(SEQ, None)),
        check_vma=False,
    )
```

time: 185 us -> 173 us (0.935)
  the two profiles are of different devices: /device:TPU:2 before, /device:TPU:8 now
where the time goes in v4:
time: 173 us; the launch traced here: 172 us
  waiting for transfers between devices  55.4 us (32%)
  starting transfers between devices  42.8 us (25%)
  Pallas kernels  35.1 us (20%)
  blocking collectives  28.1 us (16%)
  local copies, waits for them, and re-layouts  7.39 us (4%)
  other arithmetic  2.07 us (1%)
    all_to_all x1, blocking collectives, inner(): lax.all_to_all(w.reshape(SLABS, 2 * QUARTER, HEAD), 'batch', 0, 0, tiled=...  28.1 us
    ppermute x6, waiting for transfers between devices, swapped(): return lax.ppermute(array, axis, SWAP)  17.3 us
    all_to_all x1, waiting for transfers between devices, inner(): got = lax.all_to_all(packed, SEQ, 0, 0, tiled=True)  16.9 us
    ppermute x7, starting transfers between devices, inner(): lax.ppermute(back[k], SEQ, [(i, i ^ 2 * k) for i in range(SLABS)])  14.7 us
    pallas_call x1, Pallas kernels, inner(): call(attn_kernel, [SMEM, VMEM, VMEM], [shaped(TOKENS, f32), shaped(TOKENS...  14.1 us
    ppermute x5, waiting for transfers between devices, along_x(): return lax.ppermute(array, 'x', [(i, i ^ k) for i in range(XS)])  12.8 us
    ppermute x7, waiting for transfers between devices, inner(): lax.ppermute(back[k], SEQ, [(i, i ^ 2 * k) for i in range(SLABS)])  8.42 us
    ppermute x5, starting transfers between devices, along_x(): return lax.ppermute(array, 'x', [(i, i ^ k) for i in range(XS)])  8.32 us
  transfers between devices with their start and end apart: 21, of which 11 were waited for; matrix products, arithmetic and copies ran while one was open for 1% of the time, Pallas kernels for 15%

profile of v4, /device:TPU:8, one launch (start us, length us, event | category | flops | bytes accessed | tf_op | source)
XLA Modules:
  0.0 172.3 jit_solution(7672115805630380618)
XLA Ops:
  1.3 3.1 %shard_map.103 = bf16[16,392,128]{2,1,0:T(8,128)(2,1)} custom-call(s32[1,1]{1,0:T(1,128)S(6)} %copy.11.place_ref, bf16[128,2048]{1,0:T(8,128)(2,1)} %bitcast.27, bf16[128,2048]{1,0:T(8,128)(2,1)} %bitcast.28, bf16[128,2048]{1,0:T(8,128)(2,1)} %bitcast.29, bf16[128,1024]{1,0:T(8,128)(2,1)} %bitcast.30, bf16[128,1024]{1,0:T(8,128)(2,1)} %bitcast.31, ...), custom_call_target="tpu_custom_call" | custom-call | flops 1000000 | bytes 1000000 | tf_op jit(solution)/shard_map/pallas_call | solution.py:275
  4.4 6.1 %all-to-all-start = ((bf16[16,392,128]{2,1,0:T(8,128)(2,1)}), bf16[16,392,128]{2,1,0:T(8,128)(2,1)S(1)}, u32[]{:S(2)}, u32[]{:S(2)}) async-start(bf16[16,392,128]{2,1,0:T(8,128)(2,1)} %shard_map.103), calls=%async_computation | async-start | bytes 3211264 | tf_op jit(solution)/shard_map/all_to_all | solution.py:278
  10.6 0.6 add_bitcast_fusion.where_ref
  11.2 2.9 %shard_map.104 = (bf16[4,1152,128]{2,1,0:T(8,128)(2,1)}, bf16[3,1152,128]{2,1,0:T(8,128)(2,1)}) custom-call(s32[1,4]{1,0:T(1,128)} %add_bitcast_fusion.where_ref, bf16[128,4608]{1,0:T(8,128)(2,1)} %bitcast.25), custom_call_target="tpu_custom_call" | custom-call | flops 1000000 | bytes 1000000 | tf_op jit(solution)/shard_map/pallas_call | solution.py:279
  14.1 3.4 %collective-permute-start.9 = (bf16[3,1152,128]{2,1,0:T(8,128)(2,1)}, bf16[3,1152,128]{2,1,0:T(8,128)(2,1)}, u32[]{:S(2)}, u32[]{:S(2)}) collective-permute-start(bf16[3,1152,128]{2,1,0:T(8,128)(2,1)} %get-tuple-element.36), channel_id=1, source_target_pairs={{0,32},{32,0},{1,33},{33,1},{2,34},{34,2},{3,35},{35,3},{4,36},{36... | collective-permute-start | bytes 2654216 | tf_op jit(solution)/shard_map/ppermute | solution.py:263
  17.5 16.9 %all-to-all-done.in_ref = bf16[16,392,128]{2,1,0:T(8,128)(2,1)S(1)} async-done(((bf16[16,392,128]{2,1,0:T(8,128)(2,1)}), bf16[16,392,128]{2,1,0:T(8,128)(2,1)S(1)}, u32[]{:S(2)}, u32[]{:S(2)}) %all-to-all-start) | async-done | bytes 1605664 | tf_op jit(solution)/shard_map/all_to_all | solution.py:278
  34.5 0.1 collective-permute-start
  34.6 1.0 copy-done
  35.6 3.5 %all-to-all-start.1 = ((bf16[4,1152,128]{2,1,0:T(8,128)(2,1)}), bf16[4,1152,128]{2,1,0:T(8,128)(2,1)S(1)}, u32[]{:S(2)}, u32[]{:S(2)}) async-start(bf16[4,1152,128]{2,1,0:T(8,128)(2,1)} %get-tuple-element.35), calls=%async_computation.1 | async-start | bytes 2359296 | tf_op jit(solution)/shard_map/all_to_all | solution.py:286
  39.2 12.2 %collective-permute-done.9.early_ref = bf16[3,1152,128]{2,1,0:T(8,128)(2,1)} collective-permute-done((bf16[3,1152,128]{2,1,0:T(8,128)(2,1)}, bf16[3,1152,128]{2,1,0:T(8,128)(2,1)}, u32[]{:S(2)}, u32[]{:S(2)}) %collective-permute-start.9) | collective-permute-done | bytes 884768 | tf_op jit(solution)/shard_map/ppermute | solution.py:263
  51.4 1.1 slice_bitcast_fusion
  52.5 1.6 collective-permute-start.10
  54.1 2.1 %collective-permute-start.12 = (bf16[1152,128]{1,0:T(8,128)(2,1)S(1)}, bf16[1152,128]{1,0:T(8,128)(2,1)}, u32[]{:S(2)}, u32[]{:S(2)}) collective-permute-start(bf16[1152,128]{1,0:T(8,128)(2,1)S(1)} %get-tuple-element.41), channel_id=1, source_target_pairs={{0,192},{64,128},{128,64},{192,0},{1,193},{65,129},{129,65},{193,1... | collective-permute-start | bytes 884744 | tf_op jit(solution)/shard_map/ppermute | solution.py:267
  56.1 0.0 collective-permute-done.oth_ref
  56.1 14.1 %shard_map.105 = (f32[8,128,128]{2,1,0:T(8,128)}, bf16[8,128,128]{2,1,0:T(8,128)(2,1)}, bf16[8,128,128]{2,1,0:T(8,128)(2,1)}, f32[8,128,128]{2,1,0:T(8,128)}, bf16[2,8,128,128]{3,2,1,0:T(8,128)(2,1)}) custom-call(s32[1,4]{1,0:T(1,128)} %add_bitcast_fusion.where_ref, bf16[16,392,128]{2,1,0:T(8,128)(2,1)} %copy-done, ...), custom_call_target="tpu_custom_call" | custom-call | flops 6000000000 | bytes 1000000 | tf_op jit(solution)/shard_map/pallas_call | solution.py:287
  70.3 0.0 collective-permute-start.13
  70.3 0.0 all-to-all-done.1.mine_ref
  70.3 0.0 copy-start.2
  70.3 0.8 collective-permute-start.11
  71.1 0.9 collective-permute-done.13.came_ref
  72.0 0.7 copy-done.11
  72.7 1.8 %shard_map.109.refs_0_ = bf16[8,128,128]{2,1,0:T(8,128)(2,1)} custom-call(f32[8,128,128]{2,1,0:T(8,128)} %get-tuple-element.37.keep_ref, bf16[8,128,128]{2,1,0:T(8,128)(2,1)} %copy-done.11), custom_call_target="tpu_custom_call" | custom-call | flops 1000000 | bytes 1000000 | tf_op jit(solution)/shard_map/pallas_call | solution.py:294
  74.6 0.6 collective-permute-start.14
  75.1 2.1 %collective-permute-start.15 = (bf16[8,128,128]{2,1,0:T(8,128)(2,1)}, bf16[8,128,128]{2,1,0:T(8,128)(2,1)S(1)}, u32[]{:S(2)}, u32[]{:S(2)}) collective-permute-start(bf16[8,128,128]{2,1,0:T(8,128)(2,1)} %shard_map.109.refs_0_), channel_id=1, source_target_pairs={{0,128},{64,192},{128,0},{192,64},{1,129},{65,193},{129,1},{193,65... | collective-permute-start | bytes 786440 | tf_op jit(solution)/shard_map/ppermute | solution.py:267
  77.2 0.0 collective-permute-done.10.one_ref
  77.2 2.1 %collective-permute-start.16 = (bf16[8,128,128]{2,1,0:T(8,128)(2,1)}, bf16[8,128,128]{2,1,0:T(8,128)(2,1)S(1)}, u32[]{:S(2)}, u32[]{:S(2)}) collective-permute-start(bf16[8,128,128]{2,1,0:T(8,128)(2,1)} %shard_map.109.refs_0_), channel_id=1, source_target_pairs={{0,192},{64,128},{128,64},{192,0},{1,193},{65,129},{129,65},{193,1... | collective-permute-start | bytes 786440 | tf_op jit(solution)/shard_map/ppermute | solution.py:267
  79.3 0.0 collective-permute-done.12.three_ref
  79.3 4.7 %collective-permute-done.14.refs_1_ = bf16[8,128,128]{2,1,0:T(8,128)(2,1)S(1)} collective-permute-done((bf16[8,128,128]{2,1,0:T(8,128)(2,1)}, bf16[8,128,128]{2,1,0:T(8,128)(2,1)S(1)}, u32[]{:S(2)}, u32[]{:S(2)}) %collective-permute-start.14) | collective-permute-done | bytes 262176 | tf_op jit(solution)/shard_map/ppermute | solution.py:267
  84.0 5.5 %collective-permute-done.15.refs_2_ = bf16[8,128,128]{2,1,0:T(8,128)(2,1)S(1)} collective-permute-done((bf16[8,128,128]{2,1,0:T(8,128)(2,1)}, bf16[8,128,128]{2,1,0:T(8,128)(2,1)S(1)}, u32[]{:S(2)}, u32[]{:S(2)}) %collective-permute-start.15) | collective-permute-done | bytes 262176 | tf_op jit(solution)/shard_map/ppermute | solution.py:267
  89.5 2.6 %collective-permute-done.16.refs_3_ = bf16[8,128,128]{2,1,0:T(8,128)(2,1)S(1)} collective-permute-done((bf16[8,128,128]{2,1,0:T(8,128)(2,1)}, bf16[8,128,128]{2,1,0:T(8,128)(2,1)S(1)}, u32[]{:S(2)}, u32[]{:S(2)}) %collective-permute-start.16) | collective-permute-done | bytes 262176 | tf_op jit(solution)/shard_map/ppermute | solution.py:267
  92.0 0.0 collective-permute-done.11.two_ref
  92.1 0.7 copy-done.17
  92.7 0.7 copy-done.14
  93.5 4.5 %shard_map.110 = (f32[4,4,2,72,128]{4,3,2,1,0:T(8,128)}, bf16[4,4,2,72,128]{4,3,2,1,0:T(8,128)(2,1)}) custom-call(s32[1,4]{1,0:T(1,128)} %add_bitcast_fusion.where_ref, bf16[4,1152,128]{2,1,0:T(8,128)(2,1)} %copy-done.2, bf16[3,1152,128]{2,1,0:T(8,128)(2,1)} %collective-permute-done.9.early_ref, bf16[1152,128]{1,0:T(8,128)(2,1)} %copy-done.13, ...), custom_call_target="tpu_custom_call" | custom-call | flops 2000000000 | bytes 1000000 | tf_op jit(solution)/shard_map/pallas_call | solution.py:302
  98.0 0.0 collective-permute-start.17
  98.0 2.2 %collective-permute-done.17 = bf16[4,4,2,72,128]{4,3,2,1,0:T(8,128)(2,1)S(1)} collective-permute-done((bf16[4,4,2,72,128]{4,3,2,1,0:T(8,128)(2,1)}, bf16[4,4,2,72,128]{4,3,2,1,0:T(8,128)(2,1)S(1)}, u32[]{:S(2)}, u32[]{:S(2)}) %collective-permute-start.17) | collective-permute-done | bytes 589856 | tf_op jit(solution)/shard_map/ppermute | solution.py:263
  100.2 1.4 add_convert_fusion
  101.6 28.1 %all_to_all.20 = bf16[16,144,128]{2,1,0:T(8,128)(2,1)S(1)} all-to-all(bf16[16,144,128]{2,1,0:T(8,128)(2,1)S(1)} %bitcast.24), channel_id=1, replica_groups=mesh['x'=4,'yh'=2,'core'=2,'batch'=16] {'batch'}, dimensions={0} | all-to-all | bytes 1179648 | tf_op jit(solution)/shard_map/all_to_all | solution.py:309
  129.7 0.1 reduce_sum.12
  129.8 0.9 broadcast_in_dim.16
  130.6 5.8 %all-to-all-start.3 = ((bf16[32,72,128]{2,1,0:T(8,128)(2,1)}), bf16[32,72,128]{2,1,0:T(8,128)(2,1)S(1)}, u32[]{:S(2)}, u32[]{:S(2)}) async-start(bf16[32,72,128]{2,1,0:T(8,128)(2,1)} %bitcast.19), calls=%async_computation.3 | async-start | bytes 1179648 | tf_op jit(solution)/shard_map/all_to_all | solution.py:317
  136.4 0.1 collective-permute-start.1
  136.5 1.9 %collective-permute-done.1.came_ref = bf16[2,8,128,128]{3,2,1,0:T(8,128)(2,1)S(1)} collective-permute-done((bf16[2,8,128,128]{3,2,1,0:T(8,128)(2,1)S(1)}, bf16[2,8,128,128]{3,2,1,0:T(8,128)(2,1)S(1)}, u32[]{:S(2)}, u32[]{:S(2)}) %collective-permute-start.1) | collective-permute-done | bytes 524320 | tf_op jit(solution)/shard_map/ppermute | solution.py:263
  138.4 0.8 copy-done.3
  139.2 2.2 %shard_map.106 = (bf16[3,128,128]{2,1,0:T(8,128)(2,1)}, bf16[3,128,128]{2,1,0:T(8,128)(2,1)}, bf16[3,128,128]{2,1,0:T(8,128)(2,1)}, bf16[3,128,128]{2,1,0:T(8,12...) custom-call(bf16[8,128,128]{2,1,0:T(8,128)(2,1)} %get-tuple-element., ...), custom_call_target="tpu_custom_call" | custom-call | flops 1000000 | bytes 1000000 | tf_op jit(solution)/shard_map/pallas_call | solution.py:310
  141.4 2.1 %collective-permute-start.2 = (bf16[3,128,128]{2,1,0:T(8,128)(2,1)}, bf16[3,128,128]{2,1,0:T(8,128)(2,1)S(1)}, u32[]{:S(2)}, u32[]{:S(2)}) collective-permute-start(bf16[3,128,128]{2,1,0:T(8,128)(2,1)} %get-tuple-element.28), channel_id=1, source_target_pairs={{0,32},{16,48},{32,0},{48,16},{64,96},{80,112},{96,64},{112,80},{1... | collective-permute-start | bytes 294920 | tf_op jit(solution)/shard_map/ppermute | solution.py:315
  143.5 0.0 collective-permute-start.3
  143.5 2.9 %collective-permute-start.4 = (bf16[3,128,128]{2,1,0:T(8,128)(2,1)}, bf16[3,128,128]{2,1,0:T(8,128)(2,1)S(1)}, u32[]{:S(2)}, u32[]{:S(2)}) collective-permute-start(bf16[3,128,128]{2,1,0:T(8,128)(2,1)} %get-tuple-element.30), channel_id=1, source_target_pairs={{0,96},{16,112},{32,64},{48,80},{64,32},{80,48},{96,0},{112,16},{1... | collective-permute-start | bytes 294920 | tf_op jit(solution)/shard_map/ppermute | solution.py:315
  146.4 1.5 collective-permute-start.5
  147.9 3.6 %collective-permute-start.6 = (bf16[3,128,128]{2,1,0:T(8,128)(2,1)}, bf16[3,128,128]{2,1,0:T(8,128)(2,1)S(1)}, u32[]{:S(2)}, u32[]{:S(2)}) collective-permute-start(bf16[3,128,128]{2,1,0:T(8,128)(2,1)} %get-tuple-element.32), channel_id=1, source_target_pairs={{0,160},{16,176},{32,128},{48,144},{64,224},{80,240},{96,192},{112... | collective-permute-start | bytes 294920 | tf_op jit(solution)/shard_map/ppermute | solution.py:315
  151.4 1.9 %collective-permute-done.2.refs_1_ = bf16[3,128,128]{2,1,0:T(8,128)(2,1)S(1)} collective-permute-done((bf16[3,128,128]{2,1,0:T(8,128)(2,1)}, bf16[3,128,128]{2,1,0:T(8,128)(2,1)S(1)}, u32[]{:S(2)}, u32[]{:S(2)}) %collective-permute-start.2) | collective-permute-done | bytes 98336 | tf_op jit(solution)/shard_map/ppermute | solution.py:315
  153.4 2.7 %collective-permute-start.7 = (bf16[3,128,128]{2,1,0:T(8,128)(2,1)}, bf16[3,128,128]{2,1,0:T(8,128)(2,1)S(1)}, u32[]{:S(2)}, u32[]{:S(2)}) collective-permute-start(bf16[3,128,128]{2,1,0:T(8,128)(2,1)} %get-tuple-element.33), channel_id=1, source_target_pairs={{0,192},{16,208},{32,224},{48,240},{64,128},{80,144},{96,160},{112... | collective-permute-start | bytes 294920 | tf_op jit(solution)/shard_map/ppermute | solution.py:315
  156.1 0.0 collective-permute-done.3.refs_2_
  156.1 1.9 %collective-permute-start.8 = (bf16[3,128,128]{2,1,0:T(8,128)(2,1)}, bf16[3,128,128]{2,1,0:T(8,128)(2,1)S(1)}, u32[]{:S(2)}, u32[]{:S(2)}) collective-permute-start(bf16[3,128,128]{2,1,0:T(8,128)(2,1)} %get-tuple-element.34), channel_id=1, source_target_pairs={{0,224},{16,240},{32,192},{48,208},{64,160},{80,176},{96,128},{112... | collective-permute-start | bytes 294920 | tf_op jit(solution)/shard_map/ppermute | solution.py:315
  158.0 0.0 collective-permute-done.4.refs_3_
  158.0 0.0 collective-permute-done.5.refs_4_
  158.0 0.0 collective-permute-done.6.refs_5_
  158.0 1.4 collective-permute-done.7.refs_6_
  159.4 5.1 %collective-permute-done.8.refs_7_ = bf16[3,128,128]{2,1,0:T(8,128)(2,1)S(1)} collective-permute-done((bf16[3,128,128]{2,1,0:T(8,128)(2,1)}, bf16[3,128,128]{2,1,0:T(8,128)(2,1)S(1)}, u32[]{:S(2)}, u32[]{:S(2)}) %collective-permute-start.8) | collective-permute-done | bytes 98336 | tf_op jit(solution)/shard_map/ppermute | solution.py:315
  164.6 0.6 copy-done.10
  165.2 2.1 %shard_map.107 = bf16[128,2048]{1,0:T(8,128)(2,1)} custom-call(s32[1,4]{1,0:T(1,128)} %add_bitcast_fusion.where_ref, bf16[3,128,128]{2,1,0:T(8,128)(2,1)} %get-tuple-element.27.refs_0_, bf16[3,128,128]{2,1,0:T(8,128)(2,1)} %copy-done.4, bf16[3,128,128]{2,1,0:T(8,128)(2,1)} %copy-done.5, bf16[3,128,128]{2,1,0:T(8,128)(2,1)} %copy-done.6, ...), custom_call_target="tpu_custom_call" | custom-call | flops 1000000 | bytes 1000000 | tf_op jit(solution)/shard_map/pallas_call | solution.py:321
  167.3 2.0 %shard_map.108 = bf16[128,1024]{1,0:T(8,128)(2,1)} custom-call(s32[1,4]{1,0:T(1,128)} %add_bitcast_fusion.where_ref, bf16[3,128,128]{2,1,0:T(8,128)(2,1)} %get-tuple-element.27.refs_0_, bf16[3,128,128]{2,1,0:T(8,128)(2,1)} %copy-done.4, bf16[3,128,128]{2,1,0:T(8,128)(2,1)} %copy-done.5, bf16[3,128,128]{2,1,0:T(8,128)(2,1)} %copy-done.6, ...), custom_call_target="tpu_custom_call" | custom-call | flops 1000000 | bytes 1000000 | tf_op jit(solution)/shard_map/pallas_call | solution.py:324
  169.3 0.8 copy-done.1
  170.1 2.2 %shard_map.111 = f32[288,1024]{1,0:T(8,128)} custom-call(bf16[32,72,128]{2,1,0:T(8,128)(2,1)} %copy-done.1), custom_call_target="tpu_custom_call" | custom-call | flops 1000000 | bytes 1000000 | tf_op jit(solution)/shard_map/pallas_call | solution.py:327
  (31 shorter events, 0.1 us)
Async XLA Ops:
  4.4 30.1 %all-to-all-start = ((bf16[16,392,128]{2,1,0:T(8,128)(2,1)}), bf16[16,392,128]{2,1,0:T(8,128)(2,1)S(1)}, u32[]{:S(2)}, u32[]{:S(2)}) async-start(bf16[16,392,128]{2,1,0:T(8,128)(2,1)} %shard_map.103), calls=%async_computation | async-start | bytes 3211264 | tf_op jit(solution)/shard_map/all_to_all | solution.py:278
  14.1 37.3 %collective-permute-start.9 = (bf16[3,1152,128]{2,1,0:T(8,128)(2,1)}, bf16[3,1152,128]{2,1,0:T(8,128)(2,1)}, u32[]{:S(2)}, u32[]{:S(2)}) collective-permute-start(bf16[3,1152,128]{2,1,0:T(8,128)(2,1)} %get-tuple-element.36), channel_id=1, source_target_pairs={{0,32},{32,0},{1,33},{33,1},{2,34},{34,2},{3,35},{35,3},{4,36},{36... | collective-permute-start | bytes 2654216 | tf_op jit(solution)/shard_map/ppermute | solution.py:263
  34.5 1.2 copy-start
  34.5 21.6 %collective-permute-start = (bf16[16,128,128]{2,1,0:T(8,128)(2,1)S(1)}, bf16[16,128,128]{2,1,0:T(8,128)(2,1)}, u32[]{:S(2)}, u32[]{:S(2)}) collective-permute-start(bf16[16,128,128]{2,1,0:T(8,128)(2,1)S(1)} %slice.9), channel_id=1, source_target_pairs={{0,16},{16,0},{1,17},{17,1},{2,18},{18,2},{3,19},{19,3},{4,20},{20... | collective-permute-start | bytes 1572872 | tf_op jit(solution)/shard_map/ppermute | solution.py:263
  35.6 34.6 %all-to-all-start.1 = ((bf16[4,1152,128]{2,1,0:T(8,128)(2,1)}), bf16[4,1152,128]{2,1,0:T(8,128)(2,1)S(1)}, u32[]{:S(2)}, u32[]{:S(2)}) async-start(bf16[4,1152,128]{2,1,0:T(8,128)(2,1)} %get-tuple-element.35), calls=%async_computation.1 | async-start | bytes 2359296 | tf_op jit(solution)/shard_map/all_to_all | solution.py:286
  52.5 24.7 %collective-permute-start.10 = (bf16[1152,128]{1,0:T(8,128)(2,1)S(1)}, bf16[1152,128]{1,0:T(8,128)(2,1)S(1)}, u32[]{:S(2)}, u32[]{:S(2)}) collective-permute-start(bf16[1152,128]{1,0:T(8,128)(2,1)S(1)} %get-tuple-element.42), channel_id=1, source_target_pairs={{0,64},{64,0},{128,192},{192,128},{1,65},{65,1},{129,193},{193,129... | collective-permute-start | bytes 884744 | tf_op jit(solution)/shard_map/ppermute | solution.py:267
  54.1 25.2 %collective-permute-start.12 = (bf16[1152,128]{1,0:T(8,128)(2,1)S(1)}, bf16[1152,128]{1,0:T(8,128)(2,1)}, u32[]{:S(2)}, u32[]{:S(2)}) collective-permute-start(bf16[1152,128]{1,0:T(8,128)(2,1)S(1)} %get-tuple-element.41), channel_id=1, source_target_pairs={{0,192},{64,128},{128,64},{192,0},{1,193},{65,129},{129,65},{193,1... | collective-permute-start | bytes 884744 | tf_op jit(solution)/shard_map/ppermute | solution.py:267
  70.3 1.7 %collective-permute-start.13 = (bf16[8,128,128]{2,1,0:T(8,128)(2,1)}, bf16[8,128,128]{2,1,0:T(8,128)(2,1)S(1)}, u32[]{:S(2)}, u32[]{:S(2)}) collective-permute-start(bf16[8,128,128]{2,1,0:T(8,128)(2,1)} %get-tuple-element.38), channel_id=1, source_target_pairs={{0,16},{16,0},{1,17},{17,1},{2,18},{18,2},{3,19},{19,3},{4,20},{20... | collective-permute-start | bytes 786440 | tf_op jit(solution)/shard_map/ppermute | solution.py:263
  70.3 21.8 %copy-start.2 = (bf16[4,1152,128]{2,1,0:T(8,128)(2,1)}, bf16[4,1152,128]{2,1,0:T(8,128)(2,1)S(1)}, u32[]{:S(2)}) copy-start(bf16[4,1152,128]{2,1,0:T(8,128)(2,1)S(1)} %all-to-all-done.1.mine_ref) | copy-start | bytes 3538948
  70.3 21.7 %collective-permute-start.11 = (bf16[1152,128]{1,0:T(8,128)(2,1)S(1)}, bf16[1152,128]{1,0:T(8,128)(2,1)S(1)}, u32[]{:S(2)}, u32[]{:S(2)}) collective-permute-start(bf16[1152,128]{1,0:T(8,128)(2,1)S(1)} %dynamic-slice_bitcast_fusion), channel_id=1, source_target_pairs={{0,32},{32,0},{1,33},{33,1},{2,34},{34,2},{3,35},{35,3},{4,36},{36... | collective-permute-start | bytes 884744 | tf_op jit(solution)/shard_map/ppermute | solution.py:263
  72.0 0.7 copy-start.11
  74.6 9.4 %collective-permute-start.14 = (bf16[8,128,128]{2,1,0:T(8,128)(2,1)}, bf16[8,128,128]{2,1,0:T(8,128)(2,1)S(1)}, u32[]{:S(2)}, u32[]{:S(2)}) collective-permute-start(bf16[8,128,128]{2,1,0:T(8,128)(2,1)} %shard_map.109.refs_0_), channel_id=1, source_target_pairs={{0,64},{64,0},{128,192},{192,128},{1,65},{65,1},{129,193},{193,129... | collective-permute-start | bytes 786440 | tf_op jit(solution)/shard_map/ppermute | solution.py:267
  75.1 14.3 %collective-permute-start.15 = (bf16[8,128,128]{2,1,0:T(8,128)(2,1)}, bf16[8,128,128]{2,1,0:T(8,128)(2,1)S(1)}, u32[]{:S(2)}, u32[]{:S(2)}) collective-permute-start(bf16[8,128,128]{2,1,0:T(8,128)(2,1)} %shard_map.109.refs_0_), channel_id=1, source_target_pairs={{0,128},{64,192},{128,0},{192,64},{1,129},{65,193},{129,1},{193,65... | collective-permute-start | bytes 786440 | tf_op jit(solution)/shard_map/ppermute | solution.py:267
  77.2 14.8 %copy-start.13 = (bf16[1152,128]{1,0:T(8,128)(2,1)}, bf16[1152,128]{1,0:T(8,128)(2,1)S(1)}, u32[]{:S(2)}) copy-start(bf16[1152,128]{1,0:T(8,128)(2,1)S(1)} %collective-permute-done.10.one_ref) | copy-start | bytes 884740
  77.2 14.8 %collective-permute-start.16 = (bf16[8,128,128]{2,1,0:T(8,128)(2,1)}, bf16[8,128,128]{2,1,0:T(8,128)(2,1)S(1)}, u32[]{:S(2)}, u32[]{:S(2)}) collective-permute-start(bf16[8,128,128]{2,1,0:T(8,128)(2,1)} %shard_map.109.refs_0_), channel_id=1, source_target_pairs={{0,192},{64,128},{128,64},{192,0},{1,193},{65,129},{129,65},{193,1... | collective-permute-start | bytes 786440 | tf_op jit(solution)/shard_map/ppermute | solution.py:267
  84.0 8.1 %copy-start.15 = (bf16[8,128,128]{2,1,0:T(8,128)(2,1)}, bf16[8,128,128]{2,1,0:T(8,128)(2,1)S(1)}, u32[]{:S(2)}) copy-start(bf16[8,128,128]{2,1,0:T(8,128)(2,1)S(1)} %collective-permute-done.14.refs_1_) | copy-start | bytes 786436
  89.5 2.6 %copy-start.16 = (bf16[8,128,128]{2,1,0:T(8,128)(2,1)}, bf16[8,128,128]{2,1,0:T(8,128)(2,1)S(1)}, u32[]{:S(2)}) copy-start(bf16[8,128,128]{2,1,0:T(8,128)(2,1)S(1)} %collective-permute-done.15.refs_2_) | copy-start | bytes 786436
  92.0 0.7 copy-start.17
  92.7 0.7 copy-start.14
  98.0 2.2 %collective-permute-start.17 = (bf16[4,4,2,72,128]{4,3,2,1,0:T(8,128)(2,1)}, bf16[4,4,2,72,128]{4,3,2,1,0:T(8,128)(2,1)S(1)}, u32[]{:S(2)}, u32[]{:S(2)}) collective-permute-start(bf16[4,4,2,72,128]{4,3,2,1,0:T(8,128)(2,1)} %get-tuple-element.40), channel_id=1, source_target_pairs={{0,16},{16,0},{1,17},{17,1},{2,18},{18,2},{3,19},{19,3},{4,20},{20... | collective-permute-start | bytes 1769480 | tf_op jit(solution)/shard_map/ppermute | solution.py:263
  129.7 6.7 %copy-start.12 = (bf16[2,8,128,128]{3,2,1,0:T(8,128)(2,1)S(1)}, bf16[2,8,128,128]{3,2,1,0:T(8,128)(2,1)}, u32[]{:S(2)}) copy-start(bf16[2,8,128,128]{3,2,1,0:T(8,128)(2,1)} %get-tuple-element.26) | copy-start | bytes 1572868
  130.6 38.7 %all-to-all-start.3 = ((bf16[32,72,128]{2,1,0:T(8,128)(2,1)}), bf16[32,72,128]{2,1,0:T(8,128)(2,1)S(1)}, u32[]{:S(2)}, u32[]{:S(2)}) async-start(bf16[32,72,128]{2,1,0:T(8,128)(2,1)} %bitcast.19), calls=%async_computation.3 | async-start | bytes 1179648 | tf_op jit(solution)/shard_map/all_to_all | solution.py:317
  136.4 2.0 %collective-permute-start.1 = (bf16[2,8,128,128]{3,2,1,0:T(8,128)(2,1)S(1)}, bf16[2,8,128,128]{3,2,1,0:T(8,128)(2,1)S(1)}, u32[]{:S(2)}, u32[]{:S(2)}) collective-permute-start(bf16[2,8,128,128]{3,2,1,0:T(8,128)(2,1)S(1)} %copy-done.12), channel_id=1, source_target_pairs={{0,16},{16,0},{1,17},{17,1},{2,18},{18,2},{3,19},{19,3},{4,20},{20... | collective-permute-start | bytes 1572872 | tf_op jit(solution)/shard_map/ppermute | solution.py:263
  138.4 0.8 copy-start.3
  141.4 12.0 %collective-permute-start.2 = (bf16[3,128,128]{2,1,0:T(8,128)(2,1)}, bf16[3,128,128]{2,1,0:T(8,128)(2,1)S(1)}, u32[]{:S(2)}, u32[]{:S(2)}) collective-permute-start(bf16[3,128,128]{2,1,0:T(8,128)(2,1)} %get-tuple-element.28), channel_id=1, source_target_pairs={{0,32},{16,48},{32,0},{48,16},{64,96},{80,112},{96,64},{112,80},{1... | collective-permute-start | bytes 294920 | tf_op jit(solution)/shard_map/ppermute | solution.py:315
  143.5 12.6 %collective-permute-start.3 = (bf16[3,128,128]{2,1,0:T(8,128)(2,1)}, bf16[3,128,128]{2,1,0:T(8,128)(2,1)S(1)}, u32[]{:S(2)}, u32[]{:S(2)}) collective-permute-start(bf16[3,128,128]{2,1,0:T(8,128)(2,1)} %get-tuple-element.29), channel_id=1, source_target_pairs={{0,64},{16,80},{32,96},{48,112},{64,0},{80,16},{96,32},{112,48},{1... | collective-permute-start | bytes 294920 | tf_op jit(solution)/shard_map/ppermute | solution.py:315
  143.5 14.5 %collective-permute-start.4 = (bf16[3,128,128]{2,1,0:T(8,128)(2,1)}, bf16[3,128,128]{2,1,0:T(8,128)(2,1)S(1)}, u32[]{:S(2)}, u32[]{:S(2)}) collective-permute-start(bf16[3,128,128]{2,1,0:T(8,128)(2,1)} %get-tuple-element.30), channel_id=1, source_target_pairs={{0,96},{16,112},{32,64},{48,80},{64,32},{80,48},{96,0},{112,16},{1... | collective-permute-start | bytes 294920 | tf_op jit(solution)/shard_map/ppermute | solution.py:315
  146.4 11.6 %collective-permute-start.5 = (bf16[3,128,128]{2,1,0:T(8,128)(2,1)}, bf16[3,128,128]{2,1,0:T(8,128)(2,1)S(1)}, u32[]{:S(2)}, u32[]{:S(2)}) collective-permute-start(bf16[3,128,128]{2,1,0:T(8,128)(2,1)} %get-tuple-element.31), channel_id=1, source_target_pairs={{0,128},{16,144},{32,160},{48,176},{64,192},{80,208},{96,224},{112... | collective-permute-start | bytes 294920 | tf_op jit(solution)/shard_map/ppermute | solution.py:315
  147.9 10.1 %collective-permute-start.6 = (bf16[3,128,128]{2,1,0:T(8,128)(2,1)}, bf16[3,128,128]{2,1,0:T(8,128)(2,1)S(1)}, u32[]{:S(2)}, u32[]{:S(2)}) collective-permute-start(bf16[3,128,128]{2,1,0:T(8,128)(2,1)} %get-tuple-element.32), channel_id=1, source_target_pairs={{0,160},{16,176},{32,128},{48,144},{64,224},{80,240},{96,192},{112... | collective-permute-start | bytes 294920 | tf_op jit(solution)/shard_map/ppermute | solution.py:315
  153.4 11.2 %copy-start.4 = (bf16[3,128,128]{2,1,0:T(8,128)(2,1)}, bf16[3,128,128]{2,1,0:T(8,128)(2,1)S(1)}, u32[]{:S(2)}) copy-start(bf16[3,128,128]{2,1,0:T(8,128)(2,1)S(1)} %collective-permute-done.2.refs_1_) | copy-start | bytes 294916
  153.4 6.0 %collective-permute-start.7 = (bf16[3,128,128]{2,1,0:T(8,128)(2,1)}, bf16[3,128,128]{2,1,0:T(8,128)(2,1)S(1)}, u32[]{:S(2)}, u32[]{:S(2)}) collective-permute-start(bf16[3,128,128]{2,1,0:T(8,128)(2,1)} %get-tuple-element.33), channel_id=1, source_target_pairs={{0,192},{16,208},{32,224},{48,240},{64,128},{80,144},{96,160},{112... | collective-permute-start | bytes 294920 | tf_op jit(solution)/shard_map/ppermute | solution.py:315
  156.1 8.5 %copy-start.5 = (bf16[3,128,128]{2,1,0:T(8,128)(2,1)}, bf16[3,128,128]{2,1,0:T(8,128)(2,1)S(1)}, u32[]{:S(2)}) copy-start(bf16[3,128,128]{2,1,0:T(8,128)(2,1)S(1)} %collective-permute-done.3.refs_2_) | copy-start | bytes 294916
  156.1 8.4 %collective-permute-start.8 = (bf16[3,128,128]{2,1,0:T(8,128)(2,1)}, bf16[3,128,128]{2,1,0:T(8,128)(2,1)S(1)}, u32[]{:S(2)}, u32[]{:S(2)}) collective-permute-start(bf16[3,128,128]{2,1,0:T(8,128)(2,1)} %get-tuple-element.34), channel_id=1, source_target_pairs={{0,224},{16,240},{32,192},{48,208},{64,160},{80,176},{96,128},{112... | collective-permute-start | bytes 294920 | tf_op jit(solution)/shard_map/ppermute | solution.py:315
  158.0 6.5 %copy-start.6 = (bf16[3,128,128]{2,1,0:T(8,128)(2,1)}, bf16[3,128,128]{2,1,0:T(8,128)(2,1)S(1)}, u32[]{:S(2)}) copy-start(bf16[3,128,128]{2,1,0:T(8,128)(2,1)S(1)} %collective-permute-done.4.refs_3_) | copy-start | bytes 294916
  158.0 6.5 %copy-start.7 = (bf16[3,128,128]{2,1,0:T(8,128)(2,1)}, bf16[3,128,128]{2,1,0:T(8,128)(2,1)S(1)}, u32[]{:S(2)}) copy-start(bf16[3,128,128]{2,1,0:T(8,128)(2,1)S(1)} %collective-permute-done.5.refs_4_) | copy-start | bytes 294916
  158.0 6.5 %copy-start.8 = (bf16[3,128,128]{2,1,0:T(8,128)(2,1)}, bf16[3,128,128]{2,1,0:T(8,128)(2,1)S(1)}, u32[]{:S(2)}) copy-start(bf16[3,128,128]{2,1,0:T(8,128)(2,1)S(1)} %collective-permute-done.6.refs_5_) | copy-start | bytes 294916
  159.4 5.2 %copy-start.9 = (bf16[3,128,128]{2,1,0:T(8,128)(2,1)}, bf16[3,128,128]{2,1,0:T(8,128)(2,1)S(1)}, u32[]{:S(2)}) copy-start(bf16[3,128,128]{2,1,0:T(8,128)(2,1)S(1)} %collective-permute-done.7.refs_6_) | copy-start | bytes 294916
  164.5 0.6 copy-start.10
  169.3 0.8 copy-start.1

commit v5 on v4

--- a/solution.py
+++ b/solution.py
@@ -16,7 +16,7 @@
 D = 4608
 ROWS = D // SLABS
 QUARTER = ROWS // 4
-BK = 256
+BK = 512
 BQ = 512
 HALF = TOK // 2
 PACK = 3 * TOK + 8
@@ -70,9 +70,9 @@
 
 
 def sort_slabs(core, in_ref, oth_ref, q_s, g_s, k_s, v_s, nd_s, inv_s):
-    for s in range(SLABS):
+    places = [jnp.max(in_ref[s, 3 * TOK :, :].astype(f32)[6:7, :]).astype(jnp.int32) for s in range(SLABS)]
+    for s, p in enumerate(places):
         extra = in_ref[s, 3 * TOK :, :].astype(f32)
-        p = jnp.max(extra[6:7, :]).astype(jnp.int32)
         inv_s[p] = s
         at = pl.ds(pl.multiple_of(p * TOK, TOK), TOK)
         q_s[at, :] = in_ref[s, 0:TOK, :]
@@ -93,6 +93,8 @@
 
 
 def block_at(i, size):
+    if isinstance(i, int):
+        return pl.ds(i * size, size)
     return pl.ds(pl.multiple_of(i * size, size), size)
 
 
@@ -105,7 +107,7 @@
     sort_slabs(core, in_ref, oth_ref, q_s, g_s, k_s, v_s, nd_s, inv_s)
     dq_s[...] = jnp.zeros_like(dq_s)
 
-    def per_key_block(j, _):
+    def per_key_block(j):
         kb = k_s[block_at(j, BK), :]
         vb = v_s[block_at(j, BK), :]
         kt = kb.T
@@ -129,13 +131,14 @@
 
         dk_s[...], dv_s[...] = one(first, True)
 
-        def per_query_block(i, _):
+        def per_query_block(i):
             dk, dv = one(i, False)
             dk_s[...] += dk
             dv_s[...] += dv
             return 0
 
-        lax.fori_loop(first + 1, LENGTH // BQ, per_query_block, 0)
+        for i in range(first + 1, LENGTH // BQ):
+            per_query_block(i)
         for t in range(BK // TOK):
             s = inv_s[j * (BK // TOK) + t]
             to = (s // 2) ^ chip
@@ -143,8 +146,8 @@
 
             @pl.when(s % 2 == core)
             def _():
-                vkeep_ref[s // 2] = dv_s[rows, :]
-                kkeep_ref[to] = dk_s[rows, :] * SCALE
+                vkeep_ref[s // 2] = dv_s[rows, :].astype(bf16)
+                kkeep_ref[to] = (dk_s[rows, :] * SCALE).astype(bf16)
 
             @pl.when(s % 2 != core)
             def _():
@@ -153,7 +156,8 @@
 
         return 0
 
-    lax.fori_loop(0, LENGTH // BK, per_key_block, 0)
+    for j in range(LENGTH // BK):
+        per_key_block(j)
     for i in range(LENGTH // BQ):
         rows = (dq_s[i].T * SCALE).astype(bf16)
         for t in range(BQ // TOK):
@@ -168,10 +172,6 @@
             @pl.when(s % 2 != core)
             def _():
                 send_ref[0, to] = part
-
-
-def sum_kernel(keep_ref, came_ref, out_ref):
-    out_ref[...] = (keep_ref[...] + came_ref[...].astype(f32)).astype(bf16)
 
 
 def weight_kernel(where_ref, mine_ref, early_ref, one_ref, two_ref, three_ref, *refs):
@@ -192,7 +192,7 @@
         return dot(jnp.concatenate(tokens, axis=1), grads, ((1,), (0,)))
 
     for part in range(2):
-        mine = rows_of(part, core)
+        mine = rows_of(part, core).astype(bf16)
         for k in range(XS):
             for r in range(4):
                 keep_ref[r, at_x ^ k, part] = mine[r * QUARTER : (r + 1) * QUARTER, k * HEAD : (k + 1) * HEAD]
@@ -202,19 +202,11 @@
                 send_ref[r, at_x ^ k, part] = sent[r * QUARTER : (r + 1) * QUARTER, k * HEAD : (k + 1) * HEAD]
 
 
-def finish_kernel(in_ref, out_ref):
-    for high in range(2):
-        for b in range(SLABS):
-            head = 2 * (b % XS) + high
-            rows = slice((b // XS) * QUARTER, (b // XS + 1) * QUARTER)
-            out_ref[rows, head * HEAD : (head + 1) * HEAD] = in_ref[high * SLABS + b].astype(f32)
-
-
 def join_kernel(q_ref, k_ref, came_ref, *out_refs):
     for k in range(CHIPS):
         out_refs[k][0] = q_ref[k]
         out_refs[k][1] = came_ref[0, k]
-        out_refs[k][2] = (k_ref[k] + came_ref[1, k].astype(f32)).astype(bf16)
+        out_refs[k][2] = (k_ref[k].astype(f32) + came_ref[1, k].astype(f32)).astype(bf16)
 
 
 def place_query_kernel(where_ref, *refs):
@@ -286,12 +278,13 @@
     late = lax.all_to_all(late, "x", 0, 0, tiled=True)
     v_keep, v_send, q_keep, k_keep, qk_send = call(
         attn_kernel, [SMEM, VMEM, VMEM],
-        [shaped(TOKENS, f32), shaped(TOKENS, bf16), shaped(TOKENS, bf16), shaped(TOKENS, f32), shaped((2, *TOKENS), bf16)],
+        [shaped(TOKENS, bf16)] * 4 + [shaped((2, *TOKENS), bf16)],
         SORTED + ROWED + [pltpu.VMEM((LENGTH // BQ, HEAD, BQ), f32)] + BLOCK * 2 + PLACES,
         flops=6 * 10**9,
     )(where, got, other)
     v_came = swapped(v_send)
-    (dv,) = call(sum_kernel, [VMEM] * 2, [shaped(TOKENS, bf16)])(v_keep, v_came)
+    dv = (v_keep.astype(f32) + v_came.astype(f32)).astype(bf16)
+    early, dv = lax.optimization_barrier((early, dv))
     dvs = [dv]
     for k in range(1, XS):
         dvs.append(along_x(dv, k))
@@ -301,11 +294,11 @@
     w_shape = (4, XS, 2, QUARTER, HEAD)
     w_keep, w_send = call(
         weight_kernel, [SMEM] + [VMEM] * (5 + XS),
-        [shaped(w_shape, f32), shaped(w_shape, bf16)],
+        [shaped(w_shape, bf16)] * 2,
         [pltpu.VMEM((LENGTH // 2, XS * HEAD), bf16)], flops=2 * 10**9,
     )(where, late, early, one, two, three, *dvs)
     w_came = swapped(w_send)
-    w = (w_keep + w_came.astype(f32)).astype(bf16)
+    w = (w_keep.astype(f32) + w_came.astype(f32)).astype(bf16)
     parts = lax.all_to_all(w.reshape(SLABS, 2 * QUARTER, HEAD), "batch", 0, 0, tiled=True)
     back = call(join_kernel, [VMEM] * 3, [shaped((3, TOK, HEAD), bf16)] * CHIPS)(
         q_keep, k_keep, qk_came
@@ -324,8 +317,8 @@
     (grad_key,) = call(
         place_key_kernel, [SMEM] + [VMEM] * CHIPS, [shaped((TOK, KV_HEADS * HEAD), bf16)]
     )(where, *pieces)
-    (weight,) = call(finish_kernel, [VMEM], [shaped((ROWS, KV_HEADS * HEAD), f32)])(blocks)
-    return (grad_query[None], grad_key[None], weight)
+    weight = blocks.reshape(2, 4, XS, QUARTER, HEAD).transpose(1, 3, 2, 0, 4).reshape(ROWS, KV_HEADS * HEAD)
+    return (grad_query[None], grad_key[None], weight.astype(f32))
 
 
 def solution(mesh):

time: 173 us -> 171 us (0.988)
  the two profiles are of different devices: /device:TPU:8 before, /device:TPU:2 now
where the time goes in v5:
time: 171 us; the launch traced here: 168 us
  waiting for transfers between devices  57.6 us (34%)
  starting transfers between devices  44.1 us (26%)
  blocking collectives  27.8 us (16%)
  Pallas kernels  27.7 us (16%)
  local copies, waits for them, and re-layouts  6.8 us (4%)
  other arithmetic  2.08 us (1%)
    all_to_all x1, blocking collectives, inner(): lax.all_to_all(w.reshape(SLABS, 2 * QUARTER, HEAD), 'batch', 0, 0, tiled=...  27.8 us
    all_to_all x1, waiting for transfers between devices, inner(): got = lax.all_to_all(packed, SEQ, 0, 0, tiled=True)  18.5 us
    ppermute x5, waiting for transfers between devices, along_x(): return lax.ppermute(array, 'x', [(i, i ^ k) for i in range(XS)])  16.5 us
    ppermute x7, starting transfers between devices, inner(): lax.ppermute(back[k], SEQ, [(i, i ^ 2 * k) for i in range(SLABS)])  15.9 us
    pallas_call x1, Pallas kernels, inner(): call(attn_kernel, [SMEM, VMEM, VMEM], [shaped(TOKENS, bf16)] * 4 + [shape...  11 us
    ppermute x6, waiting for transfers between devices, swapped(): return lax.ppermute(array, axis, SWAP)  9.86 us
    all_to_all x1, waiting for transfers between devices, inner(): late = lax.all_to_all(late, 'x', 0, 0, tiled=True)  8.24 us
    ppermute x5, starting transfers between devices, along_x(): return lax.ppermute(array, 'x', [(i, i ^ k) for i in range(XS)])  7.8 us
  transfers between devices with their start and end apart: 21, of which 12 were waited for; matrix products, arithmetic and copies ran while one was open for 0% of the time, Pallas kernels for 12%

profile of v5, /device:TPU:2, one launch (start us, length us, event | category | flops | bytes accessed | tf_op | source)
XLA Modules:
  0.0 167.6 jit_solution(6411695511478884411)
XLA Ops:
  1.3 3.1 %shard_map.103 = bf16[16,392,128]{2,1,0:T(8,128)(2,1)} custom-call(s32[1,1]{1,0:T(1,128)S(6)} %copy.12.place_ref, bf16[128,2048]{1,0:T(8,128)(2,1)} %bitcast.32, bf16[128,2048]{1,0:T(8,128)(2,1)} %bitcast.33, bf16[128,2048]{1,0:T(8,128)(2,1)} %bitcast.34, bf16[128,1024]{1,0:T(8,128)(2,1)} %bitcast.35, bf16[128,1024]{1,0:T(8,128)(2,1)} %bitcast.36, ...), custom_call_target="tpu_custom_call" | custom-call | flops 1000000 | bytes 1000000 | tf_op jit(solution)/shard_map/pallas_call | solution.py:267
  4.4 7.5 %all-to-all-start = ((bf16[16,392,128]{2,1,0:T(8,128)(2,1)}), bf16[16,392,128]{2,1,0:T(8,128)(2,1)S(1)}, u32[]{:S(2)}, u32[]{:S(2)}) async-start(bf16[16,392,128]{2,1,0:T(8,128)(2,1)} %shard_map.103), calls=%async_computation | async-start | bytes 3211264 | tf_op jit(solution)/shard_map/all_to_all | solution.py:270
  11.9 0.6 add_bitcast_fusion.where_ref
  12.5 2.9 %shard_map.104 = (bf16[4,1152,128]{2,1,0:T(8,128)(2,1)}, bf16[3,1152,128]{2,1,0:T(8,128)(2,1)}) custom-call(s32[1,4]{1,0:T(1,128)} %add_bitcast_fusion.where_ref, bf16[128,4608]{1,0:T(8,128)(2,1)} %bitcast.30), custom_call_target="tpu_custom_call" | custom-call | flops 1000000 | bytes 1000000 | tf_op jit(solution)/shard_map/pallas_call | solution.py:271
  15.4 18.5 %all-to-all-done.in_ref = bf16[16,392,128]{2,1,0:T(8,128)(2,1)S(1)} async-done(((bf16[16,392,128]{2,1,0:T(8,128)(2,1)}), bf16[16,392,128]{2,1,0:T(8,128)(2,1)S(1)}, u32[]{:S(2)}, u32[]{:S(2)}) %all-to-all-start) | async-done | bytes 1605664 | tf_op jit(solution)/shard_map/all_to_all | solution.py:270
  34.0 0.1 collective-permute-start
  34.1 0.5 collective-permute-start.9
  34.6 1.4 collective-permute-done.oth_ref
  36.0 0.0 copy-done
  36.0 0.8 copy-done.14
  36.8 11.0 %shard_map.105 = (bf16[8,128,128]{2,1,0:T(8,128)(2,1)}, bf16[8,128,128]{2,1,0:T(8,128)(2,1)}, bf16[8,128,128]{2,1,0:T(8,128)(2,1)}, bf16[8,128,128]{2,1,0:T(8,128)(2,1)}, bf16[2,8,128,128]{3,2,1,0:T(8,128)(2,1)}) custom-call(s32[1,4]{1,0:T(1,128)} %add_bitcast_fusion.where_ref, bf16[16,392,128]{2,1,0:T(8,128)(2,1)} %copy-done, bf16[16,128,128]{2,1,0:T(8,128)(2,1)} %copy-done.14), custom_call_target="tpu_custom_call" | custom-call | flops 6000000000 | bytes 1000000 | tf_op jit(solution)/shard_map/pallas_call | solution.py:279
  47.8 0.1 collective-permute-start.10
  47.9 5.4 %all-to-all-start.1 = ((bf16[4,1152,128]{2,1,0:T(8,128)(2,1)}), bf16[4,1152,128]{2,1,0:T(8,128)(2,1)S(1)}, u32[]{:S(2)}, u32[]{:S(2)}) async-start(bf16[4,1152,128]{2,1,0:T(8,128)(2,1)} %get-tuple-element.37), calls=%async_computation.1 | async-start | bytes 2359296 | tf_op jit(solution)/shard_map/all_to_all | solution.py:278
  53.4 0.0 collective-permute-done.10
  53.4 0.1 add_convert_fusion.1.refs_0_
  53.5 0.0 copy-start.11
  53.5 4.4 %collective-permute-done.9.early_ref = bf16[3,1152,128]{2,1,0:T(8,128)(2,1)S(1)} collective-permute-done((bf16[3,1152,128]{2,1,0:T(8,128)(2,1)}, bf16[3,1152,128]{2,1,0:T(8,128)(2,1)S(1)}, u32[]{:S(2)}, u32[]{:S(2)}) %collective-permute-start.9) | collective-permute-done | bytes 884768 | tf_op jit(solution)/shard_map/ppermute | solution.py:255
  57.9 2.0 %collective-permute-start.11 = (bf16[1152,128]{1,0:T(8,128)(2,1)S(1)}, bf16[1152,128]{1,0:T(8,128)(2,1)}, u32[]{:S(2)}, u32[]{:S(2)}) collective-permute-start(bf16[1152,128]{1,0:T(8,128)(2,1)S(1)} %get-tuple-element.46), channel_id=1, source_target_pairs={{0,64},{64,0},{128,192},{192,128},{1,65},{65,1},{129,193},{193,129... | collective-permute-start | bytes 884744 | tf_op jit(solution)/shard_map/ppermute | solution.py:259
  59.9 0.3 collective-permute-start.13
  60.3 1.4 collective-permute-start.14
  61.6 8.2 %all-to-all-done.1.mine_ref = bf16[4,1152,128]{2,1,0:T(8,128)(2,1)S(1)} async-done(((bf16[4,1152,128]{2,1,0:T(8,128)(2,1)}), bf16[4,1152,128]{2,1,0:T(8,128)(2,1)S(1)}, u32[]{:S(2)}, u32[]{:S(2)}) %all-to-all-start.1) | async-done | bytes 1179680 | tf_op jit(solution)/shard_map/all_to_all | solution.py:278
  69.9 2.0 %collective-permute-start.12 = (bf16[1152,128]{1,0:T(8,128)(2,1)S(1)}, bf16[1152,128]{1,0:T(8,128)(2,1)}, u32[]{:S(2)}, u32[]{:S(2)}) collective-permute-start(bf16[1152,128]{1,0:T(8,128)(2,1)S(1)} %dynamic-slice_bitcast_fusion), channel_id=1, source_target_pairs={{0,32},{32,0},{1,33},{33,1},{2,34},{34,2},{3,35},{35,3},{4,36},{36... | collective-permute-start | bytes 884744 | tf_op jit(solution)/shard_map/ppermute | solution.py:255
  71.9 1.5 collective-permute-start.15
  73.3 6.5 %collective-permute-done.14.refs_1_ = bf16[8,128,128]{2,1,0:T(8,128)(2,1)} collective-permute-done((bf16[8,128,128]{2,1,0:T(8,128)(2,1)S(1)}, bf16[8,128,128]{2,1,0:T(8,128)(2,1)}, u32[]{:S(2)}, u32[]{:S(2)}) %collective-permute-start.14) | collective-permute-done | bytes 262176 | tf_op jit(solution)/shard_map/ppermute | solution.py:259
  79.9 2.6 %collective-permute-start.16 = (bf16[8,128,128]{2,1,0:T(8,128)(2,1)S(1)}, bf16[8,128,128]{2,1,0:T(8,128)(2,1)S(1)}, u32[]{:S(2)}, u32[]{:S(2)}) collective-permute-start(bf16[8,128,128]{2,1,0:T(8,128)(2,1)S(1)} %add_convert_fusion.1.refs_0_), channel_id=1, source_target_pairs={{0,192},{64,128},{128,64},{192,0},{1,193},{65,129},{129,65},{193,1... | collective-permute-start | bytes 786440 | tf_op jit(solution)/shard_map/ppermute | solution.py:259
  82.5 4.4 %collective-permute-done.15.refs_2_ = bf16[8,128,128]{2,1,0:T(8,128)(2,1)S(1)} collective-permute-done((bf16[8,128,128]{2,1,0:T(8,128)(2,1)S(1)}, bf16[8,128,128]{2,1,0:T(8,128)(2,1)S(1)}, u32[]{:S(2)}, u32[]{:S(2)}) %collective-permute-start.15) | collective-permute-done | bytes 262176 | tf_op jit(solution)/shard_map/ppermute | solution.py:259
  86.9 5.5 %collective-permute-done.16.refs_3_ = bf16[8,128,128]{2,1,0:T(8,128)(2,1)S(1)} collective-permute-done((bf16[8,128,128]{2,1,0:T(8,128)(2,1)S(1)}, bf16[8,128,128]{2,1,0:T(8,128)(2,1)S(1)}, u32[]{:S(2)}, u32[]{:S(2)}) %collective-permute-start.16) | collective-permute-done | bytes 262176 | tf_op jit(solution)/shard_map/ppermute | solution.py:259
  92.5 0.0 collective-permute-done.11.one_ref
  92.5 0.0 collective-permute-done.13.three_ref
  92.5 0.7 copy-done.16
  93.2 0.0 collective-permute-done.12.two_ref
  93.2 4.4 %shard_map.109 = (bf16[4,4,2,72,128]{4,3,2,1,0:T(8,128)(2,1)}, bf16[4,4,2,72,128]{4,3,2,1,0:T(8,128)(2,1)}) custom-call(s32[1,4]{1,0:T(1,128)} %add_bitcast_fusion.where_ref, bf16[4,1152,128]{2,1,0:T(8,128)(2,1)} %copy-done.1, bf16[3,1152,128]{2,1,0:T(8,128)(2,1)} %copy-done.3, bf16[1152,128]{1,0:T(8,128)(2,1)} %collective-permute-done.11.one_ref, ...), custom_call_target="tpu_custom_call" | custom-call | flops 2000000000 | bytes 1000000 | tf_op jit(solution)/shard_map/pallas_call | solution.py:295
  97.6 0.0 collective-permute-start.17
  97.7 2.2 %collective-permute-done.17 = bf16[4,4,2,72,128]{4,3,2,1,0:T(8,128)(2,1)S(1)} collective-permute-done((bf16[4,4,2,72,128]{4,3,2,1,0:T(8,128)(2,1)}, bf16[4,4,2,72,128]{4,3,2,1,0:T(8,128)(2,1)S(1)}, u32[]{:S(2)}, u32[]{:S(2)}) %collective-permute-start.17) | collective-permute-done | bytes 589856 | tf_op jit(solution)/shard_map/ppermute | solution.py:255
  99.9 1.2 add_convert_fusion
  101.1 27.8 %all_to_all.20 = bf16[16,144,128]{2,1,0:T(8,128)(2,1)S(1)} all-to-all(bf16[16,144,128]{2,1,0:T(8,128)(2,1)S(1)} %bitcast.29), channel_id=1, replica_groups=mesh['x'=4,'yh'=2,'core'=2,'batch'=16] {'batch'}, dimensions={0} | all-to-all | bytes 1179648 | tf_op jit(solution)/shard_map/all_to_all | solution.py:302
  128.9 0.1 reduce_sum.12
  129.0 0.9 broadcast_in_dim.16
  129.9 4.6 %all-to-all-start.3 = ((bf16[32,72,128]{2,1,0:T(8,128)(2,1)}), bf16[32,72,128]{2,1,0:T(8,128)(2,1)S(1)}, u32[]{:S(2)}, u32[]{:S(2)}) async-start(bf16[32,72,128]{2,1,0:T(8,128)(2,1)} %bitcast.19), calls=%async_computation.3 | async-start | bytes 1179648 | tf_op jit(solution)/shard_map/all_to_all | solution.py:310
  134.5 0.1 collective-permute-start.1
  134.6 1.9 %collective-permute-done.1.came_ref = bf16[2,8,128,128]{3,2,1,0:T(8,128)(2,1)S(1)} collective-permute-done((bf16[2,8,128,128]{3,2,1,0:T(8,128)(2,1)S(1)}, bf16[2,8,128,128]{3,2,1,0:T(8,128)(2,1)S(1)}, u32[]{:S(2)}, u32[]{:S(2)}) %collective-permute-start.1) | collective-permute-done | bytes 524320 | tf_op jit(solution)/shard_map/ppermute | solution.py:255
  136.5 0.8 copy-done.2
  137.3 2.1 %shard_map.106 = (bf16[3,128,128]{2,1,0:T(8,128)(2,1)}, bf16[3,128,128]{2,1,0:T(8,128)(2,1)}, bf16[3,128,128]{2,1,0:T(8,128)(2,1)}, bf16[3,128,128]{2,1,0:T(8,12...) custom-call(bf16[8,128,128]{2,1,0:T(8,128)(2,1)} %get-tuple-element., ...), custom_call_target="tpu_custom_call" | custom-call | flops 1000000 | bytes 1000000 | tf_op jit(solution)/shard_map/pallas_call | solution.py:303
  139.4 3.3 %collective-permute-start.2 = (bf16[3,128,128]{2,1,0:T(8,128)(2,1)}, bf16[3,128,128]{2,1,0:T(8,128)(2,1)S(1)}, u32[]{:S(2)}, u32[]{:S(2)}) collective-permute-start(bf16[3,128,128]{2,1,0:T(8,128)(2,1)} %get-tuple-element.30), channel_id=1, source_target_pairs={{0,32},{16,48},{32,0},{48,16},{64,96},{80,112},{96,64},{112,80},{1... | collective-permute-start | bytes 294920 | tf_op jit(solution)/shard_map/ppermute | solution.py:308
  142.7 1.5 collective-permute-start.3
  144.2 0.2 collective-permute-start.4
  144.4 1.5 collective-permute-start.5
  145.9 4.8 %collective-permute-start.6 = (bf16[3,128,128]{2,1,0:T(8,128)(2,1)}, bf16[3,128,128]{2,1,0:T(8,128)(2,1)S(1)}, u32[]{:S(2)}, u32[]{:S(2)}) collective-permute-start(bf16[3,128,128]{2,1,0:T(8,128)(2,1)} %get-tuple-element.34), channel_id=1, source_target_pairs={{0,160},{16,176},{32,128},{48,144},{64,224},{80,240},{96,192},{112... | collective-permute-start | bytes 294920 | tf_op jit(solution)/shard_map/ppermute | solution.py:308
  150.7 0.0 collective-permute-done.2.refs_1_
  150.7 0.0 collective-permute-start.7
  150.7 0.0 collective-permute-done.3.refs_2_
  150.7 4.7 %collective-permute-start.8 = (bf16[3,128,128]{2,1,0:T(8,128)(2,1)}, bf16[3,128,128]{2,1,0:T(8,128)(2,1)S(1)}, u32[]{:S(2)}, u32[]{:S(2)}) collective-permute-start(bf16[3,128,128]{2,1,0:T(8,128)(2,1)} %get-tuple-element.36), channel_id=1, source_target_pairs={{0,224},{16,240},{32,192},{48,208},{64,160},{80,176},{96,128},{112... | collective-permute-start | bytes 294920 | tf_op jit(solution)/shard_map/ppermute | solution.py:308
  155.4 0.0 collective-permute-done.4.refs_3_
  155.4 0.0 collective-permute-done.5.refs_4_
  155.4 0.3 collective-permute-done.6.refs_5_
  155.7 1.2 collective-permute-done.7.refs_6_
  156.8 3.0 %collective-permute-done.8.refs_7_ = bf16[3,128,128]{2,1,0:T(8,128)(2,1)S(1)} collective-permute-done((bf16[3,128,128]{2,1,0:T(8,128)(2,1)}, bf16[3,128,128]{2,1,0:T(8,128)(2,1)S(1)}, u32[]{:S(2)}, u32[]{:S(2)}) %collective-permute-start.8) | collective-permute-done | bytes 98336 | tf_op jit(solution)/shard_map/ppermute | solution.py:308
  159.9 0.6 copy-done.10
  160.5 2.1 %shard_map.107 = bf16[128,2048]{1,0:T(8,128)(2,1)} custom-call(s32[1,4]{1,0:T(1,128)} %add_bitcast_fusion.where_ref, bf16[3,128,128]{2,1,0:T(8,128)(2,1)} %get-tuple-element.29.refs_0_, bf16[3,128,128]{2,1,0:T(8,128)(2,1)} %copy-done.4, bf16[3,128,128]{2,1,0:T(8,128)(2,1)} %copy-done.5, bf16[3,128,128]{2,1,0:T(8,128)(2,1)} %copy-done.6, ...), custom_call_target="tpu_custom_call" | custom-call | flops 1000000 | bytes 1000000 | tf_op jit(solution)/shard_map/pallas_call | solution.py:314
  162.6 2.0 %shard_map.108 = bf16[128,1024]{1,0:T(8,128)(2,1)} custom-call(s32[1,4]{1,0:T(1,128)} %add_bitcast_fusion.where_ref, bf16[3,128,128]{2,1,0:T(8,128)(2,1)} %get-tuple-element.29.refs_0_, bf16[3,128,128]{2,1,0:T(8,128)(2,1)} %copy-done.4, bf16[3,128,128]{2,1,0:T(8,128)(2,1)} %copy-done.5, bf16[3,128,128]{2,1,0:T(8,128)(2,1)} %copy-done.6, ...), custom_call_target="tpu_custom_call" | custom-call | flops 1000000 | bytes 1000000 | tf_op jit(solution)/shard_map/pallas_call | solution.py:317
  164.6 0.0 all-to-all-done.3
  164.6 0.1 convert_bitcast_fusion
  164.7 0.9 copy.11
  165.6 2.0 %reshape.26 = f32[288,1024]{1,0:T(8,128)} reshape(f32[4,72,4,2,128]{4,3,2,1,0:T(2,128)S(1)} %copy.11) | data formatting | bytes 2359296 | tf_op jit(solution)/shard_map/convert_element_type | solution.py:321
  (31 shorter events, 0.2 us)
Async XLA Ops:
  4.4 29.6 %all-to-all-start = ((bf16[16,392,128]{2,1,0:T(8,128)(2,1)}), bf16[16,392,128]{2,1,0:T(8,128)(2,1)S(1)}, u32[]{:S(2)}, u32[]{:S(2)}) async-start(bf16[16,392,128]{2,1,0:T(8,128)(2,1)} %shard_map.103), calls=%async_computation | async-start | bytes 3211264 | tf_op jit(solution)/shard_map/all_to_all | solution.py:270
  34.0 2.1 %copy-start = (bf16[16,392,128]{2,1,0:T(8,128)(2,1)}, bf16[16,392,128]{2,1,0:T(8,128)(2,1)S(1)}, u32[]{:S(2)}) copy-start(bf16[16,392,128]{2,1,0:T(8,128)(2,1)S(1)} %all-to-all-done.in_ref) | copy-start | bytes 4816900
  34.0 2.0 %collective-permute-start = (bf16[16,128,128]{2,1,0:T(8,128)(2,1)S(1)}, bf16[16,128,128]{2,1,0:T(8,128)(2,1)S(1)}, u32[]{:S(2)}, u32[]{:S(2)}) collective-permute-start(bf16[16,128,128]{2,1,0:T(8,128)(2,1)S(1)} %slice.9), channel_id=1, source_target_pairs={{0,16},{16,0},{1,17},{17,1},{2,18},{18,2},{3,19},{19,3},{4,20},{20... | collective-permute-start | bytes 1572872 | tf_op jit(solution)/shard_map/ppermute | solution.py:255
  34.1 23.8 %collective-permute-start.9 = (bf16[3,1152,128]{2,1,0:T(8,128)(2,1)}, bf16[3,1152,128]{2,1,0:T(8,128)(2,1)S(1)}, u32[]{:S(2)}, u32[]{:S(2)}) collective-permute-start(bf16[3,1152,128]{2,1,0:T(8,128)(2,1)} %get-tuple-element.38), channel_id=1, source_target_pairs={{0,32},{32,0},{1,33},{33,1},{2,34},{34,2},{3,35},{35,3},{4,36},{36... | collective-permute-start | bytes 2654216 | tf_op jit(solution)/shard_map/ppermute | solution.py:255
  36.0 0.8 copy-start.14
  47.8 5.6 %copy-start.12 = (bf16[8,128,128]{2,1,0:T(8,128)(2,1)S(1)}, bf16[8,128,128]{2,1,0:T(8,128)(2,1)}, u32[]{:S(2)}) copy-start(bf16[8,128,128]{2,1,0:T(8,128)(2,1)} %get-tuple-element.39) | copy-start | bytes 786436
  47.8 5.6 %collective-permute-start.10 = (bf16[8,128,128]{2,1,0:T(8,128)(2,1)}, bf16[8,128,128]{2,1,0:T(8,128)(2,1)S(1)}, u32[]{:S(2)}, u32[]{:S(2)}) collective-permute-start(bf16[8,128,128]{2,1,0:T(8,128)(2,1)} %get-tuple-element.40), channel_id=1, source_target_pairs={{0,16},{16,0},{1,17},{17,1},{2,18},{18,2},{3,19},{19,3},{4,20},{20... | collective-permute-start | bytes 786440 | tf_op jit(solution)/shard_map/ppermute | solution.py:255
  47.9 21.9 %all-to-all-start.1 = ((bf16[4,1152,128]{2,1,0:T(8,128)(2,1)}), bf16[4,1152,128]{2,1,0:T(8,128)(2,1)S(1)}, u32[]{:S(2)}, u32[]{:S(2)}) async-start(bf16[4,1152,128]{2,1,0:T(8,128)(2,1)} %get-tuple-element.37), calls=%async_computation.1 | async-start | bytes 2359296 | tf_op jit(solution)/shard_map/all_to_all | solution.py:278
  53.5 39.7 %copy-start.11 = (bf16[8,128,128]{2,1,0:T(8,128)(2,1)}, bf16[8,128,128]{2,1,0:T(8,128)(2,1)S(1)}, u32[]{:S(2)}) copy-start(bf16[8,128,128]{2,1,0:T(8,128)(2,1)S(1)} %add_convert_fusion.1.refs_0_) | copy-start | bytes 786436
  57.9 35.3 %copy-start.3 = (bf16[3,1152,128]{2,1,0:T(8,128)(2,1)}, bf16[3,1152,128]{2,1,0:T(8,128)(2,1)S(1)}, u32[]{:S(2)}) copy-start(bf16[3,1152,128]{2,1,0:T(8,128)(2,1)S(1)} %collective-permute-done.9.early_ref) | copy-start | bytes 2654212
  57.9 34.5 %collective-permute-start.11 = (bf16[1152,128]{1,0:T(8,128)(2,1)S(1)}, bf16[1152,128]{1,0:T(8,128)(2,1)}, u32[]{:S(2)}, u32[]{:S(2)}) collective-permute-start(bf16[1152,128]{1,0:T(8,128)(2,1)S(1)} %get-tuple-element.46), channel_id=1, source_target_pairs={{0,64},{64,0},{128,192},{192,128},{1,65},{65,1},{129,193},{193,129... | collective-permute-start | bytes 884744 | tf_op jit(solution)/shard_map/ppermute | solution.py:259
  59.9 32.5 %collective-permute-start.13 = (bf16[1152,128]{1,0:T(8,128)(2,1)S(1)}, bf16[1152,128]{1,0:T(8,128)(2,1)}, u32[]{:S(2)}, u32[]{:S(2)}) collective-permute-start(bf16[1152,128]{1,0:T(8,128)(2,1)S(1)} %get-tuple-element.45), channel_id=1, source_target_pairs={{0,192},{64,128},{128,64},{192,0},{1,193},{65,129},{129,65},{193,1... | collective-permute-start | bytes 884744 | tf_op jit(solution)/shard_map/ppermute | solution.py:259
  60.3 19.6 %collective-permute-start.14 = (bf16[8,128,128]{2,1,0:T(8,128)(2,1)S(1)}, bf16[8,128,128]{2,1,0:T(8,128)(2,1)}, u32[]{:S(2)}, u32[]{:S(2)}) collective-permute-start(bf16[8,128,128]{2,1,0:T(8,128)(2,1)S(1)} %add_convert_fusion.1.refs_0_), channel_id=1, source_target_pairs={{0,64},{64,0},{128,192},{192,128},{1,65},{65,1},{129,193},{193,129... | collective-permute-start | bytes 786440 | tf_op jit(solution)/shard_map/ppermute | solution.py:259
  69.9 23.3 %copy-start.1 = (bf16[4,1152,128]{2,1,0:T(8,128)(2,1)}, bf16[4,1152,128]{2,1,0:T(8,128)(2,1)S(1)}, u32[]{:S(2)}) copy-start(bf16[4,1152,128]{2,1,0:T(8,128)(2,1)S(1)} %all-to-all-done.1.mine_ref) | copy-start | bytes 3538948
  69.9 23.3 %collective-permute-start.12 = (bf16[1152,128]{1,0:T(8,128)(2,1)S(1)}, bf16[1152,128]{1,0:T(8,128)(2,1)}, u32[]{:S(2)}, u32[]{:S(2)}) collective-permute-start(bf16[1152,128]{1,0:T(8,128)(2,1)S(1)} %dynamic-slice_bitcast_fusion), channel_id=1, source_target_pairs={{0,32},{32,0},{1,33},{33,1},{2,34},{34,2},{3,35},{35,3},{4,36},{36... | collective-permute-start | bytes 884744 | tf_op jit(solution)/shard_map/ppermute | solution.py:255
  71.9 15.0 %collective-permute-start.15 = (bf16[8,128,128]{2,1,0:T(8,128)(2,1)S(1)}, bf16[8,128,128]{2,1,0:T(8,128)(2,1)S(1)}, u32[]{:S(2)}, u32[]{:S(2)}) collective-permute-start(bf16[8,128,128]{2,1,0:T(8,128)(2,1)S(1)} %add_convert_fusion.1.refs_0_), channel_id=1, source_target_pairs={{0,128},{64,192},{128,0},{192,64},{1,129},{65,193},{129,1},{193,65... | collective-permute-start | bytes 786440 | tf_op jit(solution)/shard_map/ppermute | solution.py:259
  79.9 12.6 %collective-permute-start.16 = (bf16[8,128,128]{2,1,0:T(8,128)(2,1)S(1)}, bf16[8,128,128]{2,1,0:T(8,128)(2,1)S(1)}, u32[]{:S(2)}, u32[]{:S(2)}) collective-permute-start(bf16[8,128,128]{2,1,0:T(8,128)(2,1)S(1)} %add_convert_fusion.1.refs_0_), channel_id=1, source_target_pairs={{0,192},{64,128},{128,64},{192,0},{1,193},{65,129},{129,65},{193,1... | collective-permute-start | bytes 786440 | tf_op jit(solution)/shard_map/ppermute | solution.py:259
  86.9 5.5 %copy-start.15 = (bf16[8,128,128]{2,1,0:T(8,128)(2,1)}, bf16[8,128,128]{2,1,0:T(8,128)(2,1)S(1)}, u32[]{:S(2)}) copy-start(bf16[8,128,128]{2,1,0:T(8,128)(2,1)S(1)} %collective-permute-done.15.refs_2_) | copy-start | bytes 786436
  92.5 0.7 copy-start.16
  97.6 2.2 %collective-permute-start.17 = (bf16[4,4,2,72,128]{4,3,2,1,0:T(8,128)(2,1)}, bf16[4,4,2,72,128]{4,3,2,1,0:T(8,128)(2,1)S(1)}, u32[]{:S(2)}, u32[]{:S(2)}) collective-permute-start(bf16[4,4,2,72,128]{4,3,2,1,0:T(8,128)(2,1)} %get-tuple-element.44), channel_id=1, source_target_pairs={{0,16},{16,0},{1,17},{17,1},{2,18},{18,2},{3,19},{19,3},{4,20},{20... | collective-permute-start | bytes 1769480 | tf_op jit(solution)/shard_map/ppermute | solution.py:255
  128.9 5.6 %copy-start.13 = (bf16[2,8,128,128]{3,2,1,0:T(8,128)(2,1)S(1)}, bf16[2,8,128,128]{3,2,1,0:T(8,128)(2,1)}, u32[]{:S(2)}) copy-start(bf16[2,8,128,128]{3,2,1,0:T(8,128)(2,1)} %get-tuple-element.28) | copy-start | bytes 1572868
  129.9 34.7 %all-to-all-start.3 = ((bf16[32,72,128]{2,1,0:T(8,128)(2,1)}), bf16[32,72,128]{2,1,0:T(8,128)(2,1)S(1)}, u32[]{:S(2)}, u32[]{:S(2)}) async-start(bf16[32,72,128]{2,1,0:T(8,128)(2,1)} %bitcast.19), calls=%async_computation.3 | async-start | bytes 1179648 | tf_op jit(solution)/shard_map/all_to_all | solution.py:310
  134.5 2.0 %collective-permute-start.1 = (bf16[2,8,128,128]{3,2,1,0:T(8,128)(2,1)S(1)}, bf16[2,8,128,128]{3,2,1,0:T(8,128)(2,1)S(1)}, u32[]{:S(2)}, u32[]{:S(2)}) collective-permute-start(bf16[2,8,128,128]{3,2,1,0:T(8,128)(2,1)S(1)} %copy-done.13), channel_id=1, source_target_pairs={{0,16},{16,0},{1,17},{17,1},{2,18},{18,2},{3,19},{19,3},{4,20},{20... | collective-permute-start | bytes 1572872 | tf_op jit(solution)/shard_map/ppermute | solution.py:255
  136.5 0.8 copy-start.2
  139.4 11.3 %collective-permute-start.2 = (bf16[3,128,128]{2,1,0:T(8,128)(2,1)}, bf16[3,128,128]{2,1,0:T(8,128)(2,1)S(1)}, u32[]{:S(2)}, u32[]{:S(2)}) collective-permute-start(bf16[3,128,128]{2,1,0:T(8,128)(2,1)} %get-tuple-element.30), channel_id=1, source_target_pairs={{0,32},{16,48},{32,0},{48,16},{64,96},{80,112},{96,64},{112,80},{1... | collective-permute-start | bytes 294920 | tf_op jit(solution)/shard_map/ppermute | solution.py:308
  142.7 8.0 %collective-permute-start.3 = (bf16[3,128,128]{2,1,0:T(8,128)(2,1)}, bf16[3,128,128]{2,1,0:T(8,128)(2,1)S(1)}, u32[]{:S(2)}, u32[]{:S(2)}) collective-permute-start(bf16[3,128,128]{2,1,0:T(8,128)(2,1)} %get-tuple-element.31), channel_id=1, source_target_pairs={{0,64},{16,80},{32,96},{48,112},{64,0},{80,16},{96,32},{112,48},{1... | collective-permute-start | bytes 294920 | tf_op jit(solution)/shard_map/ppermute | solution.py:308
  144.2 11.2 %collective-permute-start.4 = (bf16[3,128,128]{2,1,0:T(8,128)(2,1)}, bf16[3,128,128]{2,1,0:T(8,128)(2,1)S(1)}, u32[]{:S(2)}, u32[]{:S(2)}) collective-permute-start(bf16[3,128,128]{2,1,0:T(8,128)(2,1)} %get-tuple-element.32), channel_id=1, source_target_pairs={{0,96},{16,112},{32,64},{48,80},{64,32},{80,48},{96,0},{112,16},{1... | collective-permute-start | bytes 294920 | tf_op jit(solution)/shard_map/ppermute | solution.py:308
  144.4 11.0 %collective-permute-start.5 = (bf16[3,128,128]{2,1,0:T(8,128)(2,1)}, bf16[3,128,128]{2,1,0:T(8,128)(2,1)S(1)}, u32[]{:S(2)}, u32[]{:S(2)}) collective-permute-start(bf16[3,128,128]{2,1,0:T(8,128)(2,1)} %get-tuple-element.33), channel_id=1, source_target_pairs={{0,128},{16,144},{32,160},{48,176},{64,192},{80,208},{96,224},{112... | collective-permute-start | bytes 294920 | tf_op jit(solution)/shard_map/ppermute | solution.py:308
  145.9 9.8 %collective-permute-start.6 = (bf16[3,128,128]{2,1,0:T(8,128)(2,1)}, bf16[3,128,128]{2,1,0:T(8,128)(2,1)S(1)}, u32[]{:S(2)}, u32[]{:S(2)}) collective-permute-start(bf16[3,128,128]{2,1,0:T(8,128)(2,1)} %get-tuple-element.34), channel_id=1, source_target_pairs={{0,160},{16,176},{32,128},{48,144},{64,224},{80,240},{96,192},{112... | collective-permute-start | bytes 294920 | tf_op jit(solution)/shard_map/ppermute | solution.py:308
  150.7 9.2 %copy-start.4 = (bf16[3,128,128]{2,1,0:T(8,128)(2,1)}, bf16[3,128,128]{2,1,0:T(8,128)(2,1)S(1)}, u32[]{:S(2)}) copy-start(bf16[3,128,128]{2,1,0:T(8,128)(2,1)S(1)} %collective-permute-done.2.refs_1_) | copy-start | bytes 294916
  150.7 6.1 %collective-permute-start.7 = (bf16[3,128,128]{2,1,0:T(8,128)(2,1)}, bf16[3,128,128]{2,1,0:T(8,128)(2,1)S(1)}, u32[]{:S(2)}, u32[]{:S(2)}) collective-permute-start(bf16[3,128,128]{2,1,0:T(8,128)(2,1)} %get-tuple-element.35), channel_id=1, source_target_pairs={{0,192},{16,208},{32,224},{48,240},{64,128},{80,144},{96,160},{112... | collective-permute-start | bytes 294920 | tf_op jit(solution)/shard_map/ppermute | solution.py:308
  150.7 9.2 %copy-start.5 = (bf16[3,128,128]{2,1,0:T(8,128)(2,1)}, bf16[3,128,128]{2,1,0:T(8,128)(2,1)S(1)}, u32[]{:S(2)}) copy-start(bf16[3,128,128]{2,1,0:T(8,128)(2,1)S(1)} %collective-permute-done.3.refs_2_) | copy-start | bytes 294916
  150.7 9.1 %collective-permute-start.8 = (bf16[3,128,128]{2,1,0:T(8,128)(2,1)}, bf16[3,128,128]{2,1,0:T(8,128)(2,1)S(1)}, u32[]{:S(2)}, u32[]{:S(2)}) collective-permute-start(bf16[3,128,128]{2,1,0:T(8,128)(2,1)} %get-tuple-element.36), channel_id=1, source_target_pairs={{0,224},{16,240},{32,192},{48,208},{64,160},{80,176},{96,128},{112... | collective-permute-start | bytes 294920 | tf_op jit(solution)/shard_map/ppermute | solution.py:308
  155.4 4.5 %copy-start.6 = (bf16[3,128,128]{2,1,0:T(8,128)(2,1)}, bf16[3,128,128]{2,1,0:T(8,128)(2,1)S(1)}, u32[]{:S(2)}) copy-start(bf16[3,128,128]{2,1,0:T(8,128)(2,1)S(1)} %collective-permute-done.4.refs_3_) | copy-start | bytes 294916
  155.4 4.5 %copy-start.7 = (bf16[3,128,128]{2,1,0:T(8,128)(2,1)}, bf16[3,128,128]{2,1,0:T(8,128)(2,1)S(1)}, u32[]{:S(2)}) copy-start(bf16[3,128,128]{2,1,0:T(8,128)(2,1)S(1)} %collective-permute-done.5.refs_4_) | copy-start | bytes 294916
  155.6 4.2 %copy-start.8 = (bf16[3,128,128]{2,1,0:T(8,128)(2,1)}, bf16[3,128,128]{2,1,0:T(8,128)(2,1)S(1)}, u32[]{:S(2)}) copy-start(bf16[3,128,128]{2,1,0:T(8,128)(2,1)S(1)} %collective-permute-done.6.refs_5_) | copy-start | bytes 294916
  156.8 3.0 %copy-start.9 = (bf16[3,128,128]{2,1,0:T(8,128)(2,1)}, bf16[3,128,128]{2,1,0:T(8,128)(2,1)S(1)}, u32[]{:S(2)}) copy-start(bf16[3,128,128]{2,1,0:T(8,128)(2,1)S(1)} %collective-permute-done.7.refs_6_) | copy-start | bytes 294916
  159.8 0.6 copy-start.10

commit v6 on v5

--- a/solution.py
+++ b/solution.py
@@ -21,6 +21,7 @@
 HALF = TOK // 2
 PACK = 3 * TOK + 8
 TILES = 9
+PACKED = 4
 XS = 4
 EARLY = (0, 1, 3)
 
@@ -45,7 +46,7 @@
 
 def pack_kernel(place_ref, q_ref, g_ref, o_ref, k_ref, v_ref, n_ref, out_ref):
     place = jnp.full((1, TOK), place_ref[0, 0], jnp.int32).astype(f32)
-    for s in range(SLABS):
+    for s in range(PACKED):
         cols = slice(s * HEAD, (s + 1) * HEAD)
         kv_cols = slice((s // 2) * HEAD, (s // 2 + 1) * HEAD)
         half = slice((s % 2) * HALF, (s % 2 + 1) * HALF)
@@ -56,17 +57,23 @@
         out_ref[s, 2 * TOK + HALF : 3 * TOK, :] = v_ref[half, kv_cols]
         prod = grads.astype(f32) * o_ref[:, cols].astype(f32)
         delta = jnp.sum(prod.T, axis=0, keepdims=True)
-        rows = (*three_parts(n_ref[s : s + 1, :]), *three_parts(delta), place, jnp.zeros_like(place))
+        norm = n_ref[pl.ds(pl.program_id(0) * PACKED + s, 1), :]
+        rows = (*three_parts(norm), *three_parts(delta), place, jnp.zeros_like(place))
         out_ref[s, 3 * TOK :, :] = jnp.concatenate(rows, axis=0).astype(bf16)
 
 
-def pack_late_kernel(where_ref, x_ref, out_ref, early_ref):
+def pack_early_kernel(where_ref, x_ref, out_ref):
+    for j, k in enumerate(EARLY):
+        for t in range(TILES):
+            tile = (where_ref[0, 3] ^ k) * TILES + t
+            out_ref[j, t * TOK : (t + 1) * TOK, :] = x_ref[:, block_at(tile, 128)].T
+
+
+def pack_late_kernel(x_ref, out_ref):
     for x in range(XS):
         for t in range(TILES):
             tile = TILES * x + t
             out_ref[x, t * TOK : (t + 1) * TOK, :] = x_ref[:, tile * 128 : (tile + 1) * 128].T
-    for j, k in enumerate(EARLY):
-        early_ref[j] = out_ref[where_ref[0, 3] ^ k]
 
 
 def sort_slabs(core, in_ref, oth_ref, q_s, g_s, k_s, v_s, nd_s, inv_s):
@@ -264,14 +271,19 @@
 ):
     core, high, at_x = (lax.axis_index(a).astype(jnp.int32) for a in ("core", "yh", "x"))
     where = jnp.stack([core, at_x * 2 + high, high, at_x]).reshape(1, 4)
-    (packed,) = call(pack_kernel, [SMEM] + [VMEM] * 6, [shaped((SLABS, PACK, HEAD), bf16)])(
+    wide = pl.BlockSpec((TOK, PACKED * HEAD), lambda i: (0, i))
+    narrow = pl.BlockSpec((TOK, PACKED // 2 * HEAD), lambda i: (0, i))
+    (packed,) = call(
+        pack_kernel, [SMEM, wide, wide, wide, narrow, narrow, VMEM], [shaped((SLABS, PACK, HEAD), bf16)],
+        grid=(SLABS // PACKED,), out_specs=[pl.BlockSpec((PACKED, PACK, HEAD), lambda i: (i, 0, 0))],
+    )(
         slab_order, query_rows[0], output_grad[0], attn_output[0], key_rows[0], value_rows[0], log_norm[0]
     )
     got = lax.all_to_all(packed, SEQ, 0, 0, tiled=True)
-    late, early = call(
-        pack_late_kernel, [SMEM, VMEM],
-        [shaped((XS, TILES * TOK, 128), bf16), shaped((len(EARLY), TILES * TOK, 128), bf16)],
+    (early,) = call(
+        pack_early_kernel, [SMEM, VMEM], [shaped((len(EARLY), TILES * TOK, 128), bf16)]
     )(where, normed_input[0])
+    (late,) = call(pack_late_kernel, [VMEM], [shaped((XS, TILES * TOK, 128), bf16)])(normed_input[0])
     early = swapped(early, "yh")
     got, late = lax.optimization_barrier((got, late))
     other = swapped(got[:, 2 * TOK : 3 * TOK, :])
@@ -284,7 +296,6 @@
     )(where, got, other)
     v_came = swapped(v_send)
     dv = (v_keep.astype(f32) + v_came.astype(f32)).astype(bf16)
-    early, dv = lax.optimization_barrier((early, dv))
     dvs = [dv]
     for k in range(1, XS):
         dvs.append(along_x(dv, k))
@@ -306,10 +317,10 @@
     pieces = [back[0]]
     for k in range(1, CHIPS):
         pieces.append(lax.ppermute(back[k], SEQ, [(i, i ^ (2 * k)) for i in range(SLABS)]))
-    piece = jnp.sum(parts.astype(f32), axis=0).astype(bf16).reshape(2, 1, QUARTER, HEAD)
+    piece = jnp.sum(parts.astype(f32), axis=0).astype(bf16).reshape(1, 2, QUARTER, HEAD)
     blocks = lax.all_to_all(
-        jnp.broadcast_to(piece, (2, SLABS, QUARTER, HEAD)).reshape(2 * SLABS, QUARTER, HEAD),
-        ("yh", "batch"), 0, 0, tiled=True,
+        jnp.broadcast_to(piece, (SLABS, 2, QUARTER, HEAD)).reshape(2 * SLABS, QUARTER, HEAD),
+        ("batch", "yh"), 0, 0, tiled=True,
     )
     (grad_query,) = call(
         place_query_kernel, [SMEM] + [VMEM] * CHIPS, [shaped((TOK, HEADS * HEAD), bf16)]
@@ -317,7 +328,7 @@
     (grad_key,) = call(
         place_key_kernel, [SMEM] + [VMEM] * CHIPS, [shaped((TOK, KV_HEADS * HEAD), bf16)]
     )(where, *pieces)
-    weight = blocks.reshape(2, 4, XS, QUARTER, HEAD).transpose(1, 3, 2, 0, 4).reshape(ROWS, KV_HEADS * HEAD)
+    weight = blocks.reshape(4, KV_HEADS, QUARTER, HEAD).transpose(0, 2, 1, 3).reshape(ROWS, KV_HEADS * HEAD)
     return (grad_query[None], grad_key[None], weight.astype(f32))
 
 

time: 171 us -> 162 us (0.947)
  the two profiles are of different devices: /device:TPU:2 before, /device:TPU:32 now
where the time goes in v6:
time: 162 us; the launch traced here: 161 us
  waiting for transfers between devices  50.1 us (31%)
  starting transfers between devices  42.4 us (26%)
  Pallas kernels  30.8 us (19%)
  blocking collectives  26.8 us (17%)
  local copies, waits for them, and re-layouts  6.05 us (4%)
  other arithmetic  3.24 us (2%)
    all_to_all x1, blocking collectives, inner(): lax.all_to_all(w.reshape(SLABS, 2 * QUARTER, HEAD), 'batch', 0, 0, tiled=...  26.8 us
    all_to_all x1, waiting for transfers between devices, inner(): got = lax.all_to_all(packed, SEQ, 0, 0, tiled=True)  21.3 us
    ppermute x7, starting transfers between devices, inner(): lax.ppermute(back[k], SEQ, [(i, i ^ 2 * k) for i in range(SLABS)])  17.3 us
    ppermute x5, waiting for transfers between devices, along_x(): return lax.ppermute(array, 'x', [(i, i ^ k) for i in range(XS)])  12.9 us
    ppermute x6, waiting for transfers between devices, swapped(): return lax.ppermute(array, axis, SWAP)  11.2 us
    pallas_call x1, Pallas kernels, inner(): call(attn_kernel, [SMEM, VMEM, VMEM], [shaped(TOKENS, bf16)] * 4 + [shape...  11 us
    all_to_all x1, starting transfers between devices, inner(): got = lax.all_to_all(packed, SEQ, 0, 0, tiled=True)  7.03 us
    all_to_all x1, starting transfers between devices, inner(): lax.all_to_all(jnp.broadcast_to(piece, (SLABS, 2, QUARTER, HEAD)).reshape...  5.42 us
  transfers between devices with their start and end apart: 21, of which 9 were waited for; matrix products, arithmetic and copies ran while one was open for 1% of the time, Pallas kernels for 14%

profile of v6, /device:TPU:32, one launch (start us, length us, event | category | flops | bytes accessed | tf_op | source)
XLA Modules:
  0.0 160.9 jit_solution(5326855895115742063)
XLA Ops:
  1.3 4.0 %shard_map.103 = bf16[16,392,128]{2,1,0:T(8,128)(2,1)} custom-call(s32[1,1]{1,0:T(1,128)S(6)} %copy.15.place_ref, bf16[128,2048]{1,0:T(8,128)(2,1)} %bitcast.40, bf16[128,2048]{1,0:T(8,128)(2,1)} %bitcast.41, bf16[128,2048]{1,0:T(8,128)(2,1)} %bitcast.42, bf16[128,1024]{1,0:T(8,128)(2,1)} %bitcast.43, bf16[128,1024]{1,0:T(8,128)(2,1)} %bitcast.44, ...), custom_call_target="tpu_custom_call" | custom-call | flops 1000000 | bytes 1000000 | tf_op jit(solution)/shard_map/pallas_call | solution.py:276
  5.3 7.0 %all-to-all-start = ((bf16[16,392,128]{2,1,0:T(8,128)(2,1)}), bf16[16,392,128]{2,1,0:T(8,128)(2,1)S(1)}, u32[]{:S(2)}, u32[]{:S(2)}) async-start(bf16[16,392,128]{2,1,0:T(8,128)(2,1)} %shard_map.103), calls=%async_computation | async-start | bytes 3211264 | tf_op jit(solution)/shard_map/all_to_all | solution.py:282
  12.3 2.6 %shard_map.104 = bf16[4,1152,128]{2,1,0:T(8,128)(2,1)} custom-call(bf16[128,4608]{1,0:T(8,128)(2,1)} %bitcast.33), custom_call_target="tpu_custom_call" | custom-call | flops 1000000 | bytes 1000000 | tf_op jit(solution)/shard_map/pallas_call | solution.py:286
  14.9 21.3 %all-to-all-done.in_ref = bf16[16,392,128]{2,1,0:T(8,128)(2,1)S(1)} async-done(((bf16[16,392,128]{2,1,0:T(8,128)(2,1)}), bf16[16,392,128]{2,1,0:T(8,128)(2,1)S(1)}, u32[]{:S(2)}, u32[]{:S(2)}) %all-to-all-start) | async-done | bytes 1605664 | tf_op jit(solution)/shard_map/all_to_all | solution.py:282
  36.3 0.1 collective-permute-start
  36.4 0.8 add_bitcast_fusion.where_ref
  37.2 2.5 %shard_map.109 = bf16[3,1152,128]{2,1,0:T(8,128)(2,1)} custom-call(s32[1,4]{1,0:T(1,128)} %add_bitcast_fusion.where_ref, bf16[128,4608]{1,0:T(8,128)(2,1)} %bitcast.34), custom_call_target="tpu_custom_call" | custom-call | flops 1000000 | bytes 1000000 | tf_op jit(solution)/shard_map/pallas_call | solution.py:283
  39.7 1.2 collective-permute-start.9
  41.0 3.5 %all-to-all-start.1 = ((bf16[4,1152,128]{2,1,0:T(8,128)(2,1)}), bf16[4,1152,128]{2,1,0:T(8,128)(2,1)S(1)}, u32[]{:S(2)}, u32[]{:S(2)}) async-start(bf16[4,1152,128]{2,1,0:T(8,128)(2,1)} %shard_map.104), calls=%async_computation.1 | async-start | bytes 2359296 | tf_op jit(solution)/shard_map/all_to_all | solution.py:290
  44.5 0.0 collective-permute-done.oth_ref
  44.5 0.0 copy-start.15
  44.5 0.8 copy-done.15
  45.3 11.0 %shard_map.105 = (bf16[8,128,128]{2,1,0:T(8,128)(2,1)}, bf16[8,128,128]{2,1,0:T(8,128)(2,1)}, bf16[8,128,128]{2,1,0:T(8,128)(2,1)}, bf16[8,128,128]{2,1,0:T(8,128)(2,1)}, bf16[2,8,128,128]{3,2,1,0:T(8,128)(2,1)}) custom-call(s32[1,4]{1,0:T(1,128)} %add_bitcast_fusion.where_ref, bf16[16,392,128]{2,1,0:T(8,128)(2,1)} %copy-done, bf16[16,128,128]{2,1,0:T(8,128)(2,1)} %copy-done.15), custom_call_target="tpu_custom_call" | custom-call | flops 6000000000 | bytes 1000000 | tf_op jit(solution)/shard_map/pallas_call | solution.py:291
  56.3 0.0 collective-permute-start.13
  56.3 7.0 %collective-permute-done.9.early_ref = bf16[3,1152,128]{2,1,0:T(8,128)(2,1)S(1)} collective-permute-done((bf16[3,1152,128]{2,1,0:T(8,128)(2,1)}, bf16[3,1152,128]{2,1,0:T(8,128)(2,1)S(1)}, u32[]{:S(2)}, u32[]{:S(2)}) %collective-permute-start.9) | collective-permute-done | bytes 884768 | tf_op jit(solution)/shard_map/ppermute | solution.py:262
  63.4 0.2 collective-permute-start.10
  63.5 1.6 collective-permute-start.12
  65.1 0.0 all-to-all-done.1.mine_ref
  65.2 2.3 %collective-permute-start.11 = (bf16[1152,128]{1,0:T(8,128)(2,1)S(1)}, bf16[1152,128]{1,0:T(8,128)(2,1)}, u32[]{:S(2)}, u32[]{:S(2)}) collective-permute-start(bf16[1152,128]{1,0:T(8,128)(2,1)S(1)} %dynamic-slice_bitcast_fusion), channel_id=1, source_target_pairs={{0,32},{32,0},{1,33},{33,1},{2,34},{34,2},{3,35},{35,3},{4,36},{36... | collective-permute-start | bytes 884744 | tf_op jit(solution)/shard_map/ppermute | solution.py:262
  67.5 0.0 collective-permute-done.13
  67.5 0.7 copy-done.13
  68.2 1.0 add_convert_fusion.1.refs_0_
  69.3 0.0 copy-start.11
  69.3 0.3 collective-permute-start.14
  69.5 2.0 %collective-permute-start.15 = (bf16[8,128,128]{2,1,0:T(8,128)(2,1)S(1)}, bf16[8,128,128]{2,1,0:T(8,128)(2,1)S(1)}, u32[]{:S(2)}, u32[]{:S(2)}) collective-permute-start(bf16[8,128,128]{2,1,0:T(8,128)(2,1)S(1)} %add_convert_fusion.1.refs_0_), channel_id=1, source_target_pairs={{0,128},{64,192},{128,0},{192,64},{1,129},{65,193},{129,1},{193,65... | collective-permute-start | bytes 786440 | tf_op jit(solution)/shard_map/ppermute | solution.py:266
  71.6 1.4 collective-permute-done.10.one_ref
  73.0 1.2 collective-permute-start.16
  74.2 0.0 collective-permute-done.12.three_ref
  74.2 4.5 %collective-permute-done.14.refs_1_ = bf16[8,128,128]{2,1,0:T(8,128)(2,1)S(1)} collective-permute-done((bf16[8,128,128]{2,1,0:T(8,128)(2,1)S(1)}, bf16[8,128,128]{2,1,0:T(8,128)(2,1)S(1)}, u32[]{:S(2)}, u32[]{:S(2)}) %collective-permute-start.14) | collective-permute-done | bytes 262176 | tf_op jit(solution)/shard_map/ppermute | solution.py:266
  78.7 4.8 %collective-permute-done.15.refs_2_ = bf16[8,128,128]{2,1,0:T(8,128)(2,1)S(1)} collective-permute-done((bf16[8,128,128]{2,1,0:T(8,128)(2,1)S(1)}, bf16[8,128,128]{2,1,0:T(8,128)(2,1)S(1)}, u32[]{:S(2)}, u32[]{:S(2)}) %collective-permute-start.15) | collective-permute-done | bytes 262176 | tf_op jit(solution)/shard_map/ppermute | solution.py:266
  83.5 2.1 %collective-permute-done.16.refs_3_ = bf16[8,128,128]{2,1,0:T(8,128)(2,1)S(1)} collective-permute-done((bf16[8,128,128]{2,1,0:T(8,128)(2,1)S(1)}, bf16[8,128,128]{2,1,0:T(8,128)(2,1)S(1)}, u32[]{:S(2)}, u32[]{:S(2)}) %collective-permute-start.16) | collective-permute-done | bytes 262176 | tf_op jit(solution)/shard_map/ppermute | solution.py:266
  85.7 0.0 collective-permute-done.11.two_ref
  85.7 0.7 copy-done.18
  86.4 4.5 %shard_map.110 = (bf16[4,4,2,72,128]{4,3,2,1,0:T(8,128)(2,1)}, bf16[4,4,2,72,128]{4,3,2,1,0:T(8,128)(2,1)}) custom-call(s32[1,4]{1,0:T(1,128)} %add_bitcast_fusion.where_ref, bf16[4,1152,128]{2,1,0:T(8,128)(2,1)} %copy-done.1, bf16[3,1152,128]{2,1,0:T(8,128)(2,1)} %copy-done.3, bf16[1152,128]{1,0:T(8,128)(2,1)} %collective-permute-done.10.one_ref, ...), custom_call_target="tpu_custom_call" | custom-call | flops 2000000000 | bytes 1000000 | tf_op jit(solution)/shard_map/pallas_call | solution.py:306
  90.8 0.0 collective-permute-start.17
  90.8 2.2 %collective-permute-done.17 = bf16[4,4,2,72,128]{4,3,2,1,0:T(8,128)(2,1)S(1)} collective-permute-done((bf16[4,4,2,72,128]{4,3,2,1,0:T(8,128)(2,1)}, bf16[4,4,2,72,128]{4,3,2,1,0:T(8,128)(2,1)S(1)}, u32[]{:S(2)}, u32[]{:S(2)}) %collective-permute-start.17) | collective-permute-done | bytes 589856 | tf_op jit(solution)/shard_map/ppermute | solution.py:262
  93.0 1.2 add_convert_fusion
  94.3 26.8 %all_to_all.20 = bf16[16,144,128]{2,1,0:T(8,128)(2,1)S(1)} all-to-all(bf16[16,144,128]{2,1,0:T(8,128)(2,1)S(1)} %bitcast.37), channel_id=1, replica_groups=mesh['x'=4,'yh'=2,'core'=2,'batch'=16] {'batch'}, dimensions={0} | all-to-all | bytes 1179648 | tf_op jit(solution)/shard_map/all_to_all | solution.py:313
  121.1 0.1 reduce_sum.12
  121.2 0.9 broadcast_in_dim.16
  122.0 5.4 %all-to-all-start.3 = ((bf16[32,72,128]{2,1,0:T(8,128)(2,1)}), bf16[32,72,128]{2,1,0:T(8,128)(2,1)S(1)}, u32[]{:S(2)}, u32[]{:S(2)}) async-start(bf16[32,72,128]{2,1,0:T(8,128)(2,1)} %bitcast.19), calls=%async_computation.3 | async-start | bytes 1179648 | tf_op jit(solution)/shard_map/all_to_all | solution.py:321
  127.5 0.1 collective-permute-start.1
  127.6 1.9 %collective-permute-done.1.came_ref = bf16[2,8,128,128]{3,2,1,0:T(8,128)(2,1)S(1)} collective-permute-done((bf16[2,8,128,128]{3,2,1,0:T(8,128)(2,1)S(1)}, bf16[2,8,128,128]{3,2,1,0:T(8,128)(2,1)S(1)}, u32[]{:S(2)}, u32[]{:S(2)}) %collective-permute-start.1) | collective-permute-done | bytes 524320 | tf_op jit(solution)/shard_map/ppermute | solution.py:262
  129.5 0.8 copy-done.2
  130.3 2.1 %shard_map.106 = (bf16[3,128,128]{2,1,0:T(8,128)(2,1)}, bf16[3,128,128]{2,1,0:T(8,128)(2,1)}, bf16[3,128,128]{2,1,0:T(8,128)(2,1)}, bf16[3,128,128]{2,1,0:T(8,12...) custom-call(bf16[8,128,128]{2,1,0:T(8,128)(2,1)} %get-tuple-element., ...), custom_call_target="tpu_custom_call" | custom-call | flops 1000000 | bytes 1000000 | tf_op jit(solution)/shard_map/pallas_call | solution.py:314
  132.4 3.0 %collective-permute-start.2 = (bf16[3,128,128]{2,1,0:T(8,128)(2,1)}, bf16[3,128,128]{2,1,0:T(8,128)(2,1)S(1)}, u32[]{:S(2)}, u32[]{:S(2)}) collective-permute-start(bf16[3,128,128]{2,1,0:T(8,128)(2,1)} %get-tuple-element.25), channel_id=1, source_target_pairs={{0,32},{16,48},{32,0},{48,16},{64,96},{80,112},{96,64},{112,80},{1... | collective-permute-start | bytes 294920 | tf_op jit(solution)/shard_map/ppermute | solution.py:319
  135.3 0.0 collective-permute-start.3
  135.3 2.0 %collective-permute-start.4 = (bf16[3,128,128]{2,1,0:T(8,128)(2,1)}, bf16[3,128,128]{2,1,0:T(8,128)(2,1)S(1)}, u32[]{:S(2)}, u32[]{:S(2)}) collective-permute-start(bf16[3,128,128]{2,1,0:T(8,128)(2,1)} %get-tuple-element.27), channel_id=1, source_target_pairs={{0,96},{16,112},{32,64},{48,80},{64,32},{80,48},{96,0},{112,16},{1... | collective-permute-start | bytes 294920 | tf_op jit(solution)/shard_map/ppermute | solution.py:319
  137.4 0.8 collective-permute-start.5
  138.1 5.2 %collective-permute-start.6 = (bf16[3,128,128]{2,1,0:T(8,128)(2,1)}, bf16[3,128,128]{2,1,0:T(8,128)(2,1)S(1)}, u32[]{:S(2)}, u32[]{:S(2)}) collective-permute-start(bf16[3,128,128]{2,1,0:T(8,128)(2,1)} %get-tuple-element.29), channel_id=1, source_target_pairs={{0,160},{16,176},{32,128},{48,144},{64,224},{80,240},{96,192},{112... | collective-permute-start | bytes 294920 | tf_op jit(solution)/shard_map/ppermute | solution.py:319
  143.3 0.0 collective-permute-done.2.refs_1_
  143.3 1.3 collective-permute-start.7
  144.6 0.0 collective-permute-done.3.refs_2_
  144.6 5.1 %collective-permute-start.8 = (bf16[3,128,128]{2,1,0:T(8,128)(2,1)}, bf16[3,128,128]{2,1,0:T(8,128)(2,1)S(1)}, u32[]{:S(2)}, u32[]{:S(2)}) collective-permute-start(bf16[3,128,128]{2,1,0:T(8,128)(2,1)} %get-tuple-element.31), channel_id=1, source_target_pairs={{0,224},{16,240},{32,192},{48,208},{64,160},{80,176},{96,128},{112... | collective-permute-start | bytes 294920 | tf_op jit(solution)/shard_map/ppermute | solution.py:319
  149.7 0.0 collective-permute-done.4.refs_3_
  149.7 0.0 collective-permute-done.6.refs_5_
  149.7 0.0 collective-permute-done.7.refs_6_
  149.8 4.8 %collective-permute-done.8.refs_7_ = bf16[3,128,128]{2,1,0:T(8,128)(2,1)S(1)} collective-permute-done((bf16[3,128,128]{2,1,0:T(8,128)(2,1)}, bf16[3,128,128]{2,1,0:T(8,128)(2,1)S(1)}, u32[]{:S(2)}, u32[]{:S(2)}) %collective-permute-start.8) | collective-permute-done | bytes 98336 | tf_op jit(solution)/shard_map/ppermute | solution.py:319
  154.6 0.6 copy-done.10
  155.3 2.1 %shard_map.107 = bf16[128,2048]{1,0:T(8,128)(2,1)} custom-call(s32[1,4]{1,0:T(1,128)} %add_bitcast_fusion.where_ref, bf16[3,128,128]{2,1,0:T(8,128)(2,1)} %get-tuple-element.24.refs_0_, bf16[3,128,128]{2,1,0:T(8,128)(2,1)} %copy-done.4, bf16[3,128,128]{2,1,0:T(8,128)(2,1)} %copy-done.5, bf16[3,128,128]{2,1,0:T(8,128)(2,1)} %copy-done.6, ...), custom_call_target="tpu_custom_call" | custom-call | flops 1000000 | bytes 1000000 | tf_op jit(solution)/shard_map/pallas_call | solution.py:325
  157.4 2.0 %shard_map.108 = bf16[128,1024]{1,0:T(8,128)(2,1)} custom-call(s32[1,4]{1,0:T(1,128)} %add_bitcast_fusion.where_ref, bf16[3,128,128]{2,1,0:T(8,128)(2,1)} %get-tuple-element.24.refs_0_, bf16[3,128,128]{2,1,0:T(8,128)(2,1)} %copy-done.4, bf16[3,128,128]{2,1,0:T(8,128)(2,1)} %copy-done.5, bf16[3,128,128]{2,1,0:T(8,128)(2,1)} %copy-done.6, ...), custom_call_target="tpu_custom_call" | custom-call | flops 1000000 | bytes 1000000 | tf_op jit(solution)/shard_map/pallas_call | solution.py:328
  159.4 0.1 convert_bitcast_fusion
  159.5 0.2 copy.11
  159.7 1.2 copy.14
  (36 shorter events, 0.2 us)
Async XLA Ops:
  5.3 31.0 %all-to-all-start = ((bf16[16,392,128]{2,1,0:T(8,128)(2,1)}), bf16[16,392,128]{2,1,0:T(8,128)(2,1)S(1)}, u32[]{:S(2)}, u32[]{:S(2)}) async-start(bf16[16,392,128]{2,1,0:T(8,128)(2,1)} %shard_map.103), calls=%async_computation | async-start | bytes 3211264 | tf_op jit(solution)/shard_map/all_to_all | solution.py:282
  36.2 3.5 %copy-start = (bf16[16,392,128]{2,1,0:T(8,128)(2,1)}, bf16[16,392,128]{2,1,0:T(8,128)(2,1)S(1)}, u32[]{:S(2)}) copy-start(bf16[16,392,128]{2,1,0:T(8,128)(2,1)S(1)} %all-to-all-done.in_ref) | copy-start | bytes 4816900
  36.3 8.2 %collective-permute-start = (bf16[16,128,128]{2,1,0:T(8,128)(2,1)S(1)}, bf16[16,128,128]{2,1,0:T(8,128)(2,1)S(1)}, u32[]{:S(2)}, u32[]{:S(2)}) collective-permute-start(bf16[16,128,128]{2,1,0:T(8,128)(2,1)S(1)} %slice.9), channel_id=1, source_target_pairs={{0,16},{16,0},{1,17},{17,1},{2,18},{18,2},{3,19},{19,3},{4,20},{20... | collective-permute-start | bytes 1572872 | tf_op jit(solution)/shard_map/ppermute | solution.py:262
  39.7 23.6 %collective-permute-start.9 = (bf16[3,1152,128]{2,1,0:T(8,128)(2,1)}, bf16[3,1152,128]{2,1,0:T(8,128)(2,1)S(1)}, u32[]{:S(2)}, u32[]{:S(2)}) collective-permute-start(bf16[3,1152,128]{2,1,0:T(8,128)(2,1)} %shard_map.109), channel_id=1, source_target_pairs={{0,32},{32,0},{1,33},{33,1},{2,34},{34,2},{3,35},{35,3},{4,36},{36... | collective-permute-start | bytes 2654216 | tf_op jit(solution)/shard_map/ppermute | solution.py:262
  41.0 24.2 %all-to-all-start.1 = ((bf16[4,1152,128]{2,1,0:T(8,128)(2,1)}), bf16[4,1152,128]{2,1,0:T(8,128)(2,1)S(1)}, u32[]{:S(2)}, u32[]{:S(2)}) async-start(bf16[4,1152,128]{2,1,0:T(8,128)(2,1)} %shard_map.104), calls=%async_computation.1 | async-start | bytes 2359296 | tf_op jit(solution)/shard_map/all_to_all | solution.py:290
  44.5 0.8 copy-start.15
  56.3 12.0 %copy-start.12 = (bf16[8,128,128]{2,1,0:T(8,128)(2,1)S(1)}, bf16[8,128,128]{2,1,0:T(8,128)(2,1)}, u32[]{:S(2)}) copy-start(bf16[8,128,128]{2,1,0:T(8,128)(2,1)} %get-tuple-element.33) | copy-start | bytes 786436
  56.3 11.3 %collective-permute-start.13 = (bf16[8,128,128]{2,1,0:T(8,128)(2,1)}, bf16[8,128,128]{2,1,0:T(8,128)(2,1)S(1)}, u32[]{:S(2)}, u32[]{:S(2)}) collective-permute-start(bf16[8,128,128]{2,1,0:T(8,128)(2,1)} %get-tuple-element.34), channel_id=1, source_target_pairs={{0,16},{16,0},{1,17},{17,1},{2,18},{18,2},{3,19},{19,3},{4,20},{20... | collective-permute-start | bytes 786440 | tf_op jit(solution)/shard_map/ppermute | solution.py:262
  63.3 5.9 %copy-start.3 = (bf16[3,1152,128]{2,1,0:T(8,128)(2,1)}, bf16[3,1152,128]{2,1,0:T(8,128)(2,1)S(1)}, u32[]{:S(2)}) copy-start(bf16[3,1152,128]{2,1,0:T(8,128)(2,1)S(1)} %collective-permute-done.9.early_ref) | copy-start | bytes 2654212
  63.4 9.7 %collective-permute-start.10 = (bf16[1152,128]{1,0:T(8,128)(2,1)S(1)}, bf16[1152,128]{1,0:T(8,128)(2,1)}, u32[]{:S(2)}, u32[]{:S(2)}) collective-permute-start(bf16[1152,128]{1,0:T(8,128)(2,1)S(1)} %get-tuple-element.38), channel_id=1, source_target_pairs={{0,64},{64,0},{128,192},{192,128},{1,65},{65,1},{129,193},{193,129... | collective-permute-start | bytes 884744 | tf_op jit(solution)/shard_map/ppermute | solution.py:266
  63.5 10.7 %collective-permute-start.12 = (bf16[1152,128]{1,0:T(8,128)(2,1)S(1)}, bf16[1152,128]{1,0:T(8,128)(2,1)}, u32[]{:S(2)}, u32[]{:S(2)}) collective-permute-start(bf16[1152,128]{1,0:T(8,128)(2,1)S(1)} %get-tuple-element.37), channel_id=1, source_target_pairs={{0,192},{64,128},{128,64},{192,0},{1,193},{65,129},{129,65},{193,1... | collective-permute-start | bytes 884744 | tf_op jit(solution)/shard_map/ppermute | solution.py:266
  65.2 20.5 %copy-start.1 = (bf16[4,1152,128]{2,1,0:T(8,128)(2,1)}, bf16[4,1152,128]{2,1,0:T(8,128)(2,1)S(1)}, u32[]{:S(2)}) copy-start(bf16[4,1152,128]{2,1,0:T(8,128)(2,1)S(1)} %all-to-all-done.1.mine_ref) | copy-start | bytes 3538948
  65.2 20.5 %collective-permute-start.11 = (bf16[1152,128]{1,0:T(8,128)(2,1)S(1)}, bf16[1152,128]{1,0:T(8,128)(2,1)}, u32[]{:S(2)}, u32[]{:S(2)}) collective-permute-start(bf16[1152,128]{1,0:T(8,128)(2,1)S(1)} %dynamic-slice_bitcast_fusion), channel_id=1, source_target_pairs={{0,32},{32,0},{1,33},{33,1},{2,34},{34,2},{3,35},{35,3},{4,36},{36... | collective-permute-start | bytes 884744 | tf_op jit(solution)/shard_map/ppermute | solution.py:262
  67.5 0.7 copy-start.13
  69.3 16.4 %copy-start.11 = (bf16[8,128,128]{2,1,0:T(8,128)(2,1)}, bf16[8,128,128]{2,1,0:T(8,128)(2,1)S(1)}, u32[]{:S(2)}) copy-start(bf16[8,128,128]{2,1,0:T(8,128)(2,1)S(1)} %add_convert_fusion.1.refs_0_) | copy-start | bytes 786436
  69.3 9.4 %collective-permute-start.14 = (bf16[8,128,128]{2,1,0:T(8,128)(2,1)S(1)}, bf16[8,128,128]{2,1,0:T(8,128)(2,1)S(1)}, u32[]{:S(2)}, u32[]{:S(2)}) collective-permute-start(bf16[8,128,128]{2,1,0:T(8,128)(2,1)S(1)} %add_convert_fusion.1.refs_0_), channel_id=1, source_target_pairs={{0,64},{64,0},{128,192},{192,128},{1,65},{65,1},{129,193},{193,129... | collective-permute-start | bytes 786440 | tf_op jit(solution)/shard_map/ppermute | solution.py:266
  69.5 14.0 %collective-permute-start.15 = (bf16[8,128,128]{2,1,0:T(8,128)(2,1)S(1)}, bf16[8,128,128]{2,1,0:T(8,128)(2,1)S(1)}, u32[]{:S(2)}, u32[]{:S(2)}) collective-permute-start(bf16[8,128,128]{2,1,0:T(8,128)(2,1)S(1)} %add_convert_fusion.1.refs_0_), channel_id=1, source_target_pairs={{0,128},{64,192},{128,0},{192,64},{1,129},{65,193},{129,1},{193,65... | collective-permute-start | bytes 786440 | tf_op jit(solution)/shard_map/ppermute | solution.py:266
  73.0 12.6 %collective-permute-start.16 = (bf16[8,128,128]{2,1,0:T(8,128)(2,1)S(1)}, bf16[8,128,128]{2,1,0:T(8,128)(2,1)S(1)}, u32[]{:S(2)}, u32[]{:S(2)}) collective-permute-start(bf16[8,128,128]{2,1,0:T(8,128)(2,1)S(1)} %add_convert_fusion.1.refs_0_), channel_id=1, source_target_pairs={{0,192},{64,128},{128,64},{192,0},{1,193},{65,129},{129,65},{193,1... | collective-permute-start | bytes 786440 | tf_op jit(solution)/shard_map/ppermute | solution.py:266
  78.7 7.0 %copy-start.16 = (bf16[8,128,128]{2,1,0:T(8,128)(2,1)}, bf16[8,128,128]{2,1,0:T(8,128)(2,1)S(1)}, u32[]{:S(2)}) copy-start(bf16[8,128,128]{2,1,0:T(8,128)(2,1)S(1)} %collective-permute-done.14.refs_1_) | copy-start | bytes 786436
  83.5 2.1 %copy-start.17 = (bf16[8,128,128]{2,1,0:T(8,128)(2,1)}, bf16[8,128,128]{2,1,0:T(8,128)(2,1)S(1)}, u32[]{:S(2)}) copy-start(bf16[8,128,128]{2,1,0:T(8,128)(2,1)S(1)} %collective-permute-done.15.refs_2_) | copy-start | bytes 786436
  85.7 0.7 copy-start.18
  90.8 2.2 %collective-permute-start.17 = (bf16[4,4,2,72,128]{4,3,2,1,0:T(8,128)(2,1)}, bf16[4,4,2,72,128]{4,3,2,1,0:T(8,128)(2,1)S(1)}, u32[]{:S(2)}, u32[]{:S(2)}) collective-permute-start(bf16[4,4,2,72,128]{4,3,2,1,0:T(8,128)(2,1)} %get-tuple-element.36), channel_id=1, source_target_pairs={{0,16},{16,0},{1,17},{17,1},{2,18},{18,2},{3,19},{19,3},{4,20},{20... | collective-permute-start | bytes 1769480 | tf_op jit(solution)/shard_map/ppermute | solution.py:262
  121.1 6.4 %copy-start.14 = (bf16[2,8,128,128]{3,2,1,0:T(8,128)(2,1)S(1)}, bf16[2,8,128,128]{3,2,1,0:T(8,128)(2,1)}, u32[]{:S(2)}) copy-start(bf16[2,8,128,128]{3,2,1,0:T(8,128)(2,1)} %get-tuple-element.23) | copy-start | bytes 1572868
  122.0 37.3 %all-to-all-start.3 = ((bf16[32,72,128]{2,1,0:T(8,128)(2,1)}), bf16[32,72,128]{2,1,0:T(8,128)(2,1)S(1)}, u32[]{:S(2)}, u32[]{:S(2)}) async-start(bf16[32,72,128]{2,1,0:T(8,128)(2,1)} %bitcast.19), calls=%async_computation.3 | async-start | bytes 1179648 | tf_op jit(solution)/shard_map/all_to_all | solution.py:321
  127.5 2.0 %collective-permute-start.1 = (bf16[2,8,128,128]{3,2,1,0:T(8,128)(2,1)S(1)}, bf16[2,8,128,128]{3,2,1,0:T(8,128)(2,1)S(1)}, u32[]{:S(2)}, u32[]{:S(2)}) collective-permute-start(bf16[2,8,128,128]{3,2,1,0:T(8,128)(2,1)S(1)} %copy-done.14), channel_id=1, source_target_pairs={{0,16},{16,0},{1,17},{17,1},{2,18},{18,2},{3,19},{19,3},{4,20},{20... | collective-permute-start | bytes 1572872 | tf_op jit(solution)/shard_map/ppermute | solution.py:262
  129.5 0.8 copy-start.2
  132.4 10.9 %collective-permute-start.2 = (bf16[3,128,128]{2,1,0:T(8,128)(2,1)}, bf16[3,128,128]{2,1,0:T(8,128)(2,1)S(1)}, u32[]{:S(2)}, u32[]{:S(2)}) collective-permute-start(bf16[3,128,128]{2,1,0:T(8,128)(2,1)} %get-tuple-element.25), channel_id=1, source_target_pairs={{0,32},{16,48},{32,0},{48,16},{64,96},{80,112},{96,64},{112,80},{1... | collective-permute-start | bytes 294920 | tf_op jit(solution)/shard_map/ppermute | solution.py:319
  135.3 9.3 %collective-permute-start.3 = (bf16[3,128,128]{2,1,0:T(8,128)(2,1)}, bf16[3,128,128]{2,1,0:T(8,128)(2,1)S(1)}, u32[]{:S(2)}, u32[]{:S(2)}) collective-permute-start(bf16[3,128,128]{2,1,0:T(8,128)(2,1)} %get-tuple-element.26), channel_id=1, source_target_pairs={{0,64},{16,80},{32,96},{48,112},{64,0},{80,16},{96,32},{112,48},{1... | collective-permute-start | bytes 294920 | tf_op jit(solution)/shard_map/ppermute | solution.py:319
  135.3 14.4 %collective-permute-start.4 = (bf16[3,128,128]{2,1,0:T(8,128)(2,1)}, bf16[3,128,128]{2,1,0:T(8,128)(2,1)S(1)}, u32[]{:S(2)}, u32[]{:S(2)}) collective-permute-start(bf16[3,128,128]{2,1,0:T(8,128)(2,1)} %get-tuple-element.27), channel_id=1, source_target_pairs={{0,96},{16,112},{32,64},{48,80},{64,32},{80,48},{96,0},{112,16},{1... | collective-permute-start | bytes 294920 | tf_op jit(solution)/shard_map/ppermute | solution.py:319
  137.4 12.3 %collective-permute-start.5 = (bf16[3,128,128]{2,1,0:T(8,128)(2,1)}, bf16[3,128,128]{2,1,0:T(8,128)(2,1)S(1)}, u32[]{:S(2)}, u32[]{:S(2)}) collective-permute-start(bf16[3,128,128]{2,1,0:T(8,128)(2,1)} %get-tuple-element.28), channel_id=1, source_target_pairs={{0,128},{16,144},{32,160},{48,176},{64,192},{80,208},{96,224},{112... | collective-permute-start | bytes 294920 | tf_op jit(solution)/shard_map/ppermute | solution.py:319
  138.1 11.6 %collective-permute-start.6 = (bf16[3,128,128]{2,1,0:T(8,128)(2,1)}, bf16[3,128,128]{2,1,0:T(8,128)(2,1)S(1)}, u32[]{:S(2)}, u32[]{:S(2)}) collective-permute-start(bf16[3,128,128]{2,1,0:T(8,128)(2,1)} %get-tuple-element.29), channel_id=1, source_target_pairs={{0,160},{16,176},{32,128},{48,144},{64,224},{80,240},{96,192},{112... | collective-permute-start | bytes 294920 | tf_op jit(solution)/shard_map/ppermute | solution.py:319
  143.3 11.3 %copy-start.4 = (bf16[3,128,128]{2,1,0:T(8,128)(2,1)}, bf16[3,128,128]{2,1,0:T(8,128)(2,1)S(1)}, u32[]{:S(2)}) copy-start(bf16[3,128,128]{2,1,0:T(8,128)(2,1)S(1)} %collective-permute-done.2.refs_1_) | copy-start | bytes 294916
  143.3 6.4 %collective-permute-start.7 = (bf16[3,128,128]{2,1,0:T(8,128)(2,1)}, bf16[3,128,128]{2,1,0:T(8,128)(2,1)S(1)}, u32[]{:S(2)}, u32[]{:S(2)}) collective-permute-start(bf16[3,128,128]{2,1,0:T(8,128)(2,1)} %get-tuple-element.30), channel_id=1, source_target_pairs={{0,192},{16,208},{32,224},{48,240},{64,128},{80,144},{96,160},{112... | collective-permute-start | bytes 294920 | tf_op jit(solution)/shard_map/ppermute | solution.py:319
  144.6 10.0 %copy-start.5 = (bf16[3,128,128]{2,1,0:T(8,128)(2,1)}, bf16[3,128,128]{2,1,0:T(8,128)(2,1)S(1)}, u32[]{:S(2)}) copy-start(bf16[3,128,128]{2,1,0:T(8,128)(2,1)S(1)} %collective-permute-done.3.refs_2_) | copy-start | bytes 294916
  144.6 10.0 %collective-permute-start.8 = (bf16[3,128,128]{2,1,0:T(8,128)(2,1)}, bf16[3,128,128]{2,1,0:T(8,128)(2,1)S(1)}, u32[]{:S(2)}, u32[]{:S(2)}) collective-permute-start(bf16[3,128,128]{2,1,0:T(8,128)(2,1)} %get-tuple-element.31), channel_id=1, source_target_pairs={{0,224},{16,240},{32,192},{48,208},{64,160},{80,176},{96,128},{112... | collective-permute-start | bytes 294920 | tf_op jit(solution)/shard_map/ppermute | solution.py:319
  149.7 4.9 %copy-start.6 = (bf16[3,128,128]{2,1,0:T(8,128)(2,1)}, bf16[3,128,128]{2,1,0:T(8,128)(2,1)S(1)}, u32[]{:S(2)}) copy-start(bf16[3,128,128]{2,1,0:T(8,128)(2,1)S(1)} %collective-permute-done.4.refs_3_) | copy-start | bytes 294916
  149.7 4.9 %copy-start.7 = (bf16[3,128,128]{2,1,0:T(8,128)(2,1)}, bf16[3,128,128]{2,1,0:T(8,128)(2,1)S(1)}, u32[]{:S(2)}) copy-start(bf16[3,128,128]{2,1,0:T(8,128)(2,1)S(1)} %collective-permute-done.5.refs_4_) | copy-start | bytes 294916
  149.7 4.9 %copy-start.8 = (bf16[3,128,128]{2,1,0:T(8,128)(2,1)}, bf16[3,128,128]{2,1,0:T(8,128)(2,1)S(1)}, u32[]{:S(2)}) copy-start(bf16[3,128,128]{2,1,0:T(8,128)(2,1)S(1)} %collective-permute-done.6.refs_5_) | copy-start | bytes 294916
  149.7 4.9 %copy-start.9 = (bf16[3,128,128]{2,1,0:T(8,128)(2,1)}, bf16[3,128,128]{2,1,0:T(8,128)(2,1)S(1)}, u32[]{:S(2)}) copy-start(bf16[3,128,128]{2,1,0:T(8,128)(2,1)S(1)} %collective-permute-done.7.refs_6_) | copy-start | bytes 294916
  154.6 0.6 copy-start.10

commit v7 on v5

--- a/solution.py
+++ b/solution.py
@@ -1,3 +1,5 @@
+import functools
+
 import jax
 import jax.numpy as jnp
 from jax import lax
@@ -22,7 +24,6 @@
 PACK = 3 * TOK + 8
 TILES = 9
 XS = 4
-EARLY = (0, 1, 3)
 
 SCALE = 144.0 ** (-0.5)
 LOG2E = 1.4426950408889634
@@ -60,13 +61,11 @@
         out_ref[s, 3 * TOK :, :] = jnp.concatenate(rows, axis=0).astype(bf16)
 
 
-def pack_late_kernel(where_ref, x_ref, out_ref, early_ref):
-    for x in range(XS):
+def turn_kernel(ks, where_ref, x_ref, *out_refs):
+    for k, out_ref in zip(ks, out_refs):
         for t in range(TILES):
-            tile = TILES * x + t
-            out_ref[x, t * TOK : (t + 1) * TOK, :] = x_ref[:, tile * 128 : (tile + 1) * 128].T
-    for j, k in enumerate(EARLY):
-        early_ref[j] = out_ref[where_ref[0, 3] ^ k]
+            tile = (where_ref[0, 3] ^ k) * TILES + t
+            out_ref[t * TOK : (t + 1) * TOK, :] = x_ref[:, block_at(tile, 128)].T
 
 
 def sort_slabs(core, in_ref, oth_ref, q_s, g_s, k_s, v_s, nd_s, inv_s):
@@ -174,21 +173,20 @@
                 send_ref[0, to] = part
 
 
-def weight_kernel(where_ref, mine_ref, early_ref, one_ref, two_ref, three_ref, *refs):
+def weight_kernel(where_ref, *refs):
     core = where_ref[0, 0]
     high = where_ref[0, 2]
     at_x = where_ref[0, 3]
-    dv_refs, (keep_ref, send_ref, grad_s) = refs[:XS], refs[XS:]
-    for i in range(CHIPS):
-        slab = 2 * i + high if i < XS else 2 * (at_x ^ (i - XS)) + 1 - high
+    x_refs, dv_refs, (keep_ref, send_ref, grad_s) = refs[: 2 * XS], refs[2 * XS : 3 * XS], refs[3 * XS :]
+    for i in range(2 * XS):
+        slab = 2 * (at_x ^ (i % XS)) + (high if i < XS else 1 - high)
         for k in range(XS):
             grad_s[i * TOK : (i + 1) * TOK, k * HEAD : (k + 1) * HEAD] = dv_refs[k][slab]
     grads = grad_s[...]
 
     def rows_of(part, c):
         at = pl.ds(pl.multiple_of(part * 2 * ROWS + c * ROWS, 32), ROWS)
-        tokens = [mine_ref[i, at, :] for i in range(XS)]
-        tokens += [early_ref[0, at, :]] + [ref[at, :] for ref in (one_ref, two_ref, three_ref)]
+        tokens = [ref[at, :] for ref in x_refs]
         return dot(jnp.concatenate(tokens, axis=1), grads, ((1,), (0,)))
 
     for part in range(2):
@@ -268,14 +266,18 @@
         slab_order, query_rows[0], output_grad[0], attn_output[0], key_rows[0], value_rows[0], log_norm[0]
     )
     got = lax.all_to_all(packed, SEQ, 0, 0, tiled=True)
-    late, early = call(
-        pack_late_kernel, [SMEM, VMEM],
-        [shaped((XS, TILES * TOK, 128), bf16), shaped((len(EARLY), TILES * TOK, 128), bf16)],
-    )(where, normed_input[0])
-    early = swapped(early, "yh")
-    got, late = lax.optimization_barrier((got, late))
+
+    def turned(*ks):
+        return call(
+            functools.partial(turn_kernel, ks), [SMEM, VMEM], [shaped((TILES * TOK, 128), bf16)] * len(ks)
+        )(where, normed_input[0])
+
+    near = turned(0, 1)
+    near = [swapped(block, "yh") for block in near]
+    far = turned(1, 2, 3)
+    mine = [along_x(block, k) for k, block in zip((1, 2, 3), far)]
+    mine = [*turned(0), *mine]
     other = swapped(got[:, 2 * TOK : 3 * TOK, :])
-    late = lax.all_to_all(late, "x", 0, 0, tiled=True)
     v_keep, v_send, q_keep, k_keep, qk_send = call(
         attn_kernel, [SMEM, VMEM, VMEM],
         [shaped(TOKENS, bf16)] * 4 + [shaped((2, *TOKENS), bf16)],
@@ -284,19 +286,18 @@
     )(where, got, other)
     v_came = swapped(v_send)
     dv = (v_keep.astype(f32) + v_came.astype(f32)).astype(bf16)
-    early, dv = lax.optimization_barrier((early, dv))
     dvs = [dv]
     for k in range(1, XS):
         dvs.append(along_x(dv, k))
-    two = swapped(lax.dynamic_index_in_dim(late, at_x ^ 2, 0, False), "yh")
-    one, three = along_x(early[1], 1), along_x(early[2], 3)
+    crossed = [swapped(mine[k], "yh") for k in (2, 3)]
+    crossed = [near[0], along_x(near[1], 1), *crossed]
     qk_came = swapped(qk_send)
     w_shape = (4, XS, 2, QUARTER, HEAD)
     w_keep, w_send = call(
-        weight_kernel, [SMEM] + [VMEM] * (5 + XS),
+        weight_kernel, [SMEM] + [VMEM] * (3 * XS),
         [shaped(w_shape, bf16)] * 2,
         [pltpu.VMEM((LENGTH // 2, XS * HEAD), bf16)], flops=2 * 10**9,
-    )(where, late, early, one, two, three, *dvs)
+    )(where, *mine, *crossed, *dvs)
     w_came = swapped(w_send)
     w = (w_keep.astype(f32) + w_came.astype(f32)).astype(bf16)
     parts = lax.all_to_all(w.reshape(SLABS, 2 * QUARTER, HEAD), "batch", 0, 0, tiled=True)
@@ -306,10 +307,10 @@
     pieces = [back[0]]
     for k in range(1, CHIPS):
         pieces.append(lax.ppermute(back[k], SEQ, [(i, i ^ (2 * k)) for i in range(SLABS)]))
-    piece = jnp.sum(parts.astype(f32), axis=0).astype(bf16).reshape(2, 1, QUARTER, HEAD)
+    piece = jnp.sum(parts.astype(f32), axis=0).astype(bf16).reshape(1, 2, QUARTER, HEAD)
     blocks = lax.all_to_all(
-        jnp.broadcast_to(piece, (2, SLABS, QUARTER, HEAD)).reshape(2 * SLABS, QUARTER, HEAD),
-        ("yh", "batch"), 0, 0, tiled=True,
+        jnp.broadcast_to(piece, (SLABS, 2, QUARTER, HEAD)).reshape(2 * SLABS, QUARTER, HEAD),
+        ("batch", "yh"), 0, 0, tiled=True,
     )
     (grad_query,) = call(
         place_query_kernel, [SMEM] + [VMEM] * CHIPS, [shaped((TOK, HEADS * HEAD), bf16)]
@@ -317,7 +318,7 @@
     (grad_key,) = call(
         place_key_kernel, [SMEM] + [VMEM] * CHIPS, [shaped((TOK, KV_HEADS * HEAD), bf16)]
     )(where, *pieces)
-    weight = blocks.reshape(2, 4, XS, QUARTER, HEAD).transpose(1, 3, 2, 0, 4).reshape(ROWS, KV_HEADS * HEAD)
+    weight = blocks.reshape(4, KV_HEADS, QUARTER, HEAD).transpose(0, 2, 1, 3).reshape(ROWS, KV_HEADS * HEAD)
     return (grad_query[None], grad_key[None], weight.astype(f32))
 
 

time: 171 us -> 164 us (0.959)
  the two profiles are of different devices: /device:TPU:2 before, /device:TPU:32 now
where the time goes in v7:
time: 164 us
  blocking collectives  57.9 us (35%)
  starting transfers between devices  41 us (25%)
  Pallas kernels  31.4 us (19%)
  waiting for transfers between devices  23.3 us (14%)
  local copies, waits for them, and re-layouts  5.35 us (3%)
  other arithmetic  3.31 us (2%)
    all_to_all x1, blocking collectives, inner(): got = lax.all_to_all(packed, SEQ, 0, 0, tiled=True)  31.1 us
    all_to_all x1, blocking collectives, inner(): lax.all_to_all(w.reshape(SLABS, 2 * QUARTER, HEAD), 'batch', 0, 0, tiled=...  26.8 us
    ppermute x7, starting transfers between devices, inner(): lax.ppermute(back[k], SEQ, [(i, i ^ 2 * k) for i in range(SLABS)])  17.4 us
    pallas_call x1, Pallas kernels, inner(): call(attn_kernel, [SMEM, VMEM, VMEM], [shaped(TOKENS, bf16)] * 4 + [shape...  11 us
    ppermute x8, waiting for transfers between devices, swapped(): return lax.ppermute(array, axis, SWAP)  10.1 us
    ppermute x7, starting transfers between devices, along_x(): return lax.ppermute(array, 'x', [(i, i ^ k) for i in range(XS)])  9.25 us
    ppermute x7, waiting for transfers between devices, along_x(): return lax.ppermute(array, 'x', [(i, i ^ k) for i in range(XS)])  8.41 us
    ppermute x8, starting transfers between devices, swapped(): return lax.ppermute(array, axis, SWAP)  7.69 us
  transfers between devices with their start and end apart: 23, of which 9 were waited for; matrix products, arithmetic and copies ran while one was open for 1% of the time, Pallas kernels for 15%

profile of v7, /device:TPU:32, one launch (start us, length us, event | category | flops | bytes accessed | tf_op | source)
XLA Modules:
  0.0 163.8 jit_solution(7234225257648431838)
XLA Ops:
  1.3 3.2 %shard_map.103 = bf16[16,392,128]{2,1,0:T(8,128)(2,1)} custom-call(s32[1,1]{1,0:T(1,128)S(6)} %copy.15.place_ref, bf16[128,2048]{1,0:T(8,128)(2,1)} %bitcast.35, bf16[128,2048]{1,0:T(8,128)(2,1)} %bitcast.36, bf16[128,2048]{1,0:T(8,128)(2,1)} %bitcast.37, bf16[128,1024]{1,0:T(8,128)(2,1)} %bitcast.38, bf16[128,1024]{1,0:T(8,128)(2,1)} %bitcast.39, ...), custom_call_target="tpu_custom_call" | custom-call | flops 1000000 | bytes 1000000 | tf_op jit(solution)/shard_map/pallas_call | solution.py:265
  4.4 31.1 %all_to_all.15.in_ref = bf16[16,392,128]{2,1,0:T(8,128)(2,1)S(1)} all-to-all(bf16[16,392,128]{2,1,0:T(8,128)(2,1)} %shard_map.103), channel_id=1, replica_groups=mesh['x'=4,'yh'=2,'core'=2,'batch'=16] {'x','yh','core'}, dimensions={0} | all-to-all | bytes 3211264 | tf_op jit(solution)/shard_map/all_to_all | solution.py:268
  35.6 0.2 collective-permute-start
  35.8 0.9 add_bitcast_fusion.where_ref
  36.7 2.4 %shard_map.109 = (bf16[1152,128]{1,0:T(8,128)(2,1)}, bf16[1152,128]{1,0:T(8,128)(2,1)}, bf16[1152,128]{1,0:T(8,128)(2,1)}) custom-call(s32[1,4]{1,0:T(1,128)} %add_bitcast_fusion.where_ref, bf16[128,4608]{1,0:T(8,128)(2,1)} %bitcast.27), custom_call_target="tpu_custom_call" | custom-call | flops 1000000 | bytes 1000000 | tf_op jit(solution)/shard_map/pallas_call | solution.py:271
  39.1 1.2 collective-permute-start.10
  40.3 2.0 %collective-permute-start.11 = (bf16[1152,128]{1,0:T(8,128)(2,1)}, bf16[1152,128]{1,0:T(8,128)(2,1)S(1)}, u32[]{:S(2)}, u32[]{:S(2)}) collective-permute-start(bf16[1152,128]{1,0:T(8,128)(2,1)} %get-tuple-element.36), channel_id=1, source_target_pairs={{0,192},{64,128},{128,64},{192,0},{1,193},{65,129},{129,65},{193,1... | collective-permute-start | bytes 884744 | tf_op jit(solution)/shard_map/ppermute | solution.py:257
  42.3 2.2 %shard_map.110 = (bf16[1152,128]{1,0:T(8,128)(2,1)}, bf16[1152,128]{1,0:T(8,128)(2,1)}) custom-call(s32[1,4]{1,0:T(1,128)} %add_bitcast_fusion.where_ref, bf16[128,4608]{1,0:T(8,128)(2,1)} %bitcast.28), custom_call_target="tpu_custom_call" | custom-call | flops 1000000 | bytes 1000000 | tf_op jit(solution)/shard_map/pallas_call | solution.py:271
  44.5 0.7 collective-permute-start.13
  45.2 0.0 collective-permute-done.oth_ref
  45.2 0.8 copy-done.11
  46.0 11.0 %shard_map.104 = (bf16[8,128,128]{2,1,0:T(8,128)(2,1)}, bf16[8,128,128]{2,1,0:T(8,128)(2,1)}, bf16[8,128,128]{2,1,0:T(8,128)(2,1)}, bf16[8,128,128]{2,1,0:T(8,128)(2,1)}, bf16[2,8,128,128]{3,2,1,0:T(8,128)(2,1)}) custom-call(s32[1,4]{1,0:T(1,128)} %add_bitcast_fusion.where_ref, bf16[16,392,128]{2,1,0:T(8,128)(2,1)} %copy-done, bf16[16,128,128]{2,1,0:T(8,128)(2,1)} %copy-done.11), custom_call_target="tpu_custom_call" | custom-call | flops 6000000000 | bytes 1000000 | tf_op jit(solution)/shard_map/pallas_call | solution.py:281
  57.0 0.0 collective-permute-start.17
  57.0 0.4 collective-permute-start.9
  57.4 0.0 collective-permute-done.10.refs_2_
  57.4 3.2 %collective-permute-start.12 = (bf16[1152,128]{1,0:T(8,128)(2,1)S(1)}, bf16[1152,128]{1,0:T(8,128)(2,1)S(1)}, u32[]{:S(2)}, u32[]{:S(2)}) collective-permute-start(bf16[1152,128]{1,0:T(8,128)(2,1)S(1)} %copy-done.17), channel_id=1, source_target_pairs={{0,32},{32,0},{1,33},{33,1},{2,34},{34,2},{3,35},{35,3},{4,36},{36... | collective-permute-start | bytes 884744 | tf_op jit(solution)/shard_map/ppermute | solution.py:253
  60.6 0.0 collective-permute-done.13
  60.6 1.8 %collective-permute-start.14 = (bf16[1152,128]{1,0:T(8,128)(2,1)S(1)}, bf16[1152,128]{1,0:T(8,128)(2,1)S(1)}, u32[]{:S(2)}, u32[]{:S(2)}) collective-permute-start(bf16[1152,128]{1,0:T(8,128)(2,1)S(1)} %collective-permute-done.13), channel_id=1, source_target_pairs={{0,64},{64,0},{128,192},{192,128},{1,65},{65,1},{129,193},{193,129... | collective-permute-start | bytes 884744 | tf_op jit(solution)/shard_map/ppermute | solution.py:257
  62.3 0.0 collective-permute-done.11.refs_3_
  62.3 0.6 collective-permute-start.15
  62.9 2.9 %collective-permute-start.16 = (bf16[1152,128]{1,0:T(8,128)(2,1)S(1)}, bf16[1152,128]{1,0:T(8,128)(2,1)S(1)}, u32[]{:S(2)}, u32[]{:S(2)}) collective-permute-start(bf16[1152,128]{1,0:T(8,128)(2,1)S(1)} %collective-permute-done.11.refs_3_), channel_id=1, source_target_pairs={{0,32},{32,0},{1,33},{33,1},{2,34},{34,2},{3,35},{35,3},{4,36},{36... | collective-permute-start | bytes 884744 | tf_op jit(solution)/shard_map/ppermute | solution.py:253
  65.9 1.0 add_convert_fusion.1.refs_8_
  66.9 0.0 copy-start.9
  66.9 0.1 collective-permute-done.9.refs_1_
  67.0 0.3 collective-permute-start.18
  67.3 1.7 %collective-permute-done.12.refs_4_ = bf16[1152,128]{1,0:T(8,128)(2,1)S(1)} collective-permute-done((bf16[1152,128]{1,0:T(8,128)(2,1)S(1)}, bf16[1152,128]{1,0:T(8,128)(2,1)S(1)}, u32[]{:S(2)}, u32[]{:S(2)}) %collective-permute-start.12) | collective-permute-done | bytes 294944 | tf_op jit(solution)/shard_map/ppermute | solution.py:253
  69.0 2.4 %collective-permute-start.19 = (bf16[8,128,128]{2,1,0:T(8,128)(2,1)S(1)}, bf16[8,128,128]{2,1,0:T(8,128)(2,1)S(1)}, u32[]{:S(2)}, u32[]{:S(2)}) collective-permute-start(bf16[8,128,128]{2,1,0:T(8,128)(2,1)S(1)} %add_convert_fusion.1.refs_8_), channel_id=1, source_target_pairs={{0,128},{64,192},{128,0},{192,64},{1,129},{65,193},{129,1},{193,65... | collective-permute-start | bytes 786440 | tf_op jit(solution)/shard_map/ppermute | solution.py:257
  71.4 1.9 %collective-permute-done.14.refs_5_ = bf16[1152,128]{1,0:T(8,128)(2,1)S(1)} collective-permute-done((bf16[1152,128]{1,0:T(8,128)(2,1)S(1)}, bf16[1152,128]{1,0:T(8,128)(2,1)S(1)}, u32[]{:S(2)}, u32[]{:S(2)}) %collective-permute-start.14) | collective-permute-done | bytes 294944 | tf_op jit(solution)/shard_map/ppermute | solution.py:257
  73.3 1.2 collective-permute-start.20
  74.5 2.1 %shard_map.108.refs_0_ = bf16[1152,128]{1,0:T(8,128)(2,1)} custom-call(s32[1,4]{1,0:T(1,128)} %add_bitcast_fusion.where_ref, bf16[128,4608]{1,0:T(8,128)(2,1)} %bitcast.29), custom_call_target="tpu_custom_call" | custom-call | flops 1000000 | bytes 1000000 | tf_op jit(solution)/shard_map/pallas_call | solution.py:271
  76.6 0.0 collective-permute-done.15.refs_6_
  76.6 4.2 %collective-permute-done.16.refs_7_ = bf16[1152,128]{1,0:T(8,128)(2,1)S(1)} collective-permute-done((bf16[1152,128]{1,0:T(8,128)(2,1)S(1)}, bf16[1152,128]{1,0:T(8,128)(2,1)S(1)}, u32[]{:S(2)}, u32[]{:S(2)}) %collective-permute-start.16) | collective-permute-done | bytes 294944 | tf_op jit(solution)/shard_map/ppermute | solution.py:253
  80.9 0.0 collective-permute-done.18.refs_9_
  80.9 3.9 %collective-permute-done.19.refs_10_ = bf16[8,128,128]{2,1,0:T(8,128)(2,1)S(1)} collective-permute-done((bf16[8,128,128]{2,1,0:T(8,128)(2,1)S(1)}, bf16[8,128,128]{2,1,0:T(8,128)(2,1)S(1)}, u32[]{:S(2)}, u32[]{:S(2)}) %collective-permute-start.19) | collective-permute-done | bytes 262176 | tf_op jit(solution)/shard_map/ppermute | solution.py:257
  84.7 2.6 %collective-permute-done.20.refs_11_ = bf16[8,128,128]{2,1,0:T(8,128)(2,1)S(1)} collective-permute-done((bf16[8,128,128]{2,1,0:T(8,128)(2,1)S(1)}, bf16[8,128,128]{2,1,0:T(8,128)(2,1)S(1)}, u32[]{:S(2)}, u32[]{:S(2)}) %collective-permute-start.20) | collective-permute-done | bytes 262176 | tf_op jit(solution)/shard_map/ppermute | solution.py:257
  87.4 0.7 copy-done.23
  88.1 4.3 %shard_map.111 = (bf16[4,4,2,72,128]{4,3,2,1,0:T(8,128)(2,1)}, bf16[4,4,2,72,128]{4,3,2,1,0:T(8,128)(2,1)}) custom-call(s32[1,4]{1,0:T(1,128)} %add_bitcast_fusion.where_ref, bf16[1152,128]{1,0:T(8,128)(2,1)} %shard_map.108.refs_0_, bf16[1152,128]{1,0:T(8,128)(2,1)} %copy-done.14, bf16[1152,128]{1,0:T(8,128)(2,1)} %copy-done.12, ...), custom_call_target="tpu_custom_call" | custom-call | flops 2000000000 | bytes 1000000 | tf_op jit(solution)/shard_map/pallas_call | solution.py:296
  92.4 0.0 collective-permute-start.21
  92.4 2.2 %collective-permute-done.21 = bf16[4,4,2,72,128]{4,3,2,1,0:T(8,128)(2,1)S(1)} collective-permute-done((bf16[4,4,2,72,128]{4,3,2,1,0:T(8,128)(2,1)}, bf16[4,4,2,72,128]{4,3,2,1,0:T(8,128)(2,1)S(1)}, u32[]{:S(2)}, u32[]{:S(2)}) %collective-permute-start.21) | collective-permute-done | bytes 589856 | tf_op jit(solution)/shard_map/ppermute | solution.py:253
  94.6 1.2 add_convert_fusion
  95.8 26.8 %all_to_all.16 = bf16[16,144,128]{2,1,0:T(8,128)(2,1)S(1)} all-to-all(bf16[16,144,128]{2,1,0:T(8,128)(2,1)S(1)} %bitcast.32), channel_id=1, replica_groups=mesh['x'=4,'yh'=2,'core'=2,'batch'=16] {'batch'}, dimensions={0} | all-to-all | bytes 1179648 | tf_op jit(solution)/shard_map/all_to_all | solution.py:303
  122.7 0.1 reduce_sum.12
  122.8 0.9 broadcast_in_dim.16
  123.7 6.7 %all-to-all-start.2 = ((bf16[32,72,128]{2,1,0:T(8,128)(2,1)}), bf16[32,72,128]{2,1,0:T(8,128)(2,1)S(1)}, u32[]{:S(2)}, u32[]{:S(2)}) async-start(bf16[32,72,128]{2,1,0:T(8,128)(2,1)} %bitcast.16), calls=%async_computation.2 | async-start | bytes 1179648 | tf_op jit(solution)/shard_map/all_to_all | solution.py:311
  130.4 0.1 collective-permute-start.1
  130.5 1.9 %collective-permute-done.1.came_ref = bf16[2,8,128,128]{3,2,1,0:T(8,128)(2,1)S(1)} collective-permute-done((bf16[2,8,128,128]{3,2,1,0:T(8,128)(2,1)S(1)}, bf16[2,8,128,128]{3,2,1,0:T(8,128)(2,1)S(1)}, u32[]{:S(2)}, u32[]{:S(2)}) %collective-permute-start.1) | collective-permute-done | bytes 524320 | tf_op jit(solution)/shard_map/ppermute | solution.py:253
  132.4 0.8 copy-done.1
  133.2 2.1 %shard_map.105 = (bf16[3,128,128]{2,1,0:T(8,128)(2,1)}, bf16[3,128,128]{2,1,0:T(8,128)(2,1)}, bf16[3,128,128]{2,1,0:T(8,128)(2,1)}, bf16[3,128,128]{2,1,0:T(8,12...) custom-call(bf16[8,128,128]{2,1,0:T(8,128)(2,1)} %get-tuple-element., ...), custom_call_target="tpu_custom_call" | custom-call | flops 1000000 | bytes 1000000 | tf_op jit(solution)/shard_map/pallas_call | solution.py:304
  135.2 3.0 %collective-permute-start.2 = (bf16[3,128,128]{2,1,0:T(8,128)(2,1)}, bf16[3,128,128]{2,1,0:T(8,128)(2,1)S(1)}, u32[]{:S(2)}, u32[]{:S(2)}) collective-permute-start(bf16[3,128,128]{2,1,0:T(8,128)(2,1)} %get-tuple-element.27), channel_id=1, source_target_pairs={{0,32},{16,48},{32,0},{48,16},{64,96},{80,112},{96,64},{112,80},{1... | collective-permute-start | bytes 294920 | tf_op jit(solution)/shard_map/ppermute | solution.py:309
  138.2 0.0 collective-permute-start.3
  138.2 2.0 %collective-permute-start.4 = (bf16[3,128,128]{2,1,0:T(8,128)(2,1)}, bf16[3,128,128]{2,1,0:T(8,128)(2,1)S(1)}, u32[]{:S(2)}, u32[]{:S(2)}) collective-permute-start(bf16[3,128,128]{2,1,0:T(8,128)(2,1)} %get-tuple-element.29), channel_id=1, source_target_pairs={{0,96},{16,112},{32,64},{48,80},{64,32},{80,48},{96,0},{112,16},{1... | collective-permute-start | bytes 294920 | tf_op jit(solution)/shard_map/ppermute | solution.py:309
  140.2 0.6 collective-permute-start.5
  140.9 5.3 %collective-permute-start.6 = (bf16[3,128,128]{2,1,0:T(8,128)(2,1)}, bf16[3,128,128]{2,1,0:T(8,128)(2,1)S(1)}, u32[]{:S(2)}, u32[]{:S(2)}) collective-permute-start(bf16[3,128,128]{2,1,0:T(8,128)(2,1)} %get-tuple-element.31), channel_id=1, source_target_pairs={{0,160},{16,176},{32,128},{48,144},{64,224},{80,240},{96,192},{112... | collective-permute-start | bytes 294920 | tf_op jit(solution)/shard_map/ppermute | solution.py:309
  146.2 1.2 collective-permute-start.7
  147.4 5.2 %collective-permute-start.8 = (bf16[3,128,128]{2,1,0:T(8,128)(2,1)}, bf16[3,128,128]{2,1,0:T(8,128)(2,1)S(1)}, u32[]{:S(2)}, u32[]{:S(2)}) collective-permute-start(bf16[3,128,128]{2,1,0:T(8,128)(2,1)} %get-tuple-element.33), channel_id=1, source_target_pairs={{0,224},{16,240},{32,192},{48,208},{64,160},{80,176},{96,128},{112... | collective-permute-start | bytes 294920 | tf_op jit(solution)/shard_map/ppermute | solution.py:309
  152.6 0.0 collective-permute-done.6.refs_5_
  152.7 4.8 %collective-permute-done.8.refs_7_ = bf16[3,128,128]{2,1,0:T(8,128)(2,1)S(1)} collective-permute-done((bf16[3,128,128]{2,1,0:T(8,128)(2,1)}, bf16[3,128,128]{2,1,0:T(8,128)(2,1)S(1)}, u32[]{:S(2)}, u32[]{:S(2)}) %collective-permute-start.8) | collective-permute-done | bytes 98336 | tf_op jit(solution)/shard_map/ppermute | solution.py:309
  157.5 0.6 copy-done.8
  158.1 2.1 %shard_map.106 = bf16[128,2048]{1,0:T(8,128)(2,1)} custom-call(s32[1,4]{1,0:T(1,128)} %add_bitcast_fusion.where_ref, bf16[3,128,128]{2,1,0:T(8,128)(2,1)} %get-tuple-element.26.refs_0_, bf16[3,128,128]{2,1,0:T(8,128)(2,1)} %copy-done.2, bf16[3,128,128]{2,1,0:T(8,128)(2,1)} %copy-done.3, bf16[3,128,128]{2,1,0:T(8,128)(2,1)} %copy-done.4, ...), custom_call_target="tpu_custom_call" | custom-call | flops 1000000 | bytes 1000000 | tf_op jit(solution)/shard_map/pallas_call | solution.py:315
  160.3 2.0 %shard_map.107 = bf16[128,1024]{1,0:T(8,128)(2,1)} custom-call(s32[1,4]{1,0:T(1,128)} %add_bitcast_fusion.where_ref, bf16[3,128,128]{2,1,0:T(8,128)(2,1)} %get-tuple-element.26.refs_0_, bf16[3,128,128]{2,1,0:T(8,128)(2,1)} %copy-done.2, bf16[3,128,128]{2,1,0:T(8,128)(2,1)} %copy-done.3, bf16[3,128,128]{2,1,0:T(8,128)(2,1)} %copy-done.4, ...), custom_call_target="tpu_custom_call" | custom-call | flops 1000000 | bytes 1000000 | tf_op jit(solution)/shard_map/pallas_call | solution.py:318
  162.3 0.0 all-to-all-done.2
  162.3 0.1 convert_bitcast_fusion
  162.4 0.2 copy.11
  162.6 1.2 copy.14
  (50 shorter events, 0.1 us)
Async XLA Ops:
  35.5 9.0 %copy-start = (bf16[16,392,128]{2,1,0:T(8,128)(2,1)}, bf16[16,392,128]{2,1,0:T(8,128)(2,1)S(1)}, u32[]{:S(2)}) copy-start(bf16[16,392,128]{2,1,0:T(8,128)(2,1)S(1)} %all_to_all.15.in_ref) | copy-start | bytes 4816900
  35.6 9.6 %collective-permute-start = (bf16[16,128,128]{2,1,0:T(8,128)(2,1)S(1)}, bf16[16,128,128]{2,1,0:T(8,128)(2,1)S(1)}, u32[]{:S(2)}, u32[]{:S(2)}) collective-permute-start(bf16[16,128,128]{2,1,0:T(8,128)(2,1)S(1)} %slice.4), channel_id=1, source_target_pairs={{0,16},{16,0},{1,17},{17,1},{2,18},{18,2},{3,19},{19,3},{4,20},{20... | collective-permute-start | bytes 1572872 | tf_op jit(solution)/shard_map/ppermute | solution.py:253
  39.1 18.3 %collective-permute-start.10 = (bf16[1152,128]{1,0:T(8,128)(2,1)}, bf16[1152,128]{1,0:T(8,128)(2,1)S(1)}, u32[]{:S(2)}, u32[]{:S(2)}) collective-permute-start(bf16[1152,128]{1,0:T(8,128)(2,1)} %get-tuple-element.35), channel_id=1, source_target_pairs={{0,128},{64,192},{128,0},{192,64},{1,129},{65,193},{129,1},{193,65... | collective-permute-start | bytes 884744 | tf_op jit(solution)/shard_map/ppermute | solution.py:257
  40.3 22.1 %collective-permute-start.11 = (bf16[1152,128]{1,0:T(8,128)(2,1)}, bf16[1152,128]{1,0:T(8,128)(2,1)S(1)}, u32[]{:S(2)}, u32[]{:S(2)}) collective-permute-start(bf16[1152,128]{1,0:T(8,128)(2,1)} %get-tuple-element.36), channel_id=1, source_target_pairs={{0,192},{64,128},{128,64},{192,0},{1,193},{65,129},{129,65},{193,1... | collective-permute-start | bytes 884744 | tf_op jit(solution)/shard_map/ppermute | solution.py:257
  44.5 12.5 %copy-start.16 = (bf16[1152,128]{1,0:T(8,128)(2,1)S(1)}, bf16[1152,128]{1,0:T(8,128)(2,1)}, u32[]{:S(2)}) copy-start(bf16[1152,128]{1,0:T(8,128)(2,1)} %get-tuple-element.34) | copy-start | bytes 884740
  44.5 12.9 %copy-start.17 = (bf16[1152,128]{1,0:T(8,128)(2,1)S(1)}, bf16[1152,128]{1,0:T(8,128)(2,1)}, u32[]{:S(2)}) copy-start(bf16[1152,128]{1,0:T(8,128)(2,1)} %get-tuple-element.37) | copy-start | bytes 884740
  44.5 16.1 %collective-permute-start.13 = (bf16[1152,128]{1,0:T(8,128)(2,1)}, bf16[1152,128]{1,0:T(8,128)(2,1)S(1)}, u32[]{:S(2)}, u32[]{:S(2)}) collective-permute-start(bf16[1152,128]{1,0:T(8,128)(2,1)} %get-tuple-element.38), channel_id=1, source_target_pairs={{0,32},{32,0},{1,33},{33,1},{2,34},{34,2},{3,35},{35,3},{4,36},{36... | collective-permute-start | bytes 884744 | tf_op jit(solution)/shard_map/ppermute | solution.py:253
  45.2 0.8 copy-start.11
  57.0 5.9 %collective-permute-start.17 = (bf16[8,128,128]{2,1,0:T(8,128)(2,1)}, bf16[8,128,128]{2,1,0:T(8,128)(2,1)S(1)}, u32[]{:S(2)}, u32[]{:S(2)}) collective-permute-start(bf16[8,128,128]{2,1,0:T(8,128)(2,1)} %get-tuple-element.40), channel_id=1, source_target_pairs={{0,16},{16,0},{1,17},{17,1},{2,18},{18,2},{3,19},{19,3},{4,20},{20... | collective-permute-start | bytes 786440 | tf_op jit(solution)/shard_map/ppermute | solution.py:253
  57.0 10.0 %collective-permute-start.9 = (bf16[1152,128]{1,0:T(8,128)(2,1)S(1)}, bf16[1152,128]{1,0:T(8,128)(2,1)S(1)}, u32[]{:S(2)}, u32[]{:S(2)}) collective-permute-start(bf16[1152,128]{1,0:T(8,128)(2,1)S(1)} %copy-done.16), channel_id=1, source_target_pairs={{0,64},{64,0},{128,192},{192,128},{1,65},{65,1},{129,193},{193,129... | collective-permute-start | bytes 884744 | tf_op jit(solution)/shard_map/ppermute | solution.py:257
  57.4 30.0 %copy-start.12 = (bf16[1152,128]{1,0:T(8,128)(2,1)}, bf16[1152,128]{1,0:T(8,128)(2,1)S(1)}, u32[]{:S(2)}) copy-start(bf16[1152,128]{1,0:T(8,128)(2,1)S(1)} %collective-permute-done.10.refs_2_) | copy-start | bytes 884740
  57.4 11.6 %collective-permute-start.12 = (bf16[1152,128]{1,0:T(8,128)(2,1)S(1)}, bf16[1152,128]{1,0:T(8,128)(2,1)S(1)}, u32[]{:S(2)}, u32[]{:S(2)}) collective-permute-start(bf16[1152,128]{1,0:T(8,128)(2,1)S(1)} %copy-done.17), channel_id=1, source_target_pairs={{0,32},{32,0},{1,33},{33,1},{2,34},{34,2},{3,35},{35,3},{4,36},{36... | collective-permute-start | bytes 884744 | tf_op jit(solution)/shard_map/ppermute | solution.py:253
  60.6 12.7 %collective-permute-start.14 = (bf16[1152,128]{1,0:T(8,128)(2,1)S(1)}, bf16[1152,128]{1,0:T(8,128)(2,1)S(1)}, u32[]{:S(2)}, u32[]{:S(2)}) collective-permute-start(bf16[1152,128]{1,0:T(8,128)(2,1)S(1)} %collective-permute-done.13), channel_id=1, source_target_pairs={{0,64},{64,0},{128,192},{192,128},{1,65},{65,1},{129,193},{193,129... | collective-permute-start | bytes 884744 | tf_op jit(solution)/shard_map/ppermute | solution.py:257
  62.3 25.0 %copy-start.13 = (bf16[1152,128]{1,0:T(8,128)(2,1)}, bf16[1152,128]{1,0:T(8,128)(2,1)S(1)}, u32[]{:S(2)}) copy-start(bf16[1152,128]{1,0:T(8,128)(2,1)S(1)} %collective-permute-done.11.refs_3_) | copy-start | bytes 884740
  62.3 14.3 %collective-permute-start.15 = (bf16[1152,128]{1,0:T(8,128)(2,1)S(1)}, bf16[1152,128]{1,0:T(8,128)(2,1)S(1)}, u32[]{:S(2)}, u32[]{:S(2)}) collective-permute-start(bf16[1152,128]{1,0:T(8,128)(2,1)S(1)} %collective-permute-done.10.refs_2_), channel_id=1, source_target_pairs={{0,32},{32,0},{1,33},{33,1},{2,34},{34,2},{3,35},{35,3},{4,36},{36... | collective-permute-start | bytes 884744 | tf_op jit(solution)/shard_map/ppermute | solution.py:253
  62.9 17.9 %collective-permute-start.16 = (bf16[1152,128]{1,0:T(8,128)(2,1)S(1)}, bf16[1152,128]{1,0:T(8,128)(2,1)S(1)}, u32[]{:S(2)}, u32[]{:S(2)}) collective-permute-start(bf16[1152,128]{1,0:T(8,128)(2,1)S(1)} %collective-permute-done.11.refs_3_), channel_id=1, source_target_pairs={{0,32},{32,0},{1,33},{33,1},{2,34},{34,2},{3,35},{35,3},{4,36},{36... | collective-permute-start | bytes 884744 | tf_op jit(solution)/shard_map/ppermute | solution.py:253
  66.9 20.5 %copy-start.9 = (bf16[8,128,128]{2,1,0:T(8,128)(2,1)}, bf16[8,128,128]{2,1,0:T(8,128)(2,1)S(1)}, u32[]{:S(2)}) copy-start(bf16[8,128,128]{2,1,0:T(8,128)(2,1)S(1)} %add_convert_fusion.1.refs_8_) | copy-start | bytes 786436
  67.0 20.4 %copy-start.14 = (bf16[1152,128]{1,0:T(8,128)(2,1)}, bf16[1152,128]{1,0:T(8,128)(2,1)S(1)}, u32[]{:S(2)}) copy-start(bf16[1152,128]{1,0:T(8,128)(2,1)S(1)} %collective-permute-done.9.refs_1_) | copy-start | bytes 884740
  67.0 13.9 %collective-permute-start.18 = (bf16[8,128,128]{2,1,0:T(8,128)(2,1)S(1)}, bf16[8,128,128]{2,1,0:T(8,128)(2,1)S(1)}, u32[]{:S(2)}, u32[]{:S(2)}) collective-permute-start(bf16[8,128,128]{2,1,0:T(8,128)(2,1)S(1)} %add_convert_fusion.1.refs_8_), channel_id=1, source_target_pairs={{0,64},{64,0},{128,192},{192,128},{1,65},{65,1},{129,193},{193,129... | collective-permute-start | bytes 786440 | tf_op jit(solution)/shard_map/ppermute | solution.py:257
  69.0 18.3 %copy-start.15 = (bf16[1152,128]{1,0:T(8,128)(2,1)}, bf16[1152,128]{1,0:T(8,128)(2,1)S(1)}, u32[]{:S(2)}) copy-start(bf16[1152,128]{1,0:T(8,128)(2,1)S(1)} %collective-permute-done.12.refs_4_) | copy-start | bytes 884740
  69.0 15.7 %collective-permute-start.19 = (bf16[8,128,128]{2,1,0:T(8,128)(2,1)S(1)}, bf16[8,128,128]{2,1,0:T(8,128)(2,1)S(1)}, u32[]{:S(2)}, u32[]{:S(2)}) collective-permute-start(bf16[8,128,128]{2,1,0:T(8,128)(2,1)S(1)} %add_convert_fusion.1.refs_8_), channel_id=1, source_target_pairs={{0,128},{64,192},{128,0},{192,64},{1,129},{65,193},{129,1},{193,65... | collective-permute-start | bytes 786440 | tf_op jit(solution)/shard_map/ppermute | solution.py:257
  73.3 14.1 %copy-start.18 = (bf16[1152,128]{1,0:T(8,128)(2,1)}, bf16[1152,128]{1,0:T(8,128)(2,1)S(1)}, u32[]{:S(2)}) copy-start(bf16[1152,128]{1,0:T(8,128)(2,1)S(1)} %collective-permute-done.14.refs_5_) | copy-start | bytes 884740
  73.3 14.1 %collective-permute-start.20 = (bf16[8,128,128]{2,1,0:T(8,128)(2,1)S(1)}, bf16[8,128,128]{2,1,0:T(8,128)(2,1)S(1)}, u32[]{:S(2)}, u32[]{:S(2)}) collective-permute-start(bf16[8,128,128]{2,1,0:T(8,128)(2,1)S(1)} %add_convert_fusion.1.refs_8_), channel_id=1, source_target_pairs={{0,192},{64,128},{128,64},{192,0},{1,193},{65,129},{129,65},{193,1... | collective-permute-start | bytes 786440 | tf_op jit(solution)/shard_map/ppermute | solution.py:257
  76.6 10.7 %copy-start.19 = (bf16[1152,128]{1,0:T(8,128)(2,1)}, bf16[1152,128]{1,0:T(8,128)(2,1)S(1)}, u32[]{:S(2)}) copy-start(bf16[1152,128]{1,0:T(8,128)(2,1)S(1)} %collective-permute-done.15.refs_6_) | copy-start | bytes 884740
  80.9 6.5 %copy-start.20 = (bf16[1152,128]{1,0:T(8,128)(2,1)}, bf16[1152,128]{1,0:T(8,128)(2,1)S(1)}, u32[]{:S(2)}) copy-start(bf16[1152,128]{1,0:T(8,128)(2,1)S(1)} %collective-permute-done.16.refs_7_) | copy-start | bytes 884740
  80.9 6.5 %copy-start.21 = (bf16[8,128,128]{2,1,0:T(8,128)(2,1)}, bf16[8,128,128]{2,1,0:T(8,128)(2,1)S(1)}, u32[]{:S(2)}) copy-start(bf16[8,128,128]{2,1,0:T(8,128)(2,1)S(1)} %collective-permute-done.18.refs_9_) | copy-start | bytes 786436
  84.7 2.7 %copy-start.22 = (bf16[8,128,128]{2,1,0:T(8,128)(2,1)}, bf16[8,128,128]{2,1,0:T(8,128)(2,1)S(1)}, u32[]{:S(2)}) copy-start(bf16[8,128,128]{2,1,0:T(8,128)(2,1)S(1)} %collective-permute-done.19.refs_10_) | copy-start | bytes 786436
  87.4 0.7 copy-start.23
  92.4 2.2 %collective-permute-start.21 = (bf16[4,4,2,72,128]{4,3,2,1,0:T(8,128)(2,1)}, bf16[4,4,2,72,128]{4,3,2,1,0:T(8,128)(2,1)S(1)}, u32[]{:S(2)}, u32[]{:S(2)}) collective-permute-start(bf16[4,4,2,72,128]{4,3,2,1,0:T(8,128)(2,1)} %get-tuple-element.42), channel_id=1, source_target_pairs={{0,16},{16,0},{1,17},{17,1},{2,18},{18,2},{3,19},{19,3},{4,20},{20... | collective-permute-start | bytes 1769480 | tf_op jit(solution)/shard_map/ppermute | solution.py:253
  122.7 7.7 %copy-start.10 = (bf16[2,8,128,128]{3,2,1,0:T(8,128)(2,1)S(1)}, bf16[2,8,128,128]{3,2,1,0:T(8,128)(2,1)}, u32[]{:S(2)}) copy-start(bf16[2,8,128,128]{3,2,1,0:T(8,128)(2,1)} %get-tuple-element.25) | copy-start | bytes 1572868
  123.7 38.6 %all-to-all-start.2 = ((bf16[32,72,128]{2,1,0:T(8,128)(2,1)}), bf16[32,72,128]{2,1,0:T(8,128)(2,1)S(1)}, u32[]{:S(2)}, u32[]{:S(2)}) async-start(bf16[32,72,128]{2,1,0:T(8,128)(2,1)} %bitcast.16), calls=%async_computation.2 | async-start | bytes 1179648 | tf_op jit(solution)/shard_map/all_to_all | solution.py:311
  130.4 2.0 %collective-permute-start.1 = (bf16[2,8,128,128]{3,2,1,0:T(8,128)(2,1)S(1)}, bf16[2,8,128,128]{3,2,1,0:T(8,128)(2,1)S(1)}, u32[]{:S(2)}, u32[]{:S(2)}) collective-permute-start(bf16[2,8,128,128]{3,2,1,0:T(8,128)(2,1)S(1)} %copy-done.10), channel_id=1, source_target_pairs={{0,16},{16,0},{1,17},{17,1},{2,18},{18,2},{3,19},{19,3},{4,20},{20... | collective-permute-start | bytes 1572872 | tf_op jit(solution)/shard_map/ppermute | solution.py:253
  132.4 0.8 copy-start.1
  135.2 10.9 %collective-permute-start.2 = (bf16[3,128,128]{2,1,0:T(8,128)(2,1)}, bf16[3,128,128]{2,1,0:T(8,128)(2,1)S(1)}, u32[]{:S(2)}, u32[]{:S(2)}) collective-permute-start(bf16[3,128,128]{2,1,0:T(8,128)(2,1)} %get-tuple-element.27), channel_id=1, source_target_pairs={{0,32},{16,48},{32,0},{48,16},{64,96},{80,112},{96,64},{112,80},{1... | collective-permute-start | bytes 294920 | tf_op jit(solution)/shard_map/ppermute | solution.py:309
  138.2 9.2 %collective-permute-start.3 = (bf16[3,128,128]{2,1,0:T(8,128)(2,1)}, bf16[3,128,128]{2,1,0:T(8,128)(2,1)S(1)}, u32[]{:S(2)}, u32[]{:S(2)}) collective-permute-start(bf16[3,128,128]{2,1,0:T(8,128)(2,1)} %get-tuple-element.28), channel_id=1, source_target_pairs={{0,64},{16,80},{32,96},{48,112},{64,0},{80,16},{96,32},{112,48},{1... | collective-permute-start | bytes 294920 | tf_op jit(solution)/shard_map/ppermute | solution.py:309
  138.2 14.4 %collective-permute-start.4 = (bf16[3,128,128]{2,1,0:T(8,128)(2,1)}, bf16[3,128,128]{2,1,0:T(8,128)(2,1)S(1)}, u32[]{:S(2)}, u32[]{:S(2)}) collective-permute-start(bf16[3,128,128]{2,1,0:T(8,128)(2,1)} %get-tuple-element.29), channel_id=1, source_target_pairs={{0,96},{16,112},{32,64},{48,80},{64,32},{80,48},{96,0},{112,16},{1... | collective-permute-start | bytes 294920 | tf_op jit(solution)/shard_map/ppermute | solution.py:309
  140.2 12.4 %collective-permute-start.5 = (bf16[3,128,128]{2,1,0:T(8,128)(2,1)}, bf16[3,128,128]{2,1,0:T(8,128)(2,1)S(1)}, u32[]{:S(2)}, u32[]{:S(2)}) collective-permute-start(bf16[3,128,128]{2,1,0:T(8,128)(2,1)} %get-tuple-element.30), channel_id=1, source_target_pairs={{0,128},{16,144},{32,160},{48,176},{64,192},{80,208},{96,224},{112... | collective-permute-start | bytes 294920 | tf_op jit(solution)/shard_map/ppermute | solution.py:309
  140.9 11.8 %collective-permute-start.6 = (bf16[3,128,128]{2,1,0:T(8,128)(2,1)}, bf16[3,128,128]{2,1,0:T(8,128)(2,1)S(1)}, u32[]{:S(2)}, u32[]{:S(2)}) collective-permute-start(bf16[3,128,128]{2,1,0:T(8,128)(2,1)} %get-tuple-element.31), channel_id=1, source_target_pairs={{0,160},{16,176},{32,128},{48,144},{64,224},{80,240},{96,192},{112... | collective-permute-start | bytes 294920 | tf_op jit(solution)/shard_map/ppermute | solution.py:309
  146.2 11.3 %copy-start.2 = (bf16[3,128,128]{2,1,0:T(8,128)(2,1)}, bf16[3,128,128]{2,1,0:T(8,128)(2,1)S(1)}, u32[]{:S(2)}) copy-start(bf16[3,128,128]{2,1,0:T(8,128)(2,1)S(1)} %collective-permute-done.2.refs_1_) | copy-start | bytes 294916
  146.2 6.5 %collective-permute-start.7 = (bf16[3,128,128]{2,1,0:T(8,128)(2,1)}, bf16[3,128,128]{2,1,0:T(8,128)(2,1)S(1)}, u32[]{:S(2)}, u32[]{:S(2)}) collective-permute-start(bf16[3,128,128]{2,1,0:T(8,128)(2,1)} %get-tuple-element.32), channel_id=1, source_target_pairs={{0,192},{16,208},{32,224},{48,240},{64,128},{80,144},{96,160},{112... | collective-permute-start | bytes 294920 | tf_op jit(solution)/shard_map/ppermute | solution.py:309
  147.4 10.1 %copy-start.3 = (bf16[3,128,128]{2,1,0:T(8,128)(2,1)}, bf16[3,128,128]{2,1,0:T(8,128)(2,1)S(1)}, u32[]{:S(2)}) copy-start(bf16[3,128,128]{2,1,0:T(8,128)(2,1)S(1)} %collective-permute-done.3.refs_2_) | copy-start | bytes 294916
  147.4 10.1 %collective-permute-start.8 = (bf16[3,128,128]{2,1,0:T(8,128)(2,1)}, bf16[3,128,128]{2,1,0:T(8,128)(2,1)S(1)}, u32[]{:S(2)}, u32[]{:S(2)}) collective-permute-start(bf16[3,128,128]{2,1,0:T(8,128)(2,1)} %get-tuple-element.33), channel_id=1, source_target_pairs={{0,224},{16,240},{32,192},{48,208},{64,160},{80,176},{96,128},{112... | collective-permute-start | bytes 294920 | tf_op jit(solution)/shard_map/ppermute | solution.py:309
  152.6 4.9 %copy-start.4 = (bf16[3,128,128]{2,1,0:T(8,128)(2,1)}, bf16[3,128,128]{2,1,0:T(8,128)(2,1)S(1)}, u32[]{:S(2)}) copy-start(bf16[3,128,128]{2,1,0:T(8,128)(2,1)S(1)} %collective-permute-done.4.refs_3_) | copy-start | bytes 294916
  152.6 4.9 %copy-start.5 = (bf16[3,128,128]{2,1,0:T(8,128)(2,1)}, bf16[3,128,128]{2,1,0:T(8,128)(2,1)S(1)}, u32[]{:S(2)}) copy-start(bf16[3,128,128]{2,1,0:T(8,128)(2,1)S(1)} %collective-permute-done.5.refs_4_) | copy-start | bytes 294916
  152.7 4.9 %copy-start.6 = (bf16[3,128,128]{2,1,0:T(8,128)(2,1)}, bf16[3,128,128]{2,1,0:T(8,128)(2,1)S(1)}, u32[]{:S(2)}) copy-start(bf16[3,128,128]{2,1,0:T(8,128)(2,1)S(1)} %collective-permute-done.6.refs_5_) | copy-start | bytes 294916
  152.7 4.9 %copy-start.7 = (bf16[3,128,128]{2,1,0:T(8,128)(2,1)}, bf16[3,128,128]{2,1,0:T(8,128)(2,1)S(1)}, u32[]{:S(2)}) copy-start(bf16[3,128,128]{2,1,0:T(8,128)(2,1)S(1)} %collective-permute-done.7.refs_6_) | copy-start | bytes 294916
  157.5 0.6 copy-start.8
